TPU v7x, 256 devices: a whole 4x4x8 slice. The times are simulated.
256 devices in a mesh: cuts: 64 (over y, x, z_lo, core), grp: 4 (over z_hi).
Axes of the slice: x: 4, y: 4, z: 8 (z_hi: 4, z_lo: 2; z = z_hi * 2 + z_lo), core: 2. Of those that a mesh axis runs over, the one named last changes fastest.
Arguments:
- boundary: float32 [32, 2, 32, 32, 32], P('grp'), may hold values from -12 to 12
- gate_stack: float32 [3, 2, 1024, 1024], P(None, None, 'cuts'), may hold values from -0.125 to 0.125
- layer_order: int32 [3], replicated, may hold values from 0 to 2, each once
- cut_index: int32 [6, 3], replicated, may hold values from 0 to 4, as said below
- slice_bits: int32 [64, 6], P('cuts'), may hold values 0 or 1
- bitstrings: int32 [64, 20], replicated, may hold values 0 or 1
Outputs:
- amplitudes: float32 [64, 2], replicated
Inputs may be any that keep to these rules, and one draw needn't show every extreme that they name: Each row of cut_index is (layer 0 to 2, group 0 to 3, bit 0 to 4); no two rows are equal. Rows of slice_bits need not differ.
All inputs are finite; a program needn't handle non-finite values.
Results may differ from a plain program's by a relative error of at most 0.0003.
Values sent between devices are 32-bit elements.
No kernel may reach another device: no remote copies, remote signals or barrier semaphores. Data moves between devices by JAX's collectives and lax.ppermute only.
A program may use at most 320 MiB of HBM per device.

v0:
```python
from functools import partial

import jax
import jax.numpy as jnp
from jax import lax
from jax.sharding import Mesh
from jax.sharding import PartitionSpec as P

CUTS = ("cuts_0", "cuts_1", "cuts_2", "cuts_3")
CUTS_GRP = ("cuts_0", "cuts_1", "cuts_2", "cuts_3", "grp")


LAYER_KINDS = (0, 1, 2, 3, 2, 3, 0, 1)
PAIR_GROUPS = ((0, 1), (2, 3), (1, 2), (1, 3))
GROUP_DIMS = (0, 3, 4, 5)
FULL_PRECISION = lax.Precision.HIGHEST


def over_axes(array, axes):
    for axis in axes:
        array = lax.psum(array, axis)
    return array


def slice_factors(cut_index, slice_bits, layer_id, group_id, extent, offset):
    positions = offset + jnp.arange(extent, dtype=jnp.int32)
    active = jnp.logical_and(cut_index[:, 0] == layer_id, cut_index[:, 1] == group_id)
    bit_values = jnp.right_shift(positions[:, None], cut_index[None, :, 2]) & 1
    agrees = bit_values[None, :, :] == slice_bits[:, None, :]
    kept = jnp.logical_or(agrees, jnp.logical_not(active)[None, None, :])
    return jnp.all(kept, axis=2).astype(jnp.float32)


def group_digits(bitstrings, group_bits):
    weights = jnp.left_shift(
        jnp.ones((group_bits,), jnp.int32), jnp.arange(group_bits, dtype=jnp.int32)
    )
    return [
        jnp.sum(
            bitstrings[:, group_id * group_bits : (group_id + 1) * group_bits] * weights, axis=1
        ).astype(jnp.int32)
        for group_id in range(4)
    ]


def rotated(current):
    return jnp.concatenate((-current[:, :, 1:2], current[:, :, 0:1]), axis=2)


def local_pair(current, first_dim, second_dim, produce):
    aligned = jnp.moveaxis(current, (first_dim, second_dim), (0, 1))
    turned = jnp.moveaxis(rotated(current), (first_dim, second_dim), (0, 1))
    in_rows = aligned.shape[0] * aligned.shape[1]
    outcome = produce(aligned.reshape(in_rows, -1), turned.reshape(in_rows, -1))
    extent = aligned.shape[1]
    outcome = outcome.reshape((extent, extent) + aligned.shape[2:])
    return jnp.moveaxis(outcome, (0, 1), (first_dim, second_dim))


def on_device(boundary, gate_stack, layer_order, cut_index, slice_bits, bitstrings):
    member = lax.axis_index("grp")
    gate_source = lax.all_gather(gate_stack, CUTS, axis=2, tiled=True)

    def gate_product(layer_id, direct, swapped, column_start, col_count):

        def rows_from(piece):
            columns = lax.dynamic_slice_in_dim(piece, column_start, col_count, 2)
            return jnp.dot(
                columns[0], direct, precision=FULL_PRECISION, preferred_element_type=jnp.float32
            ) + jnp.dot(
                columns[1], swapped, precision=FULL_PRECISION, preferred_element_type=jnp.float32
            )

        chosen = lax.dynamic_index_in_dim(gate_source, layer_order[layer_id], 0, keepdims=False)
        return rows_from(chosen)

    slice_count = slice_bits.shape[0]
    row_count = boundary.shape[0]
    extent = boundary.shape[2]
    current = jnp.broadcast_to(boundary[:, None], (row_count, slice_count) + boundary.shape[1:])
    for layer_id in range(layer_order.shape[0]):
        first_group, second_group = PAIR_GROUPS[LAYER_KINDS[layer_id % 8]]
        if first_group == 0:
            widened = lax.all_to_all(current, "grp", split_axis=5, concat_axis=0, tiled=True)
            widened = local_pair(
                widened,
                0,
                3,
                partial(gate_product, layer_id, column_start=0, col_count=extent * extent),
            )
            current = lax.all_to_all(widened, "grp", split_axis=0, concat_axis=5, tiled=True)
        else:
            current = local_pair(
                current,
                GROUP_DIMS[first_group],
                GROUP_DIMS[second_group],
                partial(gate_product, layer_id, column_start=0, col_count=extent * extent),
            )
        for group_id in range(4):
            dim_pos = GROUP_DIMS[group_id]
            if group_id == 0:
                factor = slice_factors(
                    cut_index, slice_bits, layer_id, 0, row_count, row_count * member
                ).T
                target_shape = (row_count, slice_count, 1, 1, 1, 1)
            else:
                factor = slice_factors(cut_index, slice_bits, layer_id, group_id, extent, 0)
                target_shape = tuple(
                    (
                        slice_count if position == 1 else extent if position == dim_pos else 1
                        for position in range(6)
                    )
                )
            current = current * factor.reshape(target_shape)
    digits = group_digits(bitstrings, bitstrings.shape[1] // 4)
    summed = jnp.sum(current, axis=1)
    local_row = digits[0] - row_count * member
    inside = jnp.logical_and(local_row >= 0, local_row < row_count)
    picked = summed[jnp.clip(local_row, 0, row_count - 1), :, digits[1], digits[2], digits[3]]
    picked = picked * inside[:, None].astype(jnp.float32)
    return over_axes(picked, CUTS_GRP)


def solution(mesh):
    finer = Mesh(
        mesh.devices.reshape(4, 4, 2, 2, mesh.shape["grp"]),
        ("cuts_0", "cuts_1", "cuts_2", "cuts_3", "grp"),
    )
    return jax.shard_map(
        on_device,
        mesh=finer,
        in_specs=(
            P("grp", None, None, None, None),
            P(None, None, CUTS, None),
            P(),
            P(),
            P(CUTS, None),
            P(),
        ),
        out_specs=P(),
        check_vma=False,
    )
```

profile of v0, /device:TPU:1, one launch (start us, length us, event | category | flops | bytes accessed | tf_op | source)
XLA Modules:
  0.0 618.9 jit_solution(14292279170790239234)
XLA Ops:
  7.3 10.8 %copy.83 = f32[8,2,32,32,32]{3,2,1,0,4:T(8,128)} copy(f32[8,2,32,32,32]{4,3,2,1,0:T(8,128)} %param.6) | data formatting | bytes 4194304 | tf_op args[0]
  18.1 8.5 %bitcast_bitcast_fusion = f32[32,1,8,2,32,32]{5,4,3,2,1,0:T(8,128)} fusion(f32[8,2,32,32,32]{3,2,1,0,4:T(8,128)} %copy.83), kind=kLoop, calls=%fused_computation.100 | loop fusion | bytes 4194304
  33.7 9.3 %all-to-all-start = ((f32[4,1,131072]{2,1,0:T(1,128)}), f32[4,1,131072]{2,1,0:T(1,128)S(1)}, u32[]{:S(2)}, u32[]{:S(2)}) async-start(f32[4,1,131072]{2,1,0:T(1,128)} %reshape.1435), calls=%async_computation | async-start | bytes 4194304 | tf_op jit(solution)/shard_map/all_to_all | solution.py:84
  45.6 70.1 %all-to-all-done = f32[4,1,131072]{2,1,0:T(1,128)S(1)} async-done(((f32[4,1,131072]{2,1,0:T(1,128)}), f32[4,1,131072]{2,1,0:T(1,128)S(1)}, u32[]{:S(2)}, u32[]{:S(2)}) %all-to-all-start) | async-done | bytes 2097184 | tf_op jit(solution)/shard_map/all_to_all | solution.py:84
  117.6 7.7 %reduce.12 = f32[4,131072]{1,0:T(4,128)S(1)} reduce(f32[4,1,131072]{2,1,0:T(1,128)} %copy-done.2, f32[]{:T(128)} %broadcast.1202), dimensions={1}, to_apply=%all_to_all.26.reduce_sub_computation | reduce | bytes 4194308 | tf_op jit(solution)/shard_map/all_to_all | solution.py:84
  131.5 10.4 %copy.115 = f32[8,1,2,32,32,32]{4,5,3,2,0,1:T(8,128)S(1)} copy(f32[8,1,2,32,32,32]{4,3,2,0,1,5:T(8,128)} %bitcast.155) | data formatting | bytes 4194304 | tf_op jit(solution)/shard_map/all_to_all | solution.py:84
  150.1 11.6 %copy.87 = f32[32,32,1,2,32,8]{1,0,5,4,3,2:T(8,128)} copy(f32[32,32,1,2,32,8]{4,5,1,3,2,0:T(8,128)} %maximum_bitcast_fusion) | data formatting | bytes 4194304 | tf_op jit(solution)/shard_map/transpose | solution.py:52
  168.3 11.6 %copy.86 = f32[32,32,1,2,32,8]{1,0,5,4,3,2:T(8,128)} copy(f32[32,32,1,2,32,8]{4,5,1,3,2,0:T(8,128)} %bitcast.152) | data formatting | bytes 4194304 | tf_op jit(solution)/shard_map/transpose | solution.py:51
  187.6 16.5 %all-gather.2.cloned.1.call-done = f32[3,2,1024,1024]{3,2,1,0:T(8,128)} async-done(((f32[3,2,16,1024]{3,2,1,0:T(8,128)}), f32[3,2,1024,1024]{3,2,1,0:T(8,128)}) %all-gather.2.cloned.1.call-update) | async-done | bytes 25165840 | tf_op jit(solution)/shard_map/all_gather | solution.py:62
  204.1 9.0 %fusion.11 = f32[1024,512]{1,0:T(8,128)S(1)} fusion(f32[1024,512]{0,1:T(8,128)S(1)} %reshape.1420, f32[3,2,1024,1024]{3,2,1,0:T(8,128)} %all-gather.2.cloned.1.call-done, s32[]{:T(128)S(6)} %select_n.52, s32[]{:T(128)S(6)} %add.95), kind=kOutput, calls=%fused_computation.25 | convolution fusion | flops 6442450944 | bytes 8388616 | tf_op jit(solution)/shard_map/dot_general | solution.py:70
  213.1 9.8 %fusion.17 = f32[1024,512]{1,0:T(8,128)} fusion(f32[1024,512]{1,0:T(8,128)S(1)} %fusion.11, f32[1024,512]{0,1:T(8,128)S(1)} %copy-done.3, f32[3,2,1024,1024]{3,2,1,0:T(8,128)} %all-gather.2.cloned.1.call-done, s32[]{:T(128)S(6)} %select_n.52), kind=kOutput, calls=%fused_computation.34 | convolution fusion | flops 6442975232 | bytes 10485764 | tf_op jit(solution)/shard_map/dot_general | solution.py:68
  229.8 11.4 %copy.116 = f32[32,1,2,32,32,8]{3,5,4,2,1,0:T(8,128)} copy(f32[32,1,2,32,32,8]{3,0,5,4,2,1:T(8,128)} %bitcast.156) | data formatting | bytes 4194304 | tf_op jit(solution)/shard_map/transpose | solution.py:57
  259.1 46.5 %all-to-all-done.1 = f32[4,1,131072]{2,1,0:T(1,128)} async-done(((f32[4,1,131072]{2,1,0:T(1,128)}), f32[4,1,131072]{2,1,0:T(1,128)}, u32[]{:S(2)}, u32[]{:S(2)}) %all-to-all-start.1) | async-done | bytes 2097184 | tf_op jit(solution)/shard_map/all_to_all | solution.py:91
  305.6 7.7 %reduce.13 = f32[4,131072]{1,0:T(4,128)S(1)} reduce(f32[4,1,131072]{2,1,0:T(1,128)} %all-to-all-done.1, f32[]{:T(128)} %broadcast.1202), dimensions={1}, to_apply=%all_to_all.30.reduce_sub_computation | reduce | bytes 4194308 | tf_op jit(solution)/shard_map/all_to_all | solution.py:91
  319.5 9.6 %copy.90 = f32[32,1,2,32,32,8]{4,5,3,2,1,0:T(8,128)} copy(f32[32,1,2,32,32,8]{3,5,4,2,1,0:T(8,128)} %bitcast.158) | data formatting | bytes 4194304 | tf_op jit(solution)/shard_map/all_to_all | solution.py:91
  345.2 9.0 %copy.93 = f32[32,32,8,1,2,32]{1,0,5,4,2,3:T(8,128)} copy(f32[32,32,8,1,2,32]{0,1,5,4,2,3:T(8,128)} %maximum_bitcast_fusion.1) | data formatting | bytes 4194304 | tf_op jit(solution)/shard_map/transpose | solution.py:52
  360.8 9.0 %copy.92 = f32[32,32,8,1,2,32]{1,0,5,4,2,3:T(8,128)} copy(f32[32,32,8,1,2,32]{0,1,5,4,2,3:T(8,128)} %fusion.43) | data formatting | bytes 4194304 | tf_op jit(solution)/shard_map/transpose | solution.py:51
  377.5 9.0 %fusion.10 = f32[1024,512]{1,0:T(8,128)S(1)} fusion(f32[1024,512]{0,1:T(8,128)S(1)} %reshape.1423, f32[3,2,1024,1024]{3,2,1,0:T(8,128)} %all-gather.2.cloned.1.call-done, s32[]{:T(128)S(6)} %select_n.51, s32[]{:T(128)S(6)} %add.95), kind=kOutput, calls=%fused_computation.22 | convolution fusion | flops 6442450944 | bytes 8388616 | tf_op jit(solution)/shard_map/dot_general | solution.py:70
  386.5 8.8 %fusion.16 = f32[1024,512]{1,0:T(8,128)S(1)} fusion(f32[1024,512]{1,0:T(8,128)S(1)} %fusion.10, f32[1024,512]{0,1:T(8,128)S(1)} %copy-done.5, f32[3,2,1024,1024]{3,2,1,0:T(8,128)} %all-gather.2.cloned.1.call-done, s32[]{:T(128)S(6)} %select_n.51), kind=kOutput, calls=%fused_computation.33 | convolution fusion | flops 6442975232 | bytes 10485764 | tf_op jit(solution)/shard_map/dot_general | solution.py:68
  395.3 8.3 %reshape.1424 = f32[32,32,8,1,2,32]{5,4,2,1,0,3:T(2,128)} reshape(f32[1024,512]{1,0:T(8,128)S(1)} %fusion.16) | data formatting | bytes 4194304 | tf_op jit(solution)/shard_map/reshape | solution.py:56
  403.6 14.2 %copy.94 = f32[32,32,8,1,2,32]{0,5,1,4,2,3:T(8,128)} copy(f32[32,32,8,1,2,32]{5,4,2,1,0,3:T(2,128)} %reshape.1424) | data formatting | bytes 4194304 | tf_op jit(solution)/shard_map/reshape | solution.py:56
  417.9 11.5 %fusion.8 = (f32[32,32,8,1,2,32]{1,0,5,4,2,3:T(8,128)}, f32[8,1,2,32,32,32]{4,3,5,2,0,1:T(8,128)}) fusion(f32[32,32,8,1,2,32]{0,5,1,4,2,3:T(8,128)} %copy.94, f32[32]{0:T(128)S(1)} %convert_element_type.123, f32[32]{0:T(128)S(1)} %convert_element_type.122, f32[32]{0:T(128)S(1)} %convert_element_type.121, f32[8]{0:T(128)S(1)} %convert_element_type.120), kind=kLoop, calls=%fused_computation.16 | loop fusion | flops 2097152 | bytes 6291872 | tf_op jit(solution)/shard_map/mul | solution.py:114
  444.7 7.7 %reshape.1425 = f32[1024,512]{0,1:T(8,128)} reshape(f32[32,32,8,1,2,32]{1,0,5,4,2,3:T(8,128)} %get-tuple-element.21) | data formatting | bytes 4194304 | tf_op jit(solution)/shard_map/reshape | solution.py:54
  452.5 8.8 %fusion.9 = f32[1024,512]{1,0:T(8,128)S(1)} fusion(f32[1024,512]{0,1:T(8,128)S(1)} %reshape.1426, f32[3,2,1024,1024]{3,2,1,0:T(8,128)} %all-gather.2.cloned.1.call-done, s32[]{:T(128)S(6)} %select_n.50, s32[]{:T(128)S(6)} %add.95), kind=kOutput, calls=%fused_computation.19 | convolution fusion | flops 6442450944 | bytes 8388616 | tf_op jit(solution)/shard_map/dot_general | solution.py:70
  461.3 9.1 %fusion.15 = f32[1024,512]{1,0:T(8,128)S(1)} fusion(f32[1024,512]{1,0:T(8,128)S(1)} %fusion.9, f32[1024,512]{0,1:T(8,128)S(1)} %copy-done.4, f32[3,2,1024,1024]{3,2,1,0:T(8,128)} %all-gather.2.cloned.1.call-done, s32[]{:T(128)S(6)} %select_n.50), kind=kOutput, calls=%fused_computation.32 | convolution fusion | flops 6442975232 | bytes 10485764 | tf_op jit(solution)/shard_map/dot_general | solution.py:68
  470.4 8.3 %reshape.1434 = f32[32,32,8,1,2,32]{5,4,2,1,0,3:T(2,128)} reshape(f32[1024,512]{1,0:T(8,128)S(1)} %fusion.15) | data formatting | bytes 4194304 | tf_op jit(solution)/shard_map/reshape | solution.py:56
  478.7 8.2 %fusion.3 = f32[8,2,32,32,32]{4,0,1,3,2:T(8,128)} fusion(f32[32,32,8,1,2,32]{5,4,2,1,0,3:T(2,128)} %reshape.1434, f32[32]{0:T(128)S(1)} %convert_element_type.127, f32[32]{0:T(128)S(1)} %convert_element_type.126, f32[32]{0:T(128)S(1)} %convert_element_type.125, f32[8]{0:T(128)S(1)} %convert_element_type.124), kind=kLoop, calls=%fused_computation.8 | loop fusion | flops 2097152 | bytes 4194720 | tf_op jit(solution)/shard_map/reduce_sum | solution.py:116
  487.0 66.3 %copy.97 = f32[8,2,32,32,32]{1,4,3,2,0:T(8,128)} copy(f32[8,2,32,32,32]{4,0,1,3,2:T(8,128)} %fusion.3) | data formatting | bytes 4194304 | tf_op jit(solution)/shard_map/reduce_sum | solution.py:116
  555.0 12.3 %psum.35 = f32[64,2]{1,0:T(8,128)S(1)} all-reduce(f32[64,2]{1,0:T(8,128)S(1)} %broadcast_multiply_fusion), channel_id=1, replica_groups=mesh['cuts_0'=4,'cuts_1'=4,'cuts_2'=2,'cuts_3'=2,'grp'=4] {'cuts_0'}, use_global_device_ids=true, to_apply=%region_16.17 | all-reduce | flops 128 | bytes 1024 | tf_op jit(solution)/shard_map/psum | solution.py:21
  567.3 11.1 %psum.36 = f32[64,2]{1,0:T(8,128)S(1)} all-reduce(f32[64,2]{1,0:T(8,128)S(1)} %psum.35), channel_id=1, replica_groups=mesh['cuts_0'=4,'cuts_1'=4,'cuts_2'=2,'cuts_3'=2,'grp'=4] {'cuts_1'}, use_global_device_ids=true, to_apply=%region_17.18 | all-reduce | flops 128 | bytes 1024 | tf_op jit(solution)/shard_map/psum | solution.py:21
  583.8 13.9 %psum.38 = f32[64,2]{1,0:T(8,128)S(1)} all-reduce(f32[64,2]{1,0:T(8,128)S(1)} %psum.37), channel_id=1, replica_groups=mesh['cuts_0'=4,'cuts_1'=4,'cuts_2'=2,'cuts_3'=2,'grp'=4] {'cuts_3'}, use_global_device_ids=true, to_apply=%region_19.20 | all-reduce | flops 128 | bytes 1024 | tf_op jit(solution)/shard_map/psum | solution.py:21
  597.6 13.5 %psum.39 = f32[64,2]{1,0:T(8,128)S(1)} all-reduce(f32[64,2]{1,0:T(8,128)S(1)} %psum.38), channel_id=1, replica_groups=mesh['cuts_0'=4,'cuts_1'=4,'cuts_2'=2,'cuts_3'=2,'grp'=4] {'grp'}, use_global_device_ids=true, to_apply=%region_20.21 | all-reduce | flops 128 | bytes 1024 | tf_op jit(solution)/shard_map/psum | solution.py:21
  (71 shorter events, 119.4 us)
Async XLA Ops:
  6.5 197.6 %all-gather.2.cloned.1.call-start = ((), (), s32[]{:S(2)}) async-start(), calls=%async_computation.2 | async-start | bytes 25559040 | tf_op jit(solution)/shard_map/all_gather | solution.py:62
  26.6 16.4 %copy-start.7 = (s32[3]{0:T(128)S(1)}, s32[3]{0:T(128)}, u32[]{:S(2)}) copy-start(s32[3]{0:T(128)} %param.8) | copy-start | bytes 40
  33.7 82.0 %all-to-all-start = ((f32[4,1,131072]{2,1,0:T(1,128)}), f32[4,1,131072]{2,1,0:T(1,128)S(1)}, u32[]{:S(2)}, u32[]{:S(2)}) async-start(f32[4,1,131072]{2,1,0:T(1,128)} %reshape.1435), calls=%async_computation | async-start | bytes 4194304 | tf_op jit(solution)/shard_map/all_to_all | solution.py:84
  115.7 1.4 copy-start.2
  143.0 3.2 copy-start
  204.1 9.0 %copy-start.3 = (f32[1024,512]{0,1:T(8,128)S(1)}, f32[1024,512]{0,1:T(8,128)}, u32[]{:S(2)}) copy-start(f32[1024,512]{0,1:T(8,128)} %reshape.1419) | copy-start | bytes 6291460
  241.3 15.8 %copy-start.9 = (s32[6,3]{0,1:T(4,128)S(1)}, s32[6,3]{0,1:T(4,128)}, u32[]{:S(2)}) copy-start(s32[6,3]{0,1:T(4,128)} %param.9) | copy-start | bytes 220
  241.3 15.9 %copy-start.8 = (s32[1,6]{1,0:T(1,128)S(1)}, s32[1,6]{1,0:T(1,128)}, u32[]{:S(2)}) copy-start(s32[1,6]{1,0:T(1,128)} %param.10) | copy-start | bytes 76
  241.3 17.7 %copy-start.6 = (s32[64,20]{0,1:T(8,128)S(1)}, s32[64,20]{0,1:T(8,128)}, u32[]{:S(2)}) copy-start(s32[64,20]{0,1:T(8,128)} %param.11) | copy-start | bytes 15364
  248.4 57.2 %all-to-all-start.1 = ((f32[4,1,131072]{2,1,0:T(1,128)}), f32[4,1,131072]{2,1,0:T(1,128)}, u32[]{:S(2)}, u32[]{:S(2)}) async-start(f32[4,1,131072]{2,1,0:T(1,128)} %reshape.1437), calls=%async_computation.1 | async-start | bytes 4194304 | tf_op jit(solution)/shard_map/all_to_all | solution.py:91
  329.1 5.8 copy-start.1
  377.5 9.0 %copy-start.5 = (f32[1024,512]{0,1:T(8,128)S(1)}, f32[1024,512]{0,1:T(8,128)}, u32[]{:S(2)}) copy-start(f32[1024,512]{0,1:T(8,128)} %reshape.1422) | copy-start | bytes 6291460
  452.5 8.8 %copy-start.4 = (f32[1024,512]{0,1:T(8,128)S(1)}, f32[1024,512]{0,1:T(8,128)}, u32[]{:S(2)}) copy-start(f32[1024,512]{0,1:T(8,128)} %reshape.1425) | copy-start | bytes 6291460
Sparse Core Ops, SparseCore 0:
  9.2 194.8 all-gather.1
where the time goes:
time: 626 us; the launch traced here: 619 us
  local copies, waits for them, and re-layouts  274 us (44%)
  waiting for transfers between devices  134 us (21%)
  other arithmetic  64.8 us (10%)
  blocking collectives  56.2 us (9%)
  matrix products  54.5 us (9%)
  between operations  19.9 us (3%)
  starting transfers between devices  15.4 us (2%)
    all_to_all x1, waiting for transfers between devices, on_device(): lax.all_to_all(current, 'grp', split_axis=5, concat_axis=0, tiled=True)  70.1 us
    reduce_sum x1, local copies, waits for them, and re-layouts, on_device(): summed = jnp.sum(current, axis=1)  66.3 us
    psum x5, blocking collectives, over_axes(): array = lax.psum(array, axis)  56.2 us
    unnamed x26, local copies, waits for them, and re-layouts  50.1 us
    all_to_all x1, waiting for transfers between devices, on_device(): lax.all_to_all(widened, 'grp', split_axis=0, concat_axis=5, tiled=True)  46.5 us
    reshape x6, local copies, waits for them, and re-layouts, local_pair(): outcome = produce(aligned.reshape(in_rows, -1), turned.reshape(in_rows, -1))  43 us
    reshape x4, local copies, waits for them, and re-layouts, local_pair(): outcome = outcome.reshape((extent, extent) + aligned.shape[2:])  35.8 us
    dot_general x3, matrix products, rows_from(): jnp.dot(columns[0], direct, precision=FULL_PRECISION, preferred_element_t...  27.8 us
  transfers between devices with their start and end apart: 3, of which 3 were waited for; matrix products, arithmetic and copies ran while one was open for 15% of the time, Pallas kernels for 0%

commit v1 on v0

v1 whole, which is shorter than its diff:
```python
from functools import partial

import jax
import jax.numpy as jnp
from jax import lax
from jax.experimental import pallas as pl
from jax.experimental.pallas import tpu as pltpu
from jax.sharding import Mesh
from jax.sharding import PartitionSpec as P

AXES = (4, 4, 2, 2)
CUTS = ("cuts_0", "cuts_1", "cuts_2", "cuts_3")
PLANE = ("cuts_0", "cuts_1")
COLUMN = ("cuts_2", "cuts_3", "grp")

BLOCKS_I, BLOCKS_J = 8, 8
LANES = 128
ROW_SECOND, ROW_THIRD, ROW_FIRST, ROW_BITS, PIECE = 0, 32, 64, 68, 72


def split_high_low(array):
    high = array.astype(jnp.bfloat16)
    return high, (array - high.astype(jnp.float32)).astype(jnp.bfloat16)


def dot(left, right):
    return jnp.dot(left, right, preferred_element_type=jnp.float32)


def pack_kernel(order_ref, bits_ref, gate_ref, boundary_ref, piece_ref, left_ref):
    step = pl.program_id(0)

    @pl.when(step == 0)
    def _():
        first, second, third = order_ref[0], order_ref[1], order_ref[2]
        member = lax.axis_index("grp")
        columns = pl.ds(pl.multiple_of(member * 256, 256), 256)
        real, imag = gate_ref[first, 0, :, columns], gate_ref[first, 1, :, columns]

        def interleaved(even, odd):
            parts = []
            for k0 in range(8):
                parts += [even[:, 32 * k0 : 32 * k0 + 32], odd[:, 32 * k0 : 32 * k0 + 32]]
            return jnp.concatenate(parts, axis=1)

        to_real, to_imag = interleaved(real, -imag), interleaved(imag, real)
        rows = []
        for block in range(BLOCKS_I):
            rows += [to_real[2 * block : 2 * block + 2], to_imag[2 * block : 2 * block + 2]]
        left = jnp.concatenate(rows, axis=0)
        high, low = split_high_low(left)
        left_ref[...] = jnp.concatenate((high, low), axis=0)

        lane = lax.broadcasted_iota(jnp.int32, (1, LANES), 1)
        bits = jnp.zeros((1, LANES), jnp.float32)
        for cut in range(6):
            bits = jnp.where(lane == cut, bits_ref[0, cut].astype(jnp.float32), bits)
        for part in range(2):
            at = 16 * part
            for block_j in range(BLOCKS_J):
                value = gate_ref[second, part, :, LANES * block_j : LANES * block_j + LANES]
                for block_i in range(BLOCKS_I):
                    to = block_i * BLOCKS_J + block_j
                    piece_ref[to, ROW_SECOND + at : ROW_SECOND + at + 16, :] = value
            whole = gate_ref[third, part]
            for block_i in range(BLOCKS_I):
                value = jnp.concatenate(
                    (
                        whole[:, 64 * block_i : 64 * block_i + 64],
                        whole[:, 512 + 64 * block_i : 512 + 64 * block_i + 64],
                    ),
                    axis=1,
                )
                for block_j in range(BLOCKS_J):
                    to = block_i * BLOCKS_J + block_j
                    piece_ref[to, ROW_THIRD + at : ROW_THIRD + at + 16, :] = value
        for to in range(BLOCKS_I * BLOCKS_J):
            piece_ref[to, ROW_BITS : ROW_BITS + 1, :] = bits

    left = left_ref[...]
    for half in range(2):
        pieces = []
        for quarter in range(4):
            right = boundary_ref[:, 4 * half + quarter, :]
            high, low = split_high_low(right)
            by_high = dot(left, high)
            pieces.append(by_high[:32] + by_high[32:] + dot(left[:32], low))
        value = jnp.concatenate(pieces, axis=1)
        for block_i in range(BLOCKS_I):
            to = block_i * BLOCKS_J + 2 * step + half
            piece_ref[to, ROW_FIRST : ROW_FIRST + 4, :] = value[4 * block_i : 4 * block_i + 4]


def amplitude_kernel(digit_ref, cut_ref, string_ref, got_ref, out_ref, pairs_ref, allowed_ref, strings_ref, third_ref, sum_ref):
    place = 0
    for axis, size in zip(CUTS, AXES, strict=True):
        place = place * size + lax.axis_index(axis)
    block_i, block_j = place // BLOCKS_J, place % BLOCKS_J

    bits = got_ref[pl.ds(ROW_BITS, 64, stride=PIECE), :]
    bits_t = jnp.concatenate((bits, jnp.zeros_like(bits)), axis=0).T[:8, :64]

    row = lax.broadcasted_iota(jnp.int32, (LANES, 64), 0)
    i1 = 16 * (row // 64) + 2 * block_i + (row // 32) % 2
    i2 = row % 32
    lane = lax.broadcasted_iota(jnp.int32, (64, LANES), 1)
    j2 = 4 * block_j + lane // 32
    j3 = lane % 32
    strings = string_ref[...]
    string_lane = lax.broadcasted_iota(jnp.int32, strings.shape, 1)
    pairs = jnp.ones((LANES, 64), jnp.float32)
    allowed = jnp.ones((64, LANES), jnp.float32)
    fixed = jnp.ones((64, 64), jnp.float32)
    for cut in range(6):
        layer, group, bit = cut_ref[cut, 0], cut_ref[cut, 1], cut_ref[cut, 2]
        by_row, by_column = bits_t[cut : cut + 1, :], bits[:, cut : cut + 1]
        on_i1 = (group == 1) & (layer < 2)
        on_i2 = (group == 2) & (layer == 1)
        on_j2 = (group == 2) & (layer == 0)
        on_j3 = (group == 3) & (layer == 0)
        index = jnp.where(on_i1, i1, i2)
        agrees = ((index >> bit) & 1).astype(jnp.float32) == by_row
        pairs = jnp.where(agrees | jnp.logical_not(on_i1 | on_i2), pairs, 0.0)
        index = jnp.where(on_j2, j2, j3)
        agrees = ((index >> bit) & 1).astype(jnp.float32) == by_column
        allowed = jnp.where(agrees | jnp.logical_not(on_j2 | on_j3), allowed, 0.0)
        chosen = jnp.where(string_lane == 5 * group + bit, strings, 0)
        digit_bit = jnp.sum(chosen, axis=1, keepdims=True).astype(jnp.float32)
        inner = on_i1 | on_i2 | on_j2 | on_j3
        fixed = jnp.where((digit_bit == by_row) | inner, fixed, 0.0)
    pairs_ref[...] = pairs.astype(jnp.bfloat16)
    allowed_ref[...] = allowed.astype(jnp.bfloat16)
    strings_ref[...] = fixed

    def outer(base, carry):
        for part in range(2):
            for inside in range(8):
                b = base * 8 + inside
                g1, g2 = digit_ref[1, b], digit_ref[2, b]
                source = (2 * g1 + g2 // 16) * PIECE + ROW_THIRD + 16 * part + g2 % 16
                third_ref[part, inside : inside + 1, :] = got_ref[pl.ds(source, 1), :]
        third_real, third_imag = third_ref[0].T, third_ref[1].T
        allowed = allowed_ref[...]
        for inside in range(8):
            b = base * 8 + inside
            g0, g3 = digit_ref[0, b], digit_ref[3, b]
            row_b = strings_ref[pl.ds(b, 1), :].astype(jnp.bfloat16)
            count = dot(pairs_ref[...] * row_b, allowed)
            start = (g3 // 16) * PIECE + ROW_SECOND + g3 % 16
            second_real = got_ref[pl.ds(start, 32, stride=2 * PIECE), :]
            second_imag = got_ref[pl.ds(start + 16, 32, stride=2 * PIECE), :]
            total_real = jnp.zeros((1, LANES), jnp.float32)
            total_imag = jnp.zeros((1, LANES), jnp.float32)
            for q in range(4):
                rows = slice(32 * q, 32 * q + 32)
                weight_real = third_real[rows, inside : inside + 1] * count[rows]
                weight_imag = third_imag[rows, inside : inside + 1] * count[rows]
                real = jnp.sum(weight_real * second_real - weight_imag * second_imag, axis=0, keepdims=True)
                imag = jnp.sum(weight_real * second_imag + weight_imag * second_real, axis=0, keepdims=True)
                source = (2 * g0 + q // 2) * PIECE + ROW_FIRST + q % 2
                first_real = got_ref[pl.ds(source, 1), :]
                first_imag = got_ref[pl.ds(source + 2, 1), :]
                total_real += real * first_real - imag * first_imag
                total_imag += real * first_imag + imag * first_real
            sum_ref[pl.ds(b, 1), :] = total_real
            sum_ref[pl.ds(64 + b, 1), :] = total_imag
        return carry

    lax.fori_loop(0, 8, outer, 0)
    result = jnp.sum(sum_ref[...].T, axis=0, keepdims=True)
    for to in range(16):
        out_ref[to] = result


def all_reduced(copies, axes, rows):
    got = lax.all_to_all(copies, axes, 0, 0, tiled=True)
    total = jnp.sum(got, axis=0, keepdims=True)
    return jnp.broadcast_to(total, (rows,) + total.shape[1:])


def on_device(boundary, gate_stack, layer_order, cut_index, slice_bits, bitstrings):
    smem = pl.BlockSpec(memory_space=pltpu.SMEM)
    vmem = pl.BlockSpec(memory_space=pltpu.VMEM)
    right = boundary.reshape(512, 32, 32)
    pieces = pl.pallas_call(
        pack_kernel,
        grid=(4,),
        out_shape=jax.ShapeDtypeStruct((64, PIECE, LANES), jnp.float32),
        in_specs=[
            smem,
            smem,
            pl.BlockSpec((3, 2, 16, 1024), lambda step: (0, 0, 0, 0)),
            pl.BlockSpec((512, 8, 32), lambda step: (0, step, 0)),
        ],
        out_specs=pl.BlockSpec((64, PIECE, LANES), lambda step: (0, 0, 0)),
        scratch_shapes=[pltpu.VMEM((64, 512), jnp.bfloat16)],
        name="pack",
    )(layer_order, slice_bits, gate_stack, right)
    got = lax.all_to_all(pieces, CUTS, 0, 0, tiled=True).reshape(64 * PIECE, LANES)

    weights = jnp.left_shift(jnp.ones((5,), jnp.int32), jnp.arange(5, dtype=jnp.int32))
    digits = jnp.sum(bitstrings.reshape(64, 4, 5) * weights, axis=2).T
    partial_sums = pl.pallas_call(
        amplitude_kernel,
        out_shape=jax.ShapeDtypeStruct((16, 1, LANES), jnp.float32),
        in_specs=[smem, smem, vmem, vmem],
        out_specs=vmem,
        scratch_shapes=[
            pltpu.VMEM((LANES, 64), jnp.bfloat16),
            pltpu.VMEM((64, LANES), jnp.bfloat16),
            pltpu.VMEM((64, 64), jnp.float32),
            pltpu.VMEM((2, 8, LANES), jnp.float32),
            pltpu.VMEM((LANES, LANES), jnp.float32),
        ],
        name="amplitude",
    )(digits, cut_index, bitstrings, got)
    total = all_reduced(partial_sums, COLUMN, 16)
    total = all_reduced(total, PLANE, 1)
    return total.reshape(2, 64).T


def solution(mesh):
    finer = Mesh(
        mesh.devices.reshape(AXES + (mesh.shape["grp"],)),
        CUTS + ("grp",),
    )
    return jax.shard_map(
        on_device,
        mesh=finer,
        in_specs=(
            P("grp", None, None, None, None),
            P(None, None, CUTS, None),
            P(),
            P(),
            P(CUTS, None),
            P(),
        ),
        out_specs=P(),
        check_vma=False,
    )
```

time: 626 us -> 107 us (0.17); the launches traced: 619 us -> 107 us
  local copies, waits for them, and re-layouts: 274 us -> 3.43 us
  waiting for transfers between devices: 134 us -> 30.9 us
  other arithmetic: 64.8 us -> 0.72 us
  matrix products: 54.5 us -> 0 us
  Pallas kernels: 0 us -> 33.7 us
  blocking collectives: 56.2 us -> 27.7 us
  between operations: 19.9 us -> 0.03 us
    all_to_all x2 -> x1, waiting for transfers between devices: 117 us -> 30.9 us  [on_device(): lax.all_to_all(pieces, CUTS, 0, 0, tiled=True).reshape(64 * PIECE, LANES)]
    reshape x10 -> x1, local copies, waits for them, and re-layouts: 78.8 us -> 0.01 us  [on_device(): digits = jnp.sum(bitstrings.reshape(64, 4, 5) * weights, axis=2).T]
    reduce_sum x1 -> x0, local copies, waits for them, and re-layouts: 66.3 us -> none  [on_device(): summed = jnp.sum(current, axis=1)]
    psum x5 -> x0, blocking collectives: 56.2 us -> none  [over_axes(): array = lax.psum(array, axis)]
    dot_general x6 -> x0, matrix products: 54.5 us -> none  [the longest x3 27.8 us: rows_from(): jnp.dot(columns[0], direct, precision=FULL_PRECISION, preferred_element_t...]
    transpose x5 -> x0, local copies, waits for them, and re-layouts: 52.6 us -> none  [the longest x2 20.6 us: local_pair(): turned = jnp.moveaxis(rotated(current), (first_dim, second_dim), (0, 1))]
    unnamed x26 -> x8, local copies, waits for them, and re-layouts: 50.1 us -> 2.77 us
    pallas_call x0 -> x2, Pallas kernels: none -> 33.7 us  [the longest x1 25.5 us: on_device(): pl.pallas_call(pack_kernel, grid=(4,), out_shape=jax.ShapeDtypeStruct((64...]
  transfers between devices with their start and end apart: 3 -> 1, of which waited for: 3 -> 1; matrix products, arithmetic and copies ran while one was open for 15% -> 2% of each run, Pallas kernels for 0% -> 0%
where the time goes in v1:
time: 107 us
  Pallas kernels  33.7 us (31%)
  waiting for transfers between devices  30.9 us (29%)
  blocking collectives  27.7 us (26%)
  starting transfers between devices  10.5 us (10%)
  local copies, waits for them, and re-layouts  3.43 us (3%)
    all_to_all x1, waiting for transfers between devices, on_device(): lax.all_to_all(pieces, CUTS, 0, 0, tiled=True).reshape(64 * PIECE, LANES)  30.9 us
    all_to_all x2, blocking collectives, all_reduced(): got = lax.all_to_all(copies, axes, 0, 0, tiled=True)  27.7 us
    pallas_call x1, Pallas kernels, on_device(): pl.pallas_call(pack_kernel, grid=(4,), out_shape=jax.ShapeDtypeStruct((64...  25.5 us
    all_to_all x1, starting transfers between devices, on_device(): lax.all_to_all(pieces, CUTS, 0, 0, tiled=True).reshape(64 * PIECE, LANES)  10.5 us
    pallas_call x1, Pallas kernels, on_device(): pl.pallas_call(amplitude_kernel, out_shape=jax.ShapeDtypeStruct((16, 1, L...  8.18 us
    unnamed x8, local copies, waits for them, and re-layouts  2.77 us
  transfers between devices with their start and end apart: 1, of which 1 were waited for; matrix products, arithmetic and copies ran while one was open for 2% of the time, Pallas kernels for 0%

profile of v1, /device:TPU:1, one launch (start us, length us, event | category | flops | bytes accessed | tf_op | source)
XLA Modules:
  0.0 106.9 jit_solution(5012794335227832032)
XLA Ops:
  0.0 25.5 %pack.1 = f32[64,72,128]{2,1,0:T(8,128)} custom-call(s32[3]{0:T(128)} %order_ref.1, s32[1,6]{1,0:T(1,128)} %bits_ref.1, f32[3,2,16,1024]{3,2,1,0:T(8,128)} %gate_ref.1, f32[512,32,32]{2,1,0:T(8,128)} %bitcast.8), custom_call_target="tpu_custom_call" | custom-call | tf_op jit(solution)/shard_map/pack/pallas_call | solution.py:185
  25.5 0.0 copy-start.1
  25.5 0.0 copy-start.2
  25.5 10.5 %all-to-all-start = ((f32[64,72,128]{2,1,0:T(8,128)}), f32[64,72,128]{2,1,0:T(8,128)S(1)}, u32[]{:S(2)}, u32[]{:S(2)}) async-start(f32[64,72,128]{2,1,0:T(8,128)} %pack.1), calls=%async_computation | async-start | bytes 4718592 | tf_op jit(solution)/shard_map/all_to_all | solution.py:199
  36.0 0.0 copy-done.1
  36.0 0.7 copy.14.string_ref
  36.7 0.0 copy-done.2
  36.7 0.7 copy.13.cut_ref
  37.3 0.7 multiply_reduce_fusion
  38.0 30.9 %all-to-all-done = f32[64,72,128]{2,1,0:T(8,128)S(1)} async-done(((f32[64,72,128]{2,1,0:T(8,128)}), f32[64,72,128]{2,1,0:T(8,128)S(1)}, u32[]{:S(2)}, u32[]{:S(2)}) %all-to-all-start) | async-done | bytes 2359328 | tf_op jit(solution)/shard_map/all_to_all | solution.py:199
  68.9 0.0 copy-start
  68.9 1.4 %copy-done = f32[64,72,128]{2,1,0:T(8,128)} copy-done((f32[64,72,128]{2,1,0:T(8,128)}, f32[64,72,128]{2,1,0:T(8,128)S(1)}, u32[]{:S(2)}) %copy-start) | copy-done | bytes 2359320
  70.3 8.2 %amplitude.1 = f32[16,1,128]{2,1,0:T(1,128)} custom-call(s32[4,64]{1,0:T(4,128)} %bitcast.10, s32[6,3]{1,0:T(8,128)} %copy.13.cut_ref, s32[64,20]{1,0:T(8,128)} %copy.14.string_ref, f32[4608,128]{1,0:T(8,128)} %bitcast.7), custom_call_target="tpu_custom_call" | custom-call | tf_op jit(solution)/shard_map/amplitude/pallas_call | solution.py:203
  78.5 15.8 %all_to_all.15 = f32[16,1,128]{2,1,0:T(1,128)S(1)} all-to-all(f32[16,1,128]{2,1,0:T(1,128)} %amplitude.1), channel_id=1, replica_groups=mesh['cuts_0'=4,'cuts_1'=4,'cuts_2'=2,'cuts_3'=2,'grp'=4] {'cuts_2','cut..., dimensions={0} | all-to-all | bytes 16384 | tf_op jit(solution)/shard_map/all_to_all | solution.py:176
  94.3 11.9 %all_to_all.16 = f32[16,1,128]{2,1,0:T(1,128)S(1)} all-to-all(f32[16,1,128]{2,1,0:T(1,128)S(1)} %broadcast_in_dim.2), channel_id=1, replica_groups=mesh['cuts_0'=4,'cuts_1'=4,'cuts_2'=2,'cuts_3'=2,'grp'=4] {'cuts_0','cut..., dimensions={0} | all-to-all | bytes 16384 | tf_op jit(solution)/shard_map/all_to_all | solution.py:176
  106.3 0.6 reshape_broadcast_in_dim.3
  (5 shorter events, 0.1 us)
Async XLA Ops:
  25.5 10.5 %copy-start.1 = (s32[64,20]{0,1:T(8,128)S(1)}, s32[64,20]{0,1:T(8,128)}, u32[]{:S(2)}) copy-start(s32[64,20]{0,1:T(8,128)} %param.11) | copy-start | bytes 15364
  25.5 11.2 %copy-start.2 = (s32[6,3]{0,1:T(4,128)S(1)}, s32[6,3]{0,1:T(4,128)}, u32[]{:S(2)}) copy-start(s32[6,3]{0,1:T(4,128)} %param.9) | copy-start | bytes 220
  25.5 43.4 %all-to-all-start = ((f32[64,72,128]{2,1,0:T(8,128)}), f32[64,72,128]{2,1,0:T(8,128)S(1)}, u32[]{:S(2)}, u32[]{:S(2)}) async-start(f32[64,72,128]{2,1,0:T(8,128)} %pack.1), calls=%async_computation | async-start | bytes 4718592 | tf_op jit(solution)/shard_map/all_to_all | solution.py:199
  68.9 1.4 %copy-start = (f32[64,72,128]{2,1,0:T(8,128)}, f32[64,72,128]{2,1,0:T(8,128)S(1)}, u32[]{:S(2)}) copy-start(f32[64,72,128]{2,1,0:T(8,128)S(1)} %all-to-all-done) | copy-start | bytes 7077892

commit v2 on v1

v2 whole, which is shorter than its diff:
```python
from functools import partial

import jax
import jax.numpy as jnp
from jax import lax
from jax.experimental import pallas as pl
from jax.experimental.pallas import tpu as pltpu
from jax.sharding import Mesh
from jax.sharding import PartitionSpec as P

AXES = (4, 4, 2, 2)
CUTS = ("cuts_0", "cuts_1", "cuts_2", "cuts_3")
PLANE = ("cuts_0", "cuts_1")
COLUMN = ("cuts_2", "cuts_3", "grp")

BLOCKS_I, BLOCKS_J = 8, 8
LANES = 128
ROW_SECOND, ROW_THIRD, ROW_FIRST, ROW_BITS, PIECE = 0, 32, 64, 68, 72


def split_high_low(array):
    high = array.astype(jnp.bfloat16)
    return high, (array - high.astype(jnp.float32)).astype(jnp.bfloat16)


def dot(left, right):
    return jnp.dot(left, right, preferred_element_type=jnp.float32)


def pack_kernel(order_hbm, bits_hbm, string_hbm, gate_hbm, boundary_hbm, piece_ref, row_ref, order_ref, bits_ref, string_ref, gate_ref, boundary_ref, left_ref, sems):
    small = [
        pltpu.make_async_copy(order_hbm, order_ref, sems.at[0]),
        pltpu.make_async_copy(bits_hbm, bits_ref, sems.at[1]),
        pltpu.make_async_copy(string_hbm, string_ref, sems.at[2]),
        pltpu.make_async_copy(gate_hbm, gate_ref, sems.at[3]),
    ]
    large = [
        pltpu.make_async_copy(boundary_hbm.at[:, pl.ds(8 * step, 8), :], boundary_ref.at[step], sems.at[4 + step])
        for step in range(4)
    ]
    for copy in small + large:
        copy.start()
    for copy in small:
        copy.wait()

    first, second, third = order_ref[0], order_ref[1], order_ref[2]
    member = lax.axis_index("grp")
    columns = pl.ds(pl.multiple_of(member * 256, 256), 256)
    real, imag = gate_ref[first, 0, :, columns], gate_ref[first, 1, :, columns]

    def interleaved(even, odd):
        parts = []
        for k0 in range(8):
            parts += [even[:, 32 * k0 : 32 * k0 + 32], odd[:, 32 * k0 : 32 * k0 + 32]]
        return jnp.concatenate(parts, axis=1)

    to_real, to_imag = interleaved(real, -imag), interleaved(imag, real)
    rows = []
    for block in range(BLOCKS_I):
        rows += [to_real[2 * block : 2 * block + 2], to_imag[2 * block : 2 * block + 2]]
    left = jnp.concatenate(rows, axis=0)
    high, low = split_high_low(left)
    left_ref[...] = jnp.concatenate((high, low), axis=0)

    strings = string_ref[...]

    def digit(group):
        total = strings[5 * group : 5 * group + 1]
        for bit in range(1, 5):
            total = total + (strings[5 * group + bit : 5 * group + bit + 1] << bit)
        return total

    g0, g1, g2, g3 = (digit(group) for group in range(4))
    row_ref[0:1, :] = 2 * g0 * PIECE + ROW_FIRST
    row_ref[1:2, :] = (g3 >> 4) * PIECE + ROW_SECOND + (g3 & 15)
    row_ref[2:3, :] = (2 * g1 + (g2 >> 4)) * PIECE + ROW_THIRD + (g2 & 15)

    lane = lax.broadcasted_iota(jnp.int32, (1, LANES), 1)
    bits = jnp.zeros((1, LANES), jnp.float32)
    for cut in range(6):
        bits = jnp.where(lane == cut, bits_ref[0, cut].astype(jnp.float32), bits)
    for part in range(2):
        at = 16 * part
        for block_j in range(BLOCKS_J):
            value = gate_ref[second, part, :, LANES * block_j : LANES * block_j + LANES]
            for block_i in range(BLOCKS_I):
                to = block_i * BLOCKS_J + block_j
                piece_ref[to, ROW_SECOND + at : ROW_SECOND + at + 16, :] = value
        whole = gate_ref[third, part]
        for block_i in range(BLOCKS_I):
            value = jnp.concatenate(
                (
                    whole[:, 64 * block_i : 64 * block_i + 64],
                    whole[:, 512 + 64 * block_i : 512 + 64 * block_i + 64],
                ),
                axis=1,
            )
            for block_j in range(BLOCKS_J):
                to = block_i * BLOCKS_J + block_j
                piece_ref[to, ROW_THIRD + at : ROW_THIRD + at + 16, :] = value
    for to in range(BLOCKS_I * BLOCKS_J):
        piece_ref[to, ROW_BITS : ROW_BITS + 1, :] = bits

    left = left_ref[...]
    for step in range(4):
        large[step].wait()
        flat = boundary_ref.at[step].reshape(4096, 32)
        for half in range(2):
            right = jnp.concatenate(
                [flat[pl.ds(4 * half + quarter, 512, stride=8), :] for quarter in range(4)], axis=1
            )
            high, low = split_high_low(right)
            by_high = dot(left, high)
            value = by_high[:32] + by_high[32:] + dot(left[:32], low)
            for block_i in range(BLOCKS_I):
                to = block_i * BLOCKS_J + 2 * step + half
                piece_ref[to, ROW_FIRST : ROW_FIRST + 4, :] = value[4 * block_i : 4 * block_i + 4]


def amplitude_kernel(row_ref, cut_ref, string_ref, got_ref, out_ref, pairs_ref, allowed_ref, fixed_ref, third_ref, sum_ref):
    place = 0
    for axis, size in zip(CUTS, AXES, strict=True):
        place = place * size + lax.axis_index(axis)
    block_i, block_j = place // BLOCKS_J, place % BLOCKS_J

    bits = got_ref[pl.ds(ROW_BITS, 64, stride=PIECE), :]
    bits_t = jnp.concatenate((bits, jnp.zeros_like(bits)), axis=0).T[:8, :64]

    row = lax.broadcasted_iota(jnp.int32, (LANES, 64), 0)
    i1 = 16 * (row >> 6) + 2 * block_i + ((row >> 5) & 1)
    i2 = row & 31
    lane = lax.broadcasted_iota(jnp.int32, (64, LANES), 1)
    j2 = 4 * block_j + (lane >> 5)
    j3 = lane & 31
    pairs = jnp.ones((LANES, 64), jnp.float32)
    allowed = jnp.ones((64, LANES), jnp.float32)
    fixed = jnp.ones((64, 64), jnp.float32)
    for cut in range(6):
        layer, group, bit = cut_ref[0, cut], cut_ref[1, cut], cut_ref[2, cut]
        by_row, by_column = bits_t[cut : cut + 1, :], bits[:, cut : cut + 1]
        on_i1 = (group == 1) & (layer < 2)
        on_i2 = (group == 2) & (layer == 1)
        on_j2 = (group == 2) & (layer == 0)
        on_j3 = (group == 3) & (layer == 0)
        index = jnp.where(on_i1, i1, i2)
        agrees = ((index >> bit) & 1).astype(jnp.float32) == by_row
        pairs = jnp.where(agrees | jnp.logical_not(on_i1 | on_i2), pairs, 0.0)
        index = jnp.where(on_j2, j2, j3)
        agrees = ((index >> bit) & 1).astype(jnp.float32) == by_column
        allowed = jnp.where(agrees | jnp.logical_not(on_j2 | on_j3), allowed, 0.0)
        chosen = string_ref[pl.ds(5 * group + bit, 1), :].astype(jnp.float32)
        inner = on_i1 | on_i2 | on_j2 | on_j3
        fixed = jnp.where((chosen == bits[:, cut : cut + 1]) | inner, fixed, 0.0)
    pairs_ref[...] = pairs.astype(jnp.bfloat16)
    allowed_ref[...] = allowed.astype(jnp.bfloat16)
    fixed = jnp.concatenate((fixed, jnp.zeros_like(fixed)), axis=1)
    fixed_ref[...] = jnp.concatenate((fixed, jnp.zeros_like(fixed)), axis=0).T[:64, :64]

    def outer(base, carry):
        for part in range(2):
            for inside in range(8):
                source = row_ref[2, base * 8 + inside] + 16 * part
                third_ref[part, inside : inside + 1, :] = got_ref[pl.ds(source, 1), :]
        third_real, third_imag = third_ref[0].T, third_ref[1].T
        for inside in range(8):
            b = base * 8 + inside
            row_b = fixed_ref[pl.ds(b, 1), :].astype(jnp.bfloat16)
            count = dot(pairs_ref[...] * row_b, allowed_ref[...])
            start, source = row_ref[1, b], row_ref[0, b]
            total_real = jnp.zeros((8, LANES), jnp.float32)
            total_imag = jnp.zeros((8, LANES), jnp.float32)
            for q in range(4):
                real = jnp.zeros((8, LANES), jnp.float32)
                imag = jnp.zeros((8, LANES), jnp.float32)
                for part in range(4):
                    rows = slice(32 * q + 8 * part, 32 * q + 8 * part + 8)
                    at = start + 16 * PIECE * part
                    second_real = got_ref[pl.ds(at, 8, stride=2 * PIECE), :]
                    second_imag = got_ref[pl.ds(at + 16, 8, stride=2 * PIECE), :]
                    weight_real = third_real[rows, inside : inside + 1] * count[rows]
                    weight_imag = third_imag[rows, inside : inside + 1] * count[rows]
                    real += weight_real * second_real - weight_imag * second_imag
                    imag += weight_real * second_imag + weight_imag * second_real
                at = source + (q // 2) * PIECE + q % 2
                first_real = got_ref[pl.ds(at, 1), :]
                first_imag = got_ref[pl.ds(at + 2, 1), :]
                total_real += real * first_real - imag * first_imag
                total_imag += real * first_imag + imag * first_real
            sum_ref[pl.ds(b, 1), :] = jnp.sum(total_real, axis=0, keepdims=True)
            sum_ref[pl.ds(64 + b, 1), :] = jnp.sum(total_imag, axis=0, keepdims=True)
        return carry

    lax.fori_loop(0, 8, outer, 0)
    result = jnp.sum(sum_ref[...].T, axis=0, keepdims=True)
    for to in range(16):
        out_ref[to] = result


def all_reduced(copies, axes, rows):
    got = lax.all_to_all(copies, axes, 0, 0, tiled=True)
    total = jnp.sum(got, axis=0, keepdims=True)
    return jnp.broadcast_to(total, (rows,) + total.shape[1:])


def on_device(boundary, gate_stack, layer_order, cut_index, slice_bits, bitstrings):
    smem = pl.BlockSpec(memory_space=pltpu.SMEM)
    vmem = pl.BlockSpec(memory_space=pltpu.VMEM)
    strings = bitstrings.T
    in_hbm = partial(pltpu.with_memory_space_constraint, memory_space=pltpu.HBM)
    hbm = pl.BlockSpec(memory_space=pltpu.HBM)
    pieces, rows = pl.pallas_call(
        pack_kernel,
        out_shape=(
            jax.ShapeDtypeStruct((64, PIECE, LANES), jnp.float32),
            jax.ShapeDtypeStruct((8, 64), jnp.int32),
        ),
        in_specs=[hbm] * 5,
        out_specs=(vmem, vmem),
        scratch_shapes=[
            pltpu.SMEM((3,), jnp.int32),
            pltpu.SMEM((1, 6), jnp.int32),
            pltpu.VMEM((20, 64), jnp.int32),
            pltpu.VMEM((3, 2, 16, 1024), jnp.float32),
            pltpu.VMEM((4, 512, 8, 32), jnp.float32),
            pltpu.VMEM((64, 512), jnp.bfloat16),
            pltpu.SemaphoreType.DMA((8,)),
        ],
        compiler_params=pltpu.CompilerParams(vmem_limit_bytes=24 << 20),
        name="pack",
    )(*(in_hbm(x) for x in (layer_order, slice_bits, strings, gate_stack, boundary.reshape(512, 32, 32))))
    got = lax.all_to_all(pieces, CUTS, 0, 0, tiled=True).reshape(64 * PIECE, LANES)
    partial_sums = pl.pallas_call(
        amplitude_kernel,
        out_shape=jax.ShapeDtypeStruct((16, 1, LANES), jnp.float32),
        in_specs=[smem, smem, vmem, vmem],
        out_specs=vmem,
        scratch_shapes=[
            pltpu.VMEM((LANES, 64), jnp.bfloat16),
            pltpu.VMEM((64, LANES), jnp.bfloat16),
            pltpu.VMEM((64, 64), jnp.float32),
            pltpu.VMEM((2, 8, LANES), jnp.float32),
            pltpu.VMEM((LANES, LANES), jnp.float32),
        ],
        compiler_params=pltpu.CompilerParams(vmem_limit_bytes=12 << 20),
        name="amplitude",
    )(rows, in_hbm(cut_index.T), in_hbm(strings), got)
    total = all_reduced(partial_sums, COLUMN, 16)
    total = all_reduced(total, PLANE, 1)
    return total.reshape(2, 64).T


def solution(mesh):
    finer = Mesh(
        mesh.devices.reshape(AXES + (mesh.shape["grp"],)),
        CUTS + ("grp",),
    )
    return jax.shard_map(
        on_device,
        mesh=finer,
        in_specs=(
            P("grp", None, None, None, None),
            P(None, None, CUTS, None),
            P(),
            P(),
            P(CUTS, None),
            P(),
        ),
        out_specs=P(),
        check_vma=False,
    )
```

time: 107 us -> 83 us (0.78)
  blocking collectives: 27.7 us -> 71.4 us
  waiting for transfers between devices: 30.9 us -> 0 us
  Pallas kernels: 33.7 us -> 10.7 us
  starting transfers between devices: 10.5 us -> 0 us
  local copies, waits for them, and re-layouts: 3.43 us -> 0.65 us
    all_to_all x0 -> x1, blocking collectives: none -> 45.8 us  [on_device(): lax.all_to_all(pieces, CUTS, 0, 0, tiled=True).reshape(64 * PIECE, LANES)]
    all_to_all x1 -> x0, waiting for transfers between devices: 30.9 us -> none  [on_device(): lax.all_to_all(pieces, CUTS, 0, 0, tiled=True).reshape(64 * PIECE, LANES)]
    pallas_call x1, Pallas kernels: 25.5 us -> 4.53 us  [on_device(): pl.pallas_call(pack_kernel, out_shape=(jax.ShapeDtypeStruct((64, PIECE, L...]
    all_to_all x1 -> x0, starting transfers between devices: 10.5 us -> none  [on_device(): lax.all_to_all(pieces, CUTS, 0, 0, tiled=True).reshape(64 * PIECE, LANES)]
    unnamed x8 -> x0, local copies, waits for them, and re-layouts: 2.77 us -> none
    all_to_all x2, blocking collectives: 27.7 us -> 25.6 us  [all_reduced(): got = lax.all_to_all(copies, axes, 0, 0, tiled=True)]
    pallas_call x1, Pallas kernels: 8.18 us -> 6.13 us  [on_device(): pl.pallas_call(amplitude_kernel, out_shape=jax.ShapeDtypeStruct((16, 1, L...]
  transfers between devices with their start and end apart: 1 -> 0, of which waited for: 1 -> 0; matrix products, arithmetic and copies ran while one was open for 2% -> 0% of each run, Pallas kernels for 0% -> 0%
where the time goes in v2:
time: 83 us; the launch traced here: 82.8 us
  blocking collectives  71.4 us (86%)
  Pallas kernels  10.7 us (13%)
    all_to_all x1, blocking collectives, on_device(): lax.all_to_all(pieces, CUTS, 0, 0, tiled=True).reshape(64 * PIECE, LANES)  45.8 us
    all_to_all x2, blocking collectives, all_reduced(): got = lax.all_to_all(copies, axes, 0, 0, tiled=True)  25.6 us
    pallas_call x1, Pallas kernels, on_device(): pl.pallas_call(amplitude_kernel, out_shape=jax.ShapeDtypeStruct((16, 1, L...  6.13 us
    pallas_call x1, Pallas kernels, on_device(): pl.pallas_call(pack_kernel, out_shape=(jax.ShapeDtypeStruct((64, PIECE, L...  4.53 us

profile of v2, /device:TPU:1, one launch (start us, length us, event | category | flops | bytes accessed | tf_op | source)
XLA Modules:
  0.0 82.8 jit_solution(7079327542852844060)
XLA Ops:
  0.0 4.5 %pack.1 = (f32[64,72,128]{2,1,0:T(8,128)S(1)}, s32[8,64]{1,0:T(8,128)S(1)}) custom-call(s32[3]{0:T(128)} %order_hbm.1, s32[1,6]{1,0:T(1,128)} %bits_hbm.1, s32[20,64]{1,0:T(8,128)} %bitcast.8, f32[3,2,16,1024]{3,2,1,0:T(8,128)} %gate_hbm.1, f32[512,32,32]{2,1,0:T(8,128)} %bitcast.7), custom_call_target="tpu_custom_call" | custom-call | tf_op jit(solution)/shard_map/pack/pallas_call | solution.py:211
  4.5 45.8 %all_to_all.15 = f32[64,72,128]{2,1,0:T(8,128)S(1)} all-to-all(f32[64,72,128]{2,1,0:T(8,128)S(1)} %get-tuple-element.8), channel_id=1, replica_groups=mesh['cuts_0'=4,'cuts_1'=4,'cuts_2'=2,'cuts_3'=2,'grp'=4] {'cuts_0','cut..., dimensions={0} | all-to-all | bytes 4718592 | tf_op jit(solution)/shard_map/all_to_all | solution.py:231
  50.4 6.1 %amplitude.1 = f32[16,1,128]{2,1,0:T(1,128)S(1)} custom-call(s32[8,64]{1,0:T(8,128)S(1)} %get-tuple-element.7.row_ref, s32[3,6]{1,0:T(4,128)} %bitcast.11, s32[20,64]{1,0:T(8,128)} %bitcast.9, f32[4608,128]{1,0:T(8,128)S(1)} %bitcast.6), custom_call_target="tpu_custom_call" | custom-call | tf_op jit(solution)/shard_map/amplitude/pallas_call | solution.py:232
  56.5 14.9 %all_to_all.16 = f32[16,1,128]{2,1,0:T(1,128)S(1)} all-to-all(f32[16,1,128]{2,1,0:T(1,128)S(1)} %amplitude.1), channel_id=1, replica_groups=mesh['cuts_0'=4,'cuts_1'=4,'cuts_2'=2,'cuts_3'=2,'grp'=4] {'cuts_2','cut..., dimensions={0} | all-to-all | bytes 16384 | tf_op jit(solution)/shard_map/all_to_all | solution.py:200
  71.4 10.7 %all_to_all.17 = f32[16,1,128]{2,1,0:T(1,128)S(1)} all-to-all(f32[16,1,128]{2,1,0:T(1,128)S(1)} %broadcast_in_dim.2), channel_id=1, replica_groups=mesh['cuts_0'=4,'cuts_1'=4,'cuts_2'=2,'cuts_3'=2,'grp'=4] {'cuts_0','cut..., dimensions={0} | all-to-all | bytes 16384 | tf_op jit(solution)/shard_map/all_to_all | solution.py:200
  82.2 0.6 reshape_broadcast_in_dim.3
  (3 shorter events, 0.1 us)

commit v3 on v2

v3 whole, which is shorter than its diff:
```python
from functools import partial

import jax
import jax.numpy as jnp
from jax import lax
from jax.experimental import pallas as pl
from jax.experimental.pallas import tpu as pltpu
from jax.sharding import Mesh
from jax.sharding import PartitionSpec as P

AXES = (4, 4, 2, 2)
CUTS = ("cuts_0", "cuts_1", "cuts_2", "cuts_3")
WAVE = ("cuts_1", "cuts_2", "cuts_3")
PLANE = ("cuts_0", "cuts_1")
COLUMN = ("cuts_2", "cuts_3", "grp")

BLOCKS_I, BLOCKS_J = 4, 16
LANES = 128
UNROLL = 2
ROW_SECOND, ROW_FIRST, ROW_THIRD, ROW_BITS, PIECE = 0, 16, 20, 24, 25


def split_high_low(array):
    high = array.astype(jnp.bfloat16)
    return high, (array - high.astype(jnp.float32)).astype(jnp.bfloat16)


def dot(left, right):
    return jnp.dot(left, right, preferred_element_type=jnp.float32)


def lane_of(shape):
    return lax.broadcasted_iota(jnp.int32, shape, 1)


def side_by_side(real, imag):
    low = lane_of(real.shape) < 64
    return jnp.where(low, real, pltpu.roll(imag, 64, 1)), jnp.where(low, pltpu.roll(real, 64, 1), imag)


def regrouped(parts, group):
    lane = lane_of(parts[0].shape)
    result = None
    for place, part in enumerate(parts):
        shift = 16 * (place - group) % LANES
        moved = pltpu.roll(part, shift, 1) if shift else part
        result = moved if place == 0 else jnp.where(lane >= 16 * place, moved, result)
    return result


def pack_kernel(order_hbm, bits_hbm, string_hbm, gate_hbm, boundary_hbm, piece_ref, row_ref, order_ref, bits_ref, string_ref, gate_ref, boundary_ref, left_ref, sems):
    small = [
        pltpu.make_async_copy(order_hbm, order_ref, sems.at[0]),
        pltpu.make_async_copy(bits_hbm, bits_ref, sems.at[1]),
        pltpu.make_async_copy(string_hbm, string_ref, sems.at[2]),
        pltpu.make_async_copy(gate_hbm, gate_ref, sems.at[3]),
    ]
    large = [
        pltpu.make_async_copy(boundary_hbm.at[:, pl.ds(8 * step, 8), :], boundary_ref.at[step], sems.at[4 + step])
        for step in range(4)
    ]
    for copy in small + large:
        copy.start()
    for copy in small:
        copy.wait()

    first, second, third = order_ref[0], order_ref[1], order_ref[2]
    member = lax.axis_index("grp")
    columns = pl.ds(pl.multiple_of(member * 256, 256), 256)
    real, imag = gate_ref[first, 0, :, columns], gate_ref[first, 1, :, columns]

    def interleaved(even, odd):
        parts = []
        for k0 in range(8):
            parts += [even[:, 32 * k0 : 32 * k0 + 32], odd[:, 32 * k0 : 32 * k0 + 32]]
        return jnp.concatenate(parts, axis=1)

    left = jnp.concatenate((interleaved(real, -imag), interleaved(imag, real)), axis=0)
    high, low = split_high_low(left)
    left_ref[...] = jnp.concatenate((high, low), axis=0)

    strings = string_ref[...]

    def digit(group):
        total = strings[5 * group : 5 * group + 1]
        for bit in range(1, 5):
            total = total + (strings[5 * group + bit : 5 * group + bit + 1] << bit)
        return total

    g0, g1, g2, g3 = (digit(group) for group in range(4))
    row_ref[0:1, :] = 2 * g0 * PIECE + ROW_FIRST
    row_ref[1:2, :] = (g3 >> 4) * PIECE + ROW_SECOND + (g3 & 15)
    row_ref[2:3, :] = (2 * g1 + (g2 >> 4)) * PIECE + ROW_THIRD + (g2 & 3)
    row_ref[3:4, :] = 32 * (((lane_of((1, 64)) >> 4) - ((g2 & 15) >> 2)) & 3)

    lane = lane_of((1, LANES))
    bits = jnp.zeros((1, LANES), jnp.float32)
    for cut in range(6):
        bits = jnp.where(lane == cut, bits_ref[0, cut].astype(jnp.float32), bits)

    def put(block_i, block_j, at, value):
        start = (block_i * BLOCKS_J + block_j) * PIECE + at
        piece_ref[start : start + value.shape[0], :] = value

    for tile in range(8):
        lanes = slice(LANES * tile, LANES * tile + LANES)
        values = side_by_side(gate_ref[second, 0, :, lanes], gate_ref[second, 1, :, lanes])
        for half in range(2):
            for block_i in range(BLOCKS_I):
                put(block_i, 2 * tile + half, ROW_SECOND, values[half])
    for block_i in range(BLOCKS_I):
        parts = []
        for four in range(4):
            for part in range(2):
                rows = slice(4 * four, 4 * four + 4)
                parts.append(
                    jnp.concatenate(
                        [
                            gate_ref[third, part, rows, 512 * h + LANES * block_i : 512 * h + LANES * block_i + LANES]
                            for h in range(2)
                        ],
                        axis=0,
                    )
                )
        for group in range(8):
            value = regrouped(parts, group)
            put(block_i, group, ROW_THIRD, value[:4])
            put(block_i, 8 + group, ROW_THIRD, value[4:])
    for block_i in range(BLOCKS_I):
        for block_j in range(BLOCKS_J):
            put(block_i, block_j, ROW_BITS, bits)

    left = left_ref[...]
    for step in range(4):
        large[step].wait()
        flat = boundary_ref.at[step].reshape(4096, 32)
        for half in range(2):
            right = jnp.concatenate(
                [flat[pl.ds(4 * half + quarter, 512, stride=8), :] for quarter in range(4)], axis=1
            )
            high, low = split_high_low(right)
            by_high = dot(left, high)
            value = by_high[:32] + by_high[32:] + dot(left[:32], low)
            values = side_by_side(value[:16], value[16:])
            for side in range(2):
                for block_i in range(BLOCKS_I):
                    rows = values[side][4 * block_i : 4 * block_i + 4]
                    put(block_i, 4 * step + 2 * half + side, ROW_FIRST, rows)


def inner_kernel(row_ref, cut_ref, string_ref, got_ref, out_ref, third_ref, pairs_ref, allowed_ref, fixed_ref, sum_ref, whole_ref):
    place = 0
    for axis, size in zip(CUTS, AXES, strict=True):
        place = place * size + lax.axis_index(axis)
    block_i, block_j = place // BLOCKS_J, place % BLOCKS_J

    bits = got_ref[pl.ds(ROW_BITS, 64, stride=PIECE), :]
    bits_t = jnp.concatenate((bits, jnp.zeros_like(bits)), axis=0).T[:8, :64]

    row = lax.broadcasted_iota(jnp.int32, (256, 64), 0)
    i1 = 16 * (row >> 7) + 4 * block_i + ((row >> 5) & 3)
    i2 = row & 31
    j = lane_of((64, LANES)) & 63
    j2 = 2 * block_j + (j >> 5)
    j3 = j & 31
    pairs = jnp.ones((256, 64), jnp.float32)
    allowed = jnp.ones((64, LANES), jnp.float32)
    fixed = jnp.ones((64, 64), jnp.float32)
    for cut in range(6):
        layer, group, bit = cut_ref[0, cut], cut_ref[1, cut], cut_ref[2, cut]
        by_row, by_column = bits_t[cut : cut + 1, :], bits[:, cut : cut + 1]
        on_i1 = (group == 1) & (layer < 2)
        on_i2 = (group == 2) & (layer == 1)
        on_j2 = (group == 2) & (layer == 0)
        on_j3 = (group == 3) & (layer == 0)
        index = jnp.where(on_i1, i1, i2)
        agrees = ((index >> bit) & 1).astype(jnp.float32) == by_row
        pairs = jnp.where(agrees | jnp.logical_not(on_i1 | on_i2), pairs, 0.0)
        index = jnp.where(on_j2, j2, j3)
        agrees = ((index >> bit) & 1).astype(jnp.float32) == by_column
        allowed = jnp.where(agrees | jnp.logical_not(on_j2 | on_j3), allowed, 0.0)
        chosen = string_ref[pl.ds(5 * group + bit, 1), :].astype(jnp.float32)
        inner = on_i1 | on_i2 | on_j2 | on_j3
        fixed = jnp.where((chosen == by_column) | inner, fixed, 0.0)
    pairs_ref[...] = pairs.astype(jnp.bfloat16)
    allowed_ref[...] = allowed.astype(jnp.bfloat16)
    fixed = jnp.concatenate((fixed, jnp.zeros_like(fixed)), axis=1)
    fixed_ref[...] = jnp.concatenate((fixed, jnp.zeros_like(fixed)), axis=0).T[:64, :64]

    lane = lane_of((1, LANES))
    for row in range(16):
        value = None
        for four in range(4):
            b = 16 * four + row
            moved = pltpu.roll(got_ref[pl.ds(row_ref[2, b], 1), :], row_ref[3, b], 1)
            value = moved if four == 0 else jnp.where(lane >= 32 * four, moved, value)
        third_ref[row : row + 1, :] = value

    low = lane_of((8, LANES)) < 64

    def one(b):
        row_b = fixed_ref[pl.ds(b, 1), :].astype(jnp.bfloat16)
        start, source = row_ref[1, b], row_ref[0, b]
        first = jnp.concatenate((got_ref[pl.ds(source, 4), :], got_ref[pl.ds(source + PIECE, 4), :]), axis=0)
        turned = pltpu.roll(first, 64, 1)
        by_same = jnp.where(low, first, turned)
        by_other = jnp.where(low, -turned, first)
        second = got_ref[pl.ds(start, 32, stride=2 * PIECE), :]
        other = pltpu.roll(second, 64, 1)
        for h in range(2):
            rows = slice(128 * h, 128 * h + 128)
            count = dot(pairs_ref[rows, :] * row_b, allowed_ref[...])
            terms = []
            for e in range(4):
                q = 4 * h + e
                term = by_same[q : q + 1] * second + by_other[q : q + 1] * other
                terms.append(term * count[32 * e : 32 * e + 32])
            columns = jnp.concatenate(terms, axis=0).T
            for part in range(2):
                total = jnp.sum(columns[64 * part : 64 * part + 64].reshape(8, 8, LANES), axis=0)
                sum_ref[2 * part + h, pl.ds(pl.multiple_of(8 * b, 8), 8), :] = total

    def several(base, carry):
        for inside in range(UNROLL):
            one(base * UNROLL + inside)
        return carry

    lax.fori_loop(0, 64 // UNROLL, several, 0)
    for part in range(2):
        for h in range(2):
            total = jnp.zeros((64, LANES), jnp.float32)
            for sublane in range(8):
                total += sum_ref[2 * part + h, pl.ds(sublane, 64, stride=8), :]
            whole_ref[2 * part + h] = total
    for h in range(2):
        parts = [whole_ref[2 * part + h, 16 * four : 16 * four + 16] for four in range(4) for part in range(2)]
        for group in range(8):
            out_ref[8 * h + group] = regrouped(parts, group)


def outer_kernel(third_ref, got_ref, out_ref):
    total = jnp.sum(got_ref[...], axis=0)
    second_half = (lane_of((16, LANES)) & 16) != 0
    other = jnp.where(second_half, pltpu.roll(total, 16, 1), pltpu.roll(total, LANES - 16, 1))
    third = third_ref[...]
    real = third * jnp.where(second_half, -total, total)
    imag = third * other
    columns = jnp.concatenate((real, imag, jnp.zeros((96, LANES), jnp.float32)), axis=0).T
    sums = [jnp.sum(columns[32 * four : 32 * four + 32, :32], axis=0, keepdims=True) for four in range(4)]
    result = jnp.concatenate([x[:, :16] for x in sums] + [x[:, 16:] for x in sums], axis=1)
    for to in range(16):
        out_ref[to] = result


def all_reduced(copies, axes, rows):
    got = lax.all_to_all(copies, axes, 0, 0, tiled=True)
    total = jnp.sum(got, axis=0, keepdims=True)
    return jnp.broadcast_to(total, (rows,) + total.shape[1:])


def on_device(boundary, gate_stack, layer_order, cut_index, slice_bits, bitstrings):
    smem = pl.BlockSpec(memory_space=pltpu.SMEM)
    vmem = pl.BlockSpec(memory_space=pltpu.VMEM)
    hbm = pl.BlockSpec(memory_space=pltpu.HBM)
    in_hbm = partial(pltpu.with_memory_space_constraint, memory_space=pltpu.HBM)
    strings = bitstrings.T
    pieces, rows = pl.pallas_call(
        pack_kernel,
        out_shape=(
            jax.ShapeDtypeStruct((64 * PIECE, LANES), jnp.float32),
            jax.ShapeDtypeStruct((8, 64), jnp.int32),
        ),
        in_specs=[hbm] * 5,
        out_specs=(vmem, vmem),
        scratch_shapes=[
            pltpu.SMEM((3,), jnp.int32),
            pltpu.SMEM((1, 6), jnp.int32),
            pltpu.VMEM((20, 64), jnp.int32),
            pltpu.VMEM((3, 2, 16, 1024), jnp.float32),
            pltpu.VMEM((4, 512, 8, 32), jnp.float32),
            pltpu.VMEM((64, 512), jnp.bfloat16),
            pltpu.SemaphoreType.DMA((8,)),
        ],
        compiler_params=pltpu.CompilerParams(vmem_limit_bytes=24 << 20),
        name="pack",
    )(*(in_hbm(x) for x in (layer_order, slice_bits, strings, gate_stack, boundary.reshape(512, 32, 32))))
    pieces = pieces.reshape(64, 1, PIECE * LANES)
    got = lax.all_to_all(pieces, CUTS, 0, 0, tiled=True).reshape(64 * PIECE, LANES)
    inner, third = pl.pallas_call(
        inner_kernel,
        out_shape=(
            jax.ShapeDtypeStruct((16, 16, LANES), jnp.float32),
            jax.ShapeDtypeStruct((16, LANES), jnp.float32),
        ),
        in_specs=[smem, smem, vmem, vmem],
        out_specs=(vmem, vmem),
        scratch_shapes=[
            pltpu.VMEM((256, 64), jnp.bfloat16),
            pltpu.VMEM((64, LANES), jnp.bfloat16),
            pltpu.VMEM((64, 64), jnp.float32),
            pltpu.VMEM((4, 512, LANES), jnp.float32),
            pltpu.VMEM((4, 64, LANES), jnp.float32),
        ],
        compiler_params=pltpu.CompilerParams(vmem_limit_bytes=16 << 20),
        name="inner",
    )(rows, in_hbm(cut_index.T), in_hbm(strings), got)
    inner = lax.all_to_all(inner, WAVE, 0, 0, tiled=True)
    partial_sums = pl.pallas_call(
        outer_kernel,
        out_shape=jax.ShapeDtypeStruct((16, 1, LANES), jnp.float32),
        in_specs=[vmem, vmem],
        out_specs=vmem,
        compiler_params=pltpu.CompilerParams(vmem_limit_bytes=8 << 20),
        name="outer",
    )(third, inner)
    total = all_reduced(partial_sums, COLUMN, 16)
    total = all_reduced(total, PLANE, 1)
    return total.reshape(2, 64).T


def solution(mesh):
    finer = Mesh(
        mesh.devices.reshape(AXES + (mesh.shape["grp"],)),
        CUTS + ("grp",),
    )
    return jax.shard_map(
        on_device,
        mesh=finer,
        in_specs=(
            P("grp", None, None, None, None),
            P(None, None, CUTS, None),
            P(),
            P(),
            P(CUTS, None),
            P(),
        ),
        out_specs=P(),
        check_vma=False,
    )
```

time: 83 us -> 75.7 us (0.912)
  blocking collectives: 71.4 us -> 59.3 us
  Pallas kernels: 10.7 us -> 15.4 us
    all_to_all x1, blocking collectives: 45.8 us -> 26 us  [on_device(): lax.all_to_all(pieces, CUTS, 0, 0, tiled=True).reshape(64 * PIECE, LANES)]
    all_to_all x0 -> x1, blocking collectives: none -> 8.92 us  [on_device(): inner = lax.all_to_all(inner, WAVE, 0, 0, tiled=True)]
    pallas_call x2 -> x3, Pallas kernels: 10.7 us -> 15.4 us  [the longest x1 10.3 us: on_device(): pl.pallas_call(inner_kernel, out_shape=(jax.ShapeDtypeStruct((16, 16, LAN...]
    all_to_all x2, blocking collectives: 25.6 us -> 24.4 us  [all_reduced(): got = lax.all_to_all(copies, axes, 0, 0, tiled=True)]
where the time goes in v3:
time: 75.7 us; the launch traced here: 75.4 us
  blocking collectives  59.3 us (78%)
  Pallas kernels  15.4 us (20%)
    all_to_all x1, blocking collectives, on_device(): lax.all_to_all(pieces, CUTS, 0, 0, tiled=True).reshape(64 * PIECE, LANES)  26 us
    all_to_all x2, blocking collectives, all_reduced(): got = lax.all_to_all(copies, axes, 0, 0, tiled=True)  24.4 us
    pallas_call x1, Pallas kernels, on_device(): pl.pallas_call(inner_kernel, out_shape=(jax.ShapeDtypeStruct((16, 16, LAN...  10.3 us
    all_to_all x1, blocking collectives, on_device(): inner = lax.all_to_all(inner, WAVE, 0, 0, tiled=True)  8.92 us
    pallas_call x1, Pallas kernels, on_device(): pl.pallas_call(pack_kernel, out_shape=(jax.ShapeDtypeStruct((64 * PIECE,...  4.82 us

profile of v3, /device:TPU:1, one launch (start us, length us, event | category | flops | bytes accessed | tf_op | source)
XLA Modules:
  0.0 75.4 jit_solution(8163976209039719609)
XLA Ops:
  0.0 4.8 %pack.1 = (f32[1600,128]{1,0:T(8,128)S(1)}, s32[8,64]{1,0:T(8,128)S(1)}) custom-call(s32[3]{0:T(128)} %order_hbm.1, s32[1,6]{1,0:T(1,128)} %bits_hbm.1, s32[20,64]{1,0:T(8,128)} %bitcast.10, f32[3,2,16,1024]{3,2,1,0:T(8,128)} %gate_hbm.1, f32[512,32,32]{2,1,0:T(8,128)} %bitcast.9), custom_call_target="tpu_custom_call" | custom-call | tf_op jit(solution)/shard_map/pack/pallas_call | solution.py:267
  4.8 26.0 %all_to_all.20 = f32[64,1,3200]{2,1,0:T(1,128)S(1)} all-to-all(f32[64,1,3200]{2,1,0:T(1,128)S(1)} %bitcast.8), channel_id=1, replica_groups=mesh['cuts_0'=4,'cuts_1'=4,'cuts_2'=2,'cuts_3'=2,'grp'=4] {'cuts_0','cut..., dimensions={0} | all-to-all | bytes 1638400 | tf_op jit(solution)/shard_map/all_to_all | solution.py:288
  30.8 10.3 %inner.1 = (f32[16,16,128]{2,1,0:T(8,128)S(1)}, f32[16,128]{1,0:T(8,128)S(1)}) custom-call(s32[8,64]{1,0:T(8,128)S(1)} %get-tuple-element.9.row_ref, s32[3,6]{1,0:T(4,128)} %bitcast.13, s32[20,64]{1,0:T(8,128)} %bitcast.11, f32[1600,128]{1,0:T(8,128)S(1)} %bitcast.7), custom_call_target="tpu_custom_call" | custom-call | tf_op jit(solution)/shard_map/inner/pallas_call | solution.py:289
  41.2 8.9 %all_to_all.21.got_ref = f32[16,16,128]{2,1,0:T(8,128)S(1)} all-to-all(f32[16,16,128]{2,1,0:T(8,128)S(1)} %get-tuple-element.12), channel_id=1, replica_groups=mesh['cuts_0'=4,'cuts_1'=4,'cuts_2'=2,'cuts_3'=2,'grp'=4] {'cuts_1','cut..., dimensions={0} | all-to-all | bytes 262144 | tf_op jit(solution)/shard_map/all_to_all | solution.py:307
  50.1 0.2 outer.1
  50.3 15.2 %all_to_all.22 = f32[16,1,128]{2,1,0:T(1,128)S(1)} all-to-all(f32[16,1,128]{2,1,0:T(1,128)S(1)} %outer.1), channel_id=1, replica_groups=mesh['cuts_0'=4,'cuts_1'=4,'cuts_2'=2,'cuts_3'=2,'grp'=4] {'cuts_2','cut..., dimensions={0} | all-to-all | bytes 16384 | tf_op jit(solution)/shard_map/all_to_all | solution.py:256
  65.5 9.2 %all_to_all.23 = f32[16,1,128]{2,1,0:T(1,128)S(1)} all-to-all(f32[16,1,128]{2,1,0:T(1,128)S(1)} %broadcast_in_dim.2), channel_id=1, replica_groups=mesh['cuts_0'=4,'cuts_1'=4,'cuts_2'=2,'cuts_3'=2,'grp'=4] {'cuts_0','cut..., dimensions={0} | all-to-all | bytes 16384 | tf_op jit(solution)/shard_map/all_to_all | solution.py:256
  74.8 0.6 reshape_broadcast_in_dim.3
  (3 shorter events, 0.1 us)

commit v4 on v3

--- a/solution.py
+++ b/solution.py
@@ -16,7 +16,7 @@
 
 BLOCKS_I, BLOCKS_J = 4, 16
 LANES = 128
-UNROLL = 2
+UNROLL = 8
 ROW_SECOND, ROW_FIRST, ROW_THIRD, ROW_BITS, PIECE = 0, 16, 20, 24, 25
 
 
@@ -148,7 +148,7 @@
                     put(block_i, 4 * step + 2 * half + side, ROW_FIRST, rows)
 
 
-def inner_kernel(row_ref, cut_ref, string_ref, got_ref, out_ref, third_ref, pairs_ref, allowed_ref, fixed_ref, sum_ref, whole_ref):
+def inner_kernel(row_ref, cut_ref, string_ref, got_ref, out_ref, third_ref, pairs_ref, allowed_ref, fixed_ref, sum_ref, whole_ref, turned_ref, even_ref, odd_ref):
     place = 0
     for axis, size in zip(CUTS, AXES, strict=True):
         place = place * size + lax.axis_index(axis)
@@ -197,35 +197,48 @@
         third_ref[row : row + 1, :] = value
 
     low = lane_of((8, LANES)) < 64
-
-    def one(b):
+    for start in range(0, 64 * PIECE, 200):
+        turned_ref[start : start + 200, :] = pltpu.roll(got_ref[start : start + 200, :], 64, 1)
+
+    def counted(count_ref, b, inside):
         row_b = fixed_ref[pl.ds(b, 1), :].astype(jnp.bfloat16)
+        count_ref[256 * inside : 256 * inside + 256, :] = dot(pairs_ref[...] * row_b, allowed_ref[...])
+
+    def summed(count_ref, b, inside):
         start, source = row_ref[1, b], row_ref[0, b]
-        first = jnp.concatenate((got_ref[pl.ds(source, 4), :], got_ref[pl.ds(source + PIECE, 4), :]), axis=0)
-        turned = pltpu.roll(first, 64, 1)
+
+        def first_rows(ref):
+            return jnp.concatenate((ref[pl.ds(source, 4), :], ref[pl.ds(source + PIECE, 4), :]), axis=0)
+
+        first, turned = first_rows(got_ref), first_rows(turned_ref)
         by_same = jnp.where(low, first, turned)
         by_other = jnp.where(low, -turned, first)
         second = got_ref[pl.ds(start, 32, stride=2 * PIECE), :]
-        other = pltpu.roll(second, 64, 1)
+        other = turned_ref[pl.ds(start, 32, stride=2 * PIECE), :]
         for h in range(2):
-            rows = slice(128 * h, 128 * h + 128)
-            count = dot(pairs_ref[rows, :] * row_b, allowed_ref[...])
             terms = []
             for e in range(4):
                 q = 4 * h + e
                 term = by_same[q : q + 1] * second + by_other[q : q + 1] * other
-                terms.append(term * count[32 * e : 32 * e + 32])
+                terms.append(term * count_ref[256 * inside + 32 * q : 256 * inside + 32 * q + 32, :])
             columns = jnp.concatenate(terms, axis=0).T
             for part in range(2):
                 total = jnp.sum(columns[64 * part : 64 * part + 64].reshape(8, 8, LANES), axis=0)
                 sum_ref[2 * part + h, pl.ds(pl.multiple_of(8 * b, 8), 8), :] = total
 
     def several(base, carry):
+        b = 2 * UNROLL * base
         for inside in range(UNROLL):
-            one(base * UNROLL + inside)
+            counted(odd_ref, b + UNROLL + inside, inside)
+            summed(even_ref, b + inside, inside)
+        for inside in range(UNROLL):
+            counted(even_ref, (b + 2 * UNROLL + inside) % 64, inside)
+            summed(odd_ref, b + UNROLL + inside, inside)
         return carry
 
-    lax.fori_loop(0, 64 // UNROLL, several, 0)
+    for inside in range(UNROLL):
+        counted(even_ref, inside, inside)
+    lax.fori_loop(0, 32 // UNROLL, several, 0)
     for part in range(2):
         for h in range(2):
             total = jnp.zeros((64, LANES), jnp.float32)
@@ -300,6 +313,9 @@
             pltpu.VMEM((64, 64), jnp.float32),
             pltpu.VMEM((4, 512, LANES), jnp.float32),
             pltpu.VMEM((4, 64, LANES), jnp.float32),
+            pltpu.VMEM((64 * PIECE, LANES), jnp.float32),
+            pltpu.VMEM((256 * UNROLL, LANES), jnp.float32),
+            pltpu.VMEM((256 * UNROLL, LANES), jnp.float32),
         ],
         compiler_params=pltpu.CompilerParams(vmem_limit_bytes=16 << 20),
         name="inner",

time: 75.7 us -> 70 us (0.925)
  Pallas kernels: 15.4 us -> 9.68 us
    pallas_call x1, Pallas kernels: 10.3 us -> 4.61 us  [on_device(): pl.pallas_call(inner_kernel, out_shape=(jax.ShapeDtypeStruct((16, 16, LAN...]
where the time goes in v4:
time: 70 us; the launch traced here: 69.7 us
  blocking collectives  59.3 us (85%)
  Pallas kernels  9.68 us (14%)
    all_to_all x1, blocking collectives, on_device(): lax.all_to_all(pieces, CUTS, 0, 0, tiled=True).reshape(64 * PIECE, LANES)  26 us
    all_to_all x2, blocking collectives, all_reduced(): got = lax.all_to_all(copies, axes, 0, 0, tiled=True)  24.4 us
    all_to_all x1, blocking collectives, on_device(): inner = lax.all_to_all(inner, WAVE, 0, 0, tiled=True)  8.92 us
    pallas_call x1, Pallas kernels, on_device(): pl.pallas_call(pack_kernel, out_shape=(jax.ShapeDtypeStruct((64 * PIECE,...  4.82 us
    pallas_call x1, Pallas kernels, on_device(): pl.pallas_call(inner_kernel, out_shape=(jax.ShapeDtypeStruct((16, 16, LAN...  4.61 us

profile of v4, /device:TPU:1, one launch (start us, length us, event | category | flops | bytes accessed | tf_op | source)
XLA Modules:
  0.0 69.7 jit_solution(17434067678585829516)
XLA Ops:
  0.0 4.8 %pack.1 = (f32[1600,128]{1,0:T(8,128)S(1)}, s32[8,64]{1,0:T(8,128)S(1)}) custom-call(s32[3]{0:T(128)} %order_hbm.1, s32[1,6]{1,0:T(1,128)} %bits_hbm.1, s32[20,64]{1,0:T(8,128)} %bitcast.10, f32[3,2,16,1024]{3,2,1,0:T(8,128)} %gate_hbm.1, f32[512,32,32]{2,1,0:T(8,128)} %bitcast.9), custom_call_target="tpu_custom_call" | custom-call | tf_op jit(solution)/shard_map/pack/pallas_call | solution.py:280
  4.8 26.0 %all_to_all.20 = f32[64,1,3200]{2,1,0:T(1,128)S(1)} all-to-all(f32[64,1,3200]{2,1,0:T(1,128)S(1)} %bitcast.8), channel_id=1, replica_groups=mesh['cuts_0'=4,'cuts_1'=4,'cuts_2'=2,'cuts_3'=2,'grp'=4] {'cuts_0','cut..., dimensions={0} | all-to-all | bytes 1638400 | tf_op jit(solution)/shard_map/all_to_all | solution.py:301
  30.8 4.6 %inner.1 = (f32[16,16,128]{2,1,0:T(8,128)S(1)}, f32[16,128]{1,0:T(8,128)S(1)}) custom-call(s32[8,64]{1,0:T(8,128)S(1)} %get-tuple-element.9.row_ref, s32[3,6]{1,0:T(4,128)} %bitcast.13, s32[20,64]{1,0:T(8,128)} %bitcast.11, f32[1600,128]{1,0:T(8,128)S(1)} %bitcast.7), custom_call_target="tpu_custom_call" | custom-call | tf_op jit(solution)/shard_map/inner/pallas_call | solution.py:302
  35.5 8.9 %all_to_all.21.got_ref = f32[16,16,128]{2,1,0:T(8,128)S(1)} all-to-all(f32[16,16,128]{2,1,0:T(8,128)S(1)} %get-tuple-element.12), channel_id=1, replica_groups=mesh['cuts_0'=4,'cuts_1'=4,'cuts_2'=2,'cuts_3'=2,'grp'=4] {'cuts_1','cut..., dimensions={0} | all-to-all | bytes 262144 | tf_op jit(solution)/shard_map/all_to_all | solution.py:323
  44.4 0.2 outer.1
  44.6 15.2 %all_to_all.22 = f32[16,1,128]{2,1,0:T(1,128)S(1)} all-to-all(f32[16,1,128]{2,1,0:T(1,128)S(1)} %outer.1), channel_id=1, replica_groups=mesh['cuts_0'=4,'cuts_1'=4,'cuts_2'=2,'cuts_3'=2,'grp'=4] {'cuts_2','cut..., dimensions={0} | all-to-all | bytes 16384 | tf_op jit(solution)/shard_map/all_to_all | solution.py:269
  59.8 9.2 %all_to_all.23 = f32[16,1,128]{2,1,0:T(1,128)S(1)} all-to-all(f32[16,1,128]{2,1,0:T(1,128)S(1)} %broadcast_in_dim.2), channel_id=1, replica_groups=mesh['cuts_0'=4,'cuts_1'=4,'cuts_2'=2,'cuts_3'=2,'grp'=4] {'cuts_0','cut..., dimensions={0} | all-to-all | bytes 16384 | tf_op jit(solution)/shard_map/all_to_all | solution.py:269
  69.1 0.6 reshape_broadcast_in_dim.3
  (3 shorter events, 0.1 us)

commit v5 on v4

--- a/solution.py
+++ b/solution.py
@@ -48,12 +48,59 @@
     return result
 
 
-def pack_kernel(order_hbm, bits_hbm, string_hbm, gate_hbm, boundary_hbm, piece_ref, row_ref, order_ref, bits_ref, string_ref, gate_ref, boundary_ref, left_ref, sems):
+def place_in_blocks():
+    place = 0
+    for axis, size in zip(CUTS, AXES, strict=True):
+        place = place * size + lax.axis_index(axis)
+    return place // BLOCKS_J, place % BLOCKS_J
+
+
+def sign_tables(cut_ref, string_ref, pair_ref, j_ref, fixed_ref):
+    block_i, block_j = place_in_blocks()
+    lane, sublane = lane_of((1, LANES)), lax.broadcasted_iota(jnp.int32, (8, 1), 0)
+    zero_row, zero_column = jnp.zeros((1, LANES), jnp.int32), jnp.zeros((8, 1), jnp.int32)
+    pair_on, pair_bit, pair_i1 = zero_row, zero_row, zero_row
+    j_on, j_bit, j_j2 = zero_column, zero_column, zero_column
+    pair_count, j_count, fixed_count = 0, 0, 0
+    strings = jnp.zeros((8, 64), jnp.int32)
+    for cut in range(6):
+        layer, group, bit = cut_ref[0, cut], cut_ref[1, cut], cut_ref[2, cut]
+        on_i1 = jnp.where((group == 1) & (layer < 2), 1, 0)
+        on_i2 = jnp.where((group == 2) & (layer == 1), 1, 0)
+        on_j2 = jnp.where((group == 2) & (layer == 0), 1, 0)
+        on_j3 = jnp.where((group == 3) & (layer == 0), 1, 0)
+        on_fixed = 1 - on_i1 - on_i2 - on_j2 - on_j3
+        pair_on = jnp.where(lane == cut, on_i1 + on_i2, pair_on)
+        pair_bit = jnp.where(lane == cut, bit, pair_bit)
+        pair_i1 = jnp.where(lane == cut, on_i1, pair_i1)
+        j_on = jnp.where(sublane == cut, on_j2 + on_j3, j_on)
+        j_bit = jnp.where(sublane == cut, bit, j_bit)
+        j_j2 = jnp.where(sublane == cut, on_j2, j_j2)
+        pair_count, j_count, fixed_count = pair_count + on_i1 + on_i2, j_count + on_j2 + on_j3, fixed_count + on_fixed
+        sign = on_fixed * (1 - 2 * string_ref[pl.ds(5 * group + bit, 1), :])
+        strings = jnp.where(sublane == cut, sign, strings)
+
+    row = lax.broadcasted_iota(jnp.int32, (256, 1), 0)
+    i1 = 16 * (row >> 7) + 4 * block_i + ((row >> 5) & 3)
+    index = jnp.where(pair_i1 != 0, i1, row & 31)
+    signs = jnp.where(lane == 6, -pair_count, pair_on * (1 - 2 * ((index >> pair_bit) & 1)))
+    pair_ref[...] = signs.astype(jnp.float32).astype(jnp.bfloat16)
+    j = lane & 63
+    index = jnp.where(j_j2 != 0, 2 * block_j + (j >> 5), j & 31)
+    signs = jnp.where(sublane == 6, -j_count, j_on * (1 - 2 * ((index >> j_bit) & 1)))
+    j_ref[...] = signs.astype(jnp.float32)
+    strings = jnp.where(sublane == 6, -fixed_count, strings).astype(jnp.float32)
+    strings = jnp.concatenate((strings, jnp.zeros_like(strings)), axis=1)
+    fixed_ref[...] = jnp.concatenate((strings, jnp.zeros((120, LANES), jnp.float32)), axis=0).T[:64]
+
+
+def pack_kernel(order_hbm, cut_hbm, bits_hbm, string_hbm, gate_hbm, boundary_hbm, piece_ref, row_ref, pair_ref, j_ref, fixed_ref, order_ref, cut_ref, bits_ref, string_ref, gate_ref, boundary_ref, left_ref, high_ref, low_ref, sems):
     small = [
         pltpu.make_async_copy(order_hbm, order_ref, sems.at[0]),
         pltpu.make_async_copy(bits_hbm, bits_ref, sems.at[1]),
         pltpu.make_async_copy(string_hbm, string_ref, sems.at[2]),
         pltpu.make_async_copy(gate_hbm, gate_ref, sems.at[3]),
+        pltpu.make_async_copy(cut_hbm, cut_ref, sems.at[8]),
     ]
     large = [
         pltpu.make_async_copy(boundary_hbm.at[:, pl.ds(8 * step, 8), :], boundary_ref.at[step], sems.at[4 + step])
@@ -130,63 +177,34 @@
         for block_j in range(BLOCKS_J):
             put(block_i, block_j, ROW_BITS, bits)
 
-    left = left_ref[...]
-    for step in range(4):
+    sign_tables(cut_ref, string_ref, pair_ref, j_ref, fixed_ref)
+
+    def split(step):
         large[step].wait()
         flat = boundary_ref.at[step].reshape(4096, 32)
         for half in range(2):
             right = jnp.concatenate(
                 [flat[pl.ds(4 * half + quarter, 512, stride=8), :] for quarter in range(4)], axis=1
             )
-            high, low = split_high_low(right)
-            by_high = dot(left, high)
-            value = by_high[:32] + by_high[32:] + dot(left[:32], low)
+            high_ref[2 * step + half], low_ref[2 * step + half] = split_high_low(right)
+
+    def multiplied(step):
+        for tile in (2 * step, 2 * step + 1):
+            by_high = dot(left_ref[...], high_ref[tile])
+            value = by_high[:32] + by_high[32:] + dot(left_ref[:32], low_ref[tile])
             values = side_by_side(value[:16], value[16:])
             for side in range(2):
                 for block_i in range(BLOCKS_I):
-                    rows = values[side][4 * block_i : 4 * block_i + 4]
-                    put(block_i, 4 * step + 2 * half + side, ROW_FIRST, rows)
-
-
-def inner_kernel(row_ref, cut_ref, string_ref, got_ref, out_ref, third_ref, pairs_ref, allowed_ref, fixed_ref, sum_ref, whole_ref, turned_ref, even_ref, odd_ref):
-    place = 0
-    for axis, size in zip(CUTS, AXES, strict=True):
-        place = place * size + lax.axis_index(axis)
-    block_i, block_j = place // BLOCKS_J, place % BLOCKS_J
-
-    bits = got_ref[pl.ds(ROW_BITS, 64, stride=PIECE), :]
-    bits_t = jnp.concatenate((bits, jnp.zeros_like(bits)), axis=0).T[:8, :64]
-
-    row = lax.broadcasted_iota(jnp.int32, (256, 64), 0)
-    i1 = 16 * (row >> 7) + 4 * block_i + ((row >> 5) & 3)
-    i2 = row & 31
-    j = lane_of((64, LANES)) & 63
-    j2 = 2 * block_j + (j >> 5)
-    j3 = j & 31
-    pairs = jnp.ones((256, 64), jnp.float32)
-    allowed = jnp.ones((64, LANES), jnp.float32)
-    fixed = jnp.ones((64, 64), jnp.float32)
-    for cut in range(6):
-        layer, group, bit = cut_ref[0, cut], cut_ref[1, cut], cut_ref[2, cut]
-        by_row, by_column = bits_t[cut : cut + 1, :], bits[:, cut : cut + 1]
-        on_i1 = (group == 1) & (layer < 2)
-        on_i2 = (group == 2) & (layer == 1)
-        on_j2 = (group == 2) & (layer == 0)
-        on_j3 = (group == 3) & (layer == 0)
-        index = jnp.where(on_i1, i1, i2)
-        agrees = ((index >> bit) & 1).astype(jnp.float32) == by_row
-        pairs = jnp.where(agrees | jnp.logical_not(on_i1 | on_i2), pairs, 0.0)
-        index = jnp.where(on_j2, j2, j3)
-        agrees = ((index >> bit) & 1).astype(jnp.float32) == by_column
-        allowed = jnp.where(agrees | jnp.logical_not(on_j2 | on_j3), allowed, 0.0)
-        chosen = string_ref[pl.ds(5 * group + bit, 1), :].astype(jnp.float32)
-        inner = on_i1 | on_i2 | on_j2 | on_j3
-        fixed = jnp.where((chosen == by_column) | inner, fixed, 0.0)
-    pairs_ref[...] = pairs.astype(jnp.bfloat16)
-    allowed_ref[...] = allowed.astype(jnp.bfloat16)
-    fixed = jnp.concatenate((fixed, jnp.zeros_like(fixed)), axis=1)
-    fixed_ref[...] = jnp.concatenate((fixed, jnp.zeros_like(fixed)), axis=0).T[:64, :64]
-
+                    put(block_i, 2 * tile + side, ROW_FIRST, values[side][4 * block_i : 4 * block_i + 4])
+
+    split(0)
+    for step in range(1, 4):
+        split(step)
+        multiplied(step - 1)
+    multiplied(3)
+
+
+def select_kernel(row_ref, got_ref, out_ref):
     lane = lane_of((1, LANES))
     for row in range(16):
         value = None
@@ -194,7 +212,24 @@
             b = 16 * four + row
             moved = pltpu.roll(got_ref[pl.ds(row_ref[2, b], 1), :], row_ref[3, b], 1)
             value = moved if four == 0 else jnp.where(lane >= 32 * four, moved, value)
-        third_ref[row : row + 1, :] = value
+        for to in range(16):
+            out_ref[to, row : row + 1, :] = value
+
+
+def inner_kernel(row_ref, pair_ref, j_ref, string_ref, got_ref, same_ref, other_ref, pairs_ref, allowed_ref, fixed_ref, sum_ref, whole_ref, turned_ref, even_ref, odd_ref):
+    lane = lane_of((1, LANES))
+    signs = 1.0 - 2.0 * got_ref[pl.ds(ROW_BITS, 64, stride=PIECE), :]
+    signs = jnp.where(lane < 6, signs, jnp.where(lane == 6, 1.0, 0.0)).astype(jnp.bfloat16)
+
+    def one_if_all(differing, kind):
+        return jnp.where(differing == 0.0, 1.0, 0.0).astype(kind)
+
+    def against_slices(table):
+        return lax.dot_general(table, signs, (((1,), (1,)), ((), ())), preferred_element_type=jnp.float32)
+
+    fixed_ref[...] = one_if_all(against_slices(string_ref[...].astype(jnp.bfloat16)), jnp.float32)
+    pairs_ref[...] = one_if_all(against_slices(pair_ref[...]), jnp.bfloat16)
+    allowed_ref[...] = one_if_all(dot(signs[:, :8], j_ref[...].astype(jnp.bfloat16)), jnp.bfloat16)
 
     low = lane_of((8, LANES)) < 64
     for start in range(0, 64 * PIECE, 200):
@@ -248,21 +283,24 @@
     for h in range(2):
         parts = [whole_ref[2 * part + h, 16 * four : 16 * four + 16] for four in range(4) for part in range(2)]
         for group in range(8):
-            out_ref[8 * h + group] = regrouped(parts, group)
-
-
-def outer_kernel(third_ref, got_ref, out_ref):
-    total = jnp.sum(got_ref[...], axis=0)
-    second_half = (lane_of((16, LANES)) & 16) != 0
-    other = jnp.where(second_half, pltpu.roll(total, 16, 1), pltpu.roll(total, LANES - 16, 1))
+            value = regrouped(parts, group)
+            imag = (lane_of(value.shape) & 16) != 0
+            same_ref[8 * h + group] = jnp.where(imag, -value, value)
+            other_ref[8 * h + group] = jnp.where(imag, pltpu.roll(value, 16, 1), pltpu.roll(value, LANES - 16, 1))
+
+
+def outer_kernel(third_ref, same_ref, other_ref, out_ref):
     third = third_ref[...]
-    real = third * jnp.where(second_half, -total, total)
-    imag = third * other
+    real = jnp.sum(third * same_ref[...], axis=0)
+    imag = jnp.sum(third * other_ref[...], axis=0)
     columns = jnp.concatenate((real, imag, jnp.zeros((96, LANES), jnp.float32)), axis=0).T
     sums = [jnp.sum(columns[32 * four : 32 * four + 32, :32], axis=0, keepdims=True) for four in range(4)]
-    result = jnp.concatenate([x[:, :16] for x in sums] + [x[:, 16:] for x in sums], axis=1)
+    unused = [jnp.zeros((1, 64), jnp.float32)]
+    real = jnp.concatenate([x[:, :16] for x in sums] + unused, axis=1)
+    imag = jnp.concatenate([x[:, 16:] for x in sums] + unused, axis=1)
     for to in range(16):
-        out_ref[to] = result
+        out_ref[to, 0:1, :] = real
+        out_ref[to, 1:2, :] = imag
 
 
 def all_reduced(copies, axes, rows):
@@ -277,35 +315,47 @@
     hbm = pl.BlockSpec(memory_space=pltpu.HBM)
     in_hbm = partial(pltpu.with_memory_space_constraint, memory_space=pltpu.HBM)
     strings = bitstrings.T
-    pieces, rows = pl.pallas_call(
+    pieces, rows, *tables = pl.pallas_call(
         pack_kernel,
         out_shape=(
             jax.ShapeDtypeStruct((64 * PIECE, LANES), jnp.float32),
             jax.ShapeDtypeStruct((8, 64), jnp.int32),
+            jax.ShapeDtypeStruct((256, LANES), jnp.bfloat16),
+            jax.ShapeDtypeStruct((8, LANES), jnp.float32),
+            jax.ShapeDtypeStruct((64, LANES), jnp.float32),
         ),
-        in_specs=[hbm] * 5,
-        out_specs=(vmem, vmem),
+        in_specs=[hbm] * 6,
+        out_specs=(vmem,) * 5,
         scratch_shapes=[
             pltpu.SMEM((3,), jnp.int32),
+            pltpu.SMEM((3, 6), jnp.int32),
             pltpu.SMEM((1, 6), jnp.int32),
             pltpu.VMEM((20, 64), jnp.int32),
             pltpu.VMEM((3, 2, 16, 1024), jnp.float32),
             pltpu.VMEM((4, 512, 8, 32), jnp.float32),
             pltpu.VMEM((64, 512), jnp.bfloat16),
-            pltpu.SemaphoreType.DMA((8,)),
+            pltpu.VMEM((8, 512, LANES), jnp.bfloat16),
+            pltpu.VMEM((8, 512, LANES), jnp.bfloat16),
+            pltpu.SemaphoreType.DMA((9,)),
         ],
         compiler_params=pltpu.CompilerParams(vmem_limit_bytes=24 << 20),
         name="pack",
-    )(*(in_hbm(x) for x in (layer_order, slice_bits, strings, gate_stack, boundary.reshape(512, 32, 32))))
+    )(*(in_hbm(x) for x in (layer_order, cut_index.T, slice_bits, strings, gate_stack, boundary.reshape(512, 32, 32))))
     pieces = pieces.reshape(64, 1, PIECE * LANES)
     got = lax.all_to_all(pieces, CUTS, 0, 0, tiled=True).reshape(64 * PIECE, LANES)
-    inner, third = pl.pallas_call(
+    third = pl.pallas_call(
+        select_kernel,
+        out_shape=jax.ShapeDtypeStruct((16, 16, LANES), jnp.float32),
+        in_specs=[smem, vmem],
+        out_specs=vmem,
+        compiler_params=pltpu.CompilerParams(vmem_limit_bytes=8 << 20),
+        name="select",
+    )(rows, got)
+    third = lax.all_to_all(third, WAVE, 0, 0, tiled=True)
+    same, other = pl.pallas_call(
         inner_kernel,
-        out_shape=(
-            jax.ShapeDtypeStruct((16, 16, LANES), jnp.float32),
-            jax.ShapeDtypeStruct((16, LANES), jnp.float32),
-        ),
-        in_specs=[smem, smem, vmem, vmem],
+        out_shape=(jax.ShapeDtypeStruct((16, 16, LANES), jnp.float32),) * 2,
+        in_specs=[smem] + [vmem] * 4,
         out_specs=(vmem, vmem),
         scratch_shapes=[
             pltpu.VMEM((256, 64), jnp.bfloat16),
@@ -318,20 +368,20 @@
             pltpu.VMEM((256 * UNROLL, LANES), jnp.float32),
         ],
         compiler_params=pltpu.CompilerParams(vmem_limit_bytes=16 << 20),
+        cost_estimate=pl.CostEstimate(flops=1 << 30, bytes_accessed=1 << 20, transcendentals=0),
         name="inner",
-    )(rows, in_hbm(cut_index.T), in_hbm(strings), got)
-    inner = lax.all_to_all(inner, WAVE, 0, 0, tiled=True)
+    )(rows, *tables, got)
     partial_sums = pl.pallas_call(
         outer_kernel,
-        out_shape=jax.ShapeDtypeStruct((16, 1, LANES), jnp.float32),
-        in_specs=[vmem, vmem],
+        out_shape=jax.ShapeDtypeStruct((16, 2, LANES), jnp.float32),
+        in_specs=[vmem, vmem, vmem],
         out_specs=vmem,
         compiler_params=pltpu.CompilerParams(vmem_limit_bytes=8 << 20),
         name="outer",
-    )(third, inner)
+    )(third, same, other)
     total = all_reduced(partial_sums, COLUMN, 16)
     total = all_reduced(total, PLANE, 1)
-    return total.reshape(2, 64).T
+    return total[0, :, :64].T
 
 
 def solution(mesh):

time: 70 us -> 67.5 us (0.964)
  blocking collectives: 59.3 us -> 50.6 us
  starting transfers between devices: 0 us -> 3.69 us
  Pallas kernels: 9.68 us -> 11 us
  waiting for transfers between devices: 0 us -> 1.29 us
    all_to_all x1 -> x0, blocking collectives: 8.92 us -> none  [on_device(): inner = lax.all_to_all(inner, WAVE, 0, 0, tiled=True)]
    all_to_all x0 -> x1, starting transfers between devices: none -> 3.69 us  [on_device(): third = lax.all_to_all(third, WAVE, 0, 0, tiled=True)]
    pallas_call x1 -> x2, Pallas kernels: 0.25 us -> 1.61 us  [the longest x1 1.4 us: on_device(): pl.pallas_call(select_kernel, out_shape=jax.ShapeDtypeStruct((16, 16, LAN...]
    all_to_all x0 -> x1, waiting for transfers between devices: none -> 1.29 us  [on_device(): third = lax.all_to_all(third, WAVE, 0, 0, tiled=True)]
  transfers between devices with their start and end apart: 0 -> 1, of which waited for: 0 -> 1; matrix products, arithmetic and copies ran while one was open for 0% -> 0% of each run, Pallas kernels for 0% -> 7%
where the time goes in v5:
time: 67.5 us; the launch traced here: 67.3 us
  blocking collectives  50.6 us (75%)
  Pallas kernels  11 us (16%)
  starting transfers between devices  3.69 us (5%)
  waiting for transfers between devices  1.29 us (2%)
    all_to_all x1, blocking collectives, on_device(): lax.all_to_all(pieces, CUTS, 0, 0, tiled=True).reshape(64 * PIECE, LANES)  26 us
    all_to_all x2, blocking collectives, all_reduced(): got = lax.all_to_all(copies, axes, 0, 0, tiled=True)  24.6 us
    pallas_call x1, Pallas kernels, on_device(): pl.pallas_call(inner_kernel, out_shape=(jax.ShapeDtypeStruct((16, 16, LAN...  4.82 us
    pallas_call x1, Pallas kernels, on_device(): pl.pallas_call(pack_kernel, out_shape=(jax.ShapeDtypeStruct((64 * PIECE,...  4.54 us
    all_to_all x1, starting transfers between devices, on_device(): third = lax.all_to_all(third, WAVE, 0, 0, tiled=True)  3.69 us
    pallas_call x1, Pallas kernels, on_device(): pl.pallas_call(select_kernel, out_shape=jax.ShapeDtypeStruct((16, 16, LAN...  1.4 us
  transfers between devices with their start and end apart: 1, of which 1 were waited for; matrix products, arithmetic and copies ran while one was open for 0% of the time, Pallas kernels for 7%

profile of v5, /device:TPU:1, one launch (start us, length us, event | category | flops | bytes accessed | tf_op | source)
XLA Modules:
  0.0 67.3 jit_solution(1584067870724367922)
XLA Ops:
  0.0 4.5 %pack.1 = (f32[1600,128]{1,0:T(8,128)S(1)}, s32[8,64]{1,0:T(8,128)S(1)}, bf16[256,128]{1,0:T(8,128)(2,1)S(1)}, f32[8,128]{1,0:T(8,128)S(1)}, f32[64,128]{1,0:T(8,128)S(1)}) custom-call(s32[3]{0:T(128)} %order_hbm.1, s32[3,6]{1,0:T(4,128)} %bitcast.16, s32[1,6]{1,0:T(1,128)} %bits_hbm.1, s32[20,64]{1,0:T(8,128)} %bitcast.14, f32[3,2,16,1024]{3,2,1,0:T(8,128)} %gate_hbm.1, ...), custom_call_target="tpu_custom_call" | custom-call | tf_op jit(solution)/shard_map/pack/pallas_call | solution.py:318
  4.5 26.0 %all_to_all.20 = f32[64,1,3200]{2,1,0:T(1,128)S(1)} all-to-all(f32[64,1,3200]{2,1,0:T(1,128)S(1)} %bitcast.12), channel_id=1, replica_groups=mesh['cuts_0'=4,'cuts_1'=4,'cuts_2'=2,'cuts_3'=2,'grp'=4] {'cuts_0','cut..., dimensions={0} | all-to-all | bytes 1638400 | tf_op jit(solution)/shard_map/all_to_all | solution.py:345
  30.6 1.4 %select.1 = f32[16,16,128]{2,1,0:T(8,128)} custom-call(s32[8,64]{1,0:T(8,128)S(1)} %get-tuple-element.12.row_ref, f32[1600,128]{1,0:T(8,128)S(1)} %bitcast.10), custom_call_target="tpu_custom_call" | custom-call | tf_op jit(solution)/shard_map/select/pallas_call | solution.py:346
  32.0 3.7 %all-to-all-start.1 = ((f32[16,16,128]{2,1,0:T(8,128)}), f32[16,16,128]{2,1,0:T(8,128)S(1)}, u32[]{:S(2)}, u32[]{:S(2)}) async-start(f32[16,16,128]{2,1,0:T(8,128)} %select.1), calls=%async_computation.1 | async-start | bytes 262144 | tf_op jit(solution)/shard_map/all_to_all | solution.py:354
  35.7 4.8 %inner.1 = (f32[16,16,128]{2,1,0:T(8,128)S(1)}, f32[16,16,128]{2,1,0:T(8,128)S(1)}) custom-call(s32[8,64]{1,0:T(8,128)S(1)} %get-tuple-element.12.row_ref, bf16[256,128]{1,0:T(8,128)(2,1)S(1)} %get-tuple-element.14.pair_ref, f32[8,128]{1,0:T(8,128)S(1)} %get-tuple-element.15.j_ref, f32[64,128]{1,0:T(8,128)S(1)} %get-tuple-element.16.string_ref, ...), custom_call_target="tpu_custom_call" | custom-call | flops 1073741824 | bytes 1048576 | tf_op jit(solution)/shard_map/inner/pallas_call | solution.py:355
  40.5 1.3 %all-to-all-done.1.third_ref = f32[16,16,128]{2,1,0:T(8,128)S(1)} async-done(((f32[16,16,128]{2,1,0:T(8,128)}), f32[16,16,128]{2,1,0:T(8,128)S(1)}, u32[]{:S(2)}, u32[]{:S(2)}) %all-to-all-start.1) | async-done | bytes 131104 | tf_op jit(solution)/shard_map/all_to_all | solution.py:354
  41.8 0.2 outer.1
  42.0 15.4 %all_to_all.21 = f32[16,2,128]{2,1,0:T(2,128)S(1)} all-to-all(f32[16,2,128]{2,1,0:T(2,128)S(1)} %outer.1), channel_id=1, replica_groups=mesh['cuts_0'=4,'cuts_1'=4,'cuts_2'=2,'cuts_3'=2,'grp'=4] {'cuts_2','cut..., dimensions={0} | all-to-all | bytes 32768 | tf_op jit(solution)/shard_map/all_to_all | solution.py:307
  57.4 9.2 %all_to_all.22 = f32[16,2,128]{2,1,0:T(2,128)S(1)} all-to-all(f32[16,2,128]{2,1,0:T(2,128)S(1)} %broadcast_in_dim.4), channel_id=1, replica_groups=mesh['cuts_0'=4,'cuts_1'=4,'cuts_2'=2,'cuts_3'=2,'grp'=4] {'cuts_0','cut..., dimensions={0} | all-to-all | bytes 32768 | tf_op jit(solution)/shard_map/all_to_all | solution.py:307
  66.7 0.6 slice_bitcast_fusion
  (3 shorter events, 0.1 us)
Async XLA Ops:
  32.0 9.8 %all-to-all-start.1 = ((f32[16,16,128]{2,1,0:T(8,128)}), f32[16,16,128]{2,1,0:T(8,128)S(1)}, u32[]{:S(2)}, u32[]{:S(2)}) async-start(f32[16,16,128]{2,1,0:T(8,128)} %select.1), calls=%async_computation.1 | async-start | bytes 262144 | tf_op jit(solution)/shard_map/all_to_all | solution.py:354

commit v6 on v5

--- a/solution.py
+++ b/solution.py
@@ -8,21 +8,28 @@
 from jax.sharding import Mesh
 from jax.sharding import PartitionSpec as P
 
-AXES = (4, 4, 2, 2)
-CUTS = ("cuts_0", "cuts_1", "cuts_2", "cuts_3")
+AXES = (2, 2, 4, 2, 2)
+CUTS = ("cuts_0", "cuts_1", "cuts_2", "cuts_3", "cuts_4")
 WAVE = ("cuts_1", "cuts_2", "cuts_3")
-PLANE = ("cuts_0", "cuts_1")
-COLUMN = ("cuts_2", "cuts_3", "grp")
+CORES = "cuts_4"
+PLANE = ("cuts_0", "cuts_1", "cuts_2")
+COLUMN = ("cuts_3", "cuts_4", "grp")
 
 BLOCKS_I, BLOCKS_J = 4, 16
 LANES = 128
 UNROLL = 8
-ROW_SECOND, ROW_FIRST, ROW_THIRD, ROW_BITS, PIECE = 0, 16, 20, 24, 25
+ROW_SECOND, ROW_FIRST, ROW_THIRD, ROW_BITS, PIECE = 0, 8, 12, 16, 17
+SPACED, HALF = 9, 64 * 9
+
+
+def split_high_rest(array):
+    high = array.astype(jnp.bfloat16)
+    return high, array - high.astype(jnp.float32)
 
 
 def split_high_low(array):
-    high = array.astype(jnp.bfloat16)
-    return high, (array - high.astype(jnp.float32)).astype(jnp.bfloat16)
+    high, rest = split_high_rest(array)
+    return high, rest.astype(jnp.bfloat16)
 
 
 def dot(left, right):
@@ -49,13 +56,13 @@
 
 
 def place_in_blocks():
-    place = 0
-    for axis, size in zip(CUTS, AXES, strict=True):
-        place = place * size + lax.axis_index(axis)
-    return place // BLOCKS_J, place % BLOCKS_J
-
-
-def sign_tables(cut_ref, string_ref, pair_ref, j_ref, fixed_ref):
+    block_j = 0
+    for axis, size in zip(WAVE, AXES[1:4], strict=True):
+        block_j = block_j * size + lax.axis_index(axis)
+    return 2 * lax.axis_index(CUTS[0]) + lax.axis_index(CORES), block_j
+
+
+def sign_tables(cut_ref, string_ref, third_row, third_move, pair_ref, j_ref, fixed_ref, chosen_ref):
     block_i, block_j = place_in_blocks()
     lane, sublane = lane_of((1, LANES)), lax.broadcasted_iota(jnp.int32, (8, 1), 0)
     zero_row, zero_column = jnp.zeros((1, LANES), jnp.int32), jnp.zeros((8, 1), jnp.int32)
@@ -89,12 +96,18 @@
     index = jnp.where(j_j2 != 0, 2 * block_j + (j >> 5), j & 31)
     signs = jnp.where(sublane == 6, -j_count, j_on * (1 - 2 * ((index >> j_bit) & 1)))
     j_ref[...] = signs.astype(jnp.float32)
-    strings = jnp.where(sublane == 6, -fixed_count, strings).astype(jnp.float32)
-    strings = jnp.concatenate((strings, jnp.zeros_like(strings)), axis=1)
-    fixed_ref[...] = jnp.concatenate((strings, jnp.zeros((120, LANES), jnp.float32)), axis=0).T[:64]
-
-
-def pack_kernel(order_hbm, cut_hbm, bits_hbm, string_hbm, gate_hbm, boundary_hbm, piece_ref, row_ref, pair_ref, j_ref, fixed_ref, order_ref, cut_ref, bits_ref, string_ref, gate_ref, boundary_ref, left_ref, high_ref, low_ref, sems):
+    strings = jnp.where(sublane == 6, -fixed_count, strings)
+    strings = jnp.concatenate((strings, third_row, third_move), axis=0).astype(jnp.float32)
+    strings = jnp.concatenate((strings, jnp.zeros((118, 64), jnp.float32)), axis=0)
+    columns = jnp.concatenate((strings, jnp.zeros_like(strings)), axis=1).T[:64]
+    fixed_ref[...] = columns
+    hit = lane_of((64, 256)).astype(jnp.float32) == columns[:, 8:9]
+    for move in range(4):
+        one = jnp.where(hit & (columns[:, 9:10] == move), 1.0, 0.0)
+        chosen_ref[64 * move : 64 * move + 64, :] = one.astype(jnp.bfloat16)
+
+
+def pack_kernel(order_hbm, cut_hbm, bits_hbm, string_hbm, gate_hbm, boundary_hbm, piece_ref, row_ref, chosen_ref, pair_ref, j_ref, fixed_ref, order_ref, cut_ref, bits_ref, string_ref, gate_ref, boundary_ref, left_ref, high_ref, low_ref, sems):
     small = [
         pltpu.make_async_copy(order_hbm, order_ref, sems.at[0]),
         pltpu.make_async_copy(bits_hbm, bits_ref, sems.at[1]),
@@ -135,10 +148,10 @@
         return total
 
     g0, g1, g2, g3 = (digit(group) for group in range(4))
-    row_ref[0:1, :] = 2 * g0 * PIECE + ROW_FIRST
-    row_ref[1:2, :] = (g3 >> 4) * PIECE + ROW_SECOND + (g3 & 15)
-    row_ref[2:3, :] = (2 * g1 + (g2 >> 4)) * PIECE + ROW_THIRD + (g2 & 3)
-    row_ref[3:4, :] = 32 * (((lane_of((1, 64)) >> 4) - ((g2 & 15) >> 2)) & 3)
+    row_ref[0:1, :] = 8 * g0
+    row_ref[1:2, :] = ((g3 & 15) >> 3) * HALF + (g3 >> 4) * SPACED + (g3 & 7)
+    third_row = (g2 & 3) * 64 + 2 * g1 + (g2 >> 4)
+    third_move = ((lane_of((1, 64)) >> 4) - ((g2 & 15) >> 2)) & 3
 
     lane = lane_of((1, LANES))
     bits = jnp.zeros((1, LANES), jnp.float32)
@@ -146,7 +159,7 @@
         bits = jnp.where(lane == cut, bits_ref[0, cut].astype(jnp.float32), bits)
 
     def put(block_i, block_j, at, value):
-        start = (block_i * BLOCKS_J + block_j) * PIECE + at
+        start = ((block_i // 2 * BLOCKS_J + block_j) * 2 + block_i % 2) * PIECE + at
         piece_ref[start : start + value.shape[0], :] = value
 
     for tile in range(8):
@@ -154,7 +167,8 @@
         values = side_by_side(gate_ref[second, 0, :, lanes], gate_ref[second, 1, :, lanes])
         for half in range(2):
             for block_i in range(BLOCKS_I):
-                put(block_i, 2 * tile + half, ROW_SECOND, values[half])
+                eight = 8 * (block_i % 2)
+                put(block_i, 2 * tile + half, ROW_SECOND, values[half][eight : eight + 8])
     for block_i in range(BLOCKS_I):
         parts = []
         for four in range(4):
@@ -177,7 +191,7 @@
         for block_j in range(BLOCKS_J):
             put(block_i, block_j, ROW_BITS, bits)
 
-    sign_tables(cut_ref, string_ref, pair_ref, j_ref, fixed_ref)
+    sign_tables(cut_ref, string_ref, third_row, third_move, pair_ref, j_ref, fixed_ref, chosen_ref)
 
     def split(step):
         large[step].wait()
@@ -204,19 +218,25 @@
     multiplied(3)
 
 
-def select_kernel(row_ref, got_ref, out_ref):
-    lane = lane_of((1, LANES))
-    for row in range(16):
-        value = None
-        for four in range(4):
-            b = 16 * four + row
-            moved = pltpu.roll(got_ref[pl.ds(row_ref[2, b], 1), :], row_ref[3, b], 1)
-            value = moved if four == 0 else jnp.where(lane >= 32 * four, moved, value)
-        for to in range(16):
-            out_ref[to, row : row + 1, :] = value
-
-
-def inner_kernel(row_ref, pair_ref, j_ref, string_ref, got_ref, same_ref, other_ref, pairs_ref, allowed_ref, fixed_ref, sum_ref, whole_ref, turned_ref, even_ref, odd_ref):
+def select_kernel(chosen_ref, got_ref, out_ref, half_ref):
+    rows = [got_ref[pl.ds(ROW_THIRD + row, 64, stride=PIECE), :] for row in range(4)]
+    high, rest = split_high_rest(jnp.concatenate(rows, axis=0))
+    middle, rest = split_high_rest(rest)
+    chosen = chosen_ref[...]
+    found = dot(chosen, high) + (dot(chosen, middle) + dot(chosen, rest.astype(jnp.bfloat16)))
+    total = found[:64]
+    for move in range(1, 4):
+        total = total + pltpu.roll(found[64 * move : 64 * move + 64], 32 * move, 1)
+    lane, value = lane_of((16, LANES)), total[:16]
+    for four in range(1, 4):
+        value = jnp.where(lane >= 32 * four, total[16 * four : 16 * four + 16], value)
+    for to in range(16):
+        out_ref[to] = value
+    for source in range(64):
+        half_ref[8 * source : 8 * source + 8, :] = got_ref[PIECE * source : PIECE * source + 8, :]
+
+
+def inner_kernel(row_ref, pair_ref, j_ref, string_ref, got_ref, mine_ref, theirs_ref, same_ref, other_ref, pairs_ref, allowed_ref, fixed_ref, sum_ref, whole_ref, second_ref, turned_ref, by_same_ref, by_other_ref, even_ref, odd_ref):
     lane = lane_of((1, LANES))
     signs = 1.0 - 2.0 * got_ref[pl.ds(ROW_BITS, 64, stride=PIECE), :]
     signs = jnp.where(lane < 6, signs, jnp.where(lane == 6, 1.0, 0.0)).astype(jnp.bfloat16)
@@ -231,25 +251,31 @@
     pairs_ref[...] = one_if_all(against_slices(pair_ref[...]), jnp.bfloat16)
     allowed_ref[...] = one_if_all(dot(signs[:, :8], j_ref[...].astype(jnp.bfloat16)), jnp.bfloat16)
 
+    core = lax.axis_index(CORES)
+    for ref, half in ((mine_ref, core), (theirs_ref, 1 - core)):
+        for source in range(64):
+            rows = ref[8 * source : 8 * source + 8, :]
+            at = pl.ds(half * HALF + SPACED * source, 8)
+            second_ref[at, :] = rows
+            turned_ref[at, :] = pltpu.roll(rows, 64, 1)
     low = lane_of((8, LANES)) < 64
-    for start in range(0, 64 * PIECE, 200):
-        turned_ref[start : start + 200, :] = pltpu.roll(got_ref[start : start + 200, :], 64, 1)
+    for g0 in range(32):
+        start = 2 * g0 * PIECE + ROW_FIRST
+        first = jnp.concatenate((got_ref[start : start + 4, :], got_ref[start + PIECE : start + PIECE + 4, :]), axis=0)
+        turned = pltpu.roll(first, 64, 1)
+        by_same_ref[8 * g0 : 8 * g0 + 8, :] = jnp.where(low, first, turned)
+        by_other_ref[8 * g0 : 8 * g0 + 8, :] = jnp.where(low, -turned, first)
 
     def counted(count_ref, b, inside):
         row_b = fixed_ref[pl.ds(b, 1), :].astype(jnp.bfloat16)
         count_ref[256 * inside : 256 * inside + 256, :] = dot(pairs_ref[...] * row_b, allowed_ref[...])
 
     def summed(count_ref, b, inside):
-        start, source = row_ref[1, b], row_ref[0, b]
-
-        def first_rows(ref):
-            return jnp.concatenate((ref[pl.ds(source, 4), :], ref[pl.ds(source + PIECE, 4), :]), axis=0)
-
-        first, turned = first_rows(got_ref), first_rows(turned_ref)
-        by_same = jnp.where(low, first, turned)
-        by_other = jnp.where(low, -turned, first)
-        second = got_ref[pl.ds(start, 32, stride=2 * PIECE), :]
-        other = turned_ref[pl.ds(start, 32, stride=2 * PIECE), :]
+        start = row_ref[1, b]
+        eight = pl.ds(pl.multiple_of(row_ref[0, b], 8), 8)
+        by_same, by_other = by_same_ref[eight, :], by_other_ref[eight, :]
+        second = second_ref[pl.ds(start, 32, stride=2 * SPACED), :]
+        other = turned_ref[pl.ds(start, 32, stride=2 * SPACED), :]
         for h in range(2):
             terms = []
             for e in range(4):
@@ -315,17 +341,18 @@
     hbm = pl.BlockSpec(memory_space=pltpu.HBM)
     in_hbm = partial(pltpu.with_memory_space_constraint, memory_space=pltpu.HBM)
     strings = bitstrings.T
-    pieces, rows, *tables = pl.pallas_call(
+    pieces, rows, chosen, *tables = pl.pallas_call(
         pack_kernel,
         out_shape=(
             jax.ShapeDtypeStruct((64 * PIECE, LANES), jnp.float32),
             jax.ShapeDtypeStruct((8, 64), jnp.int32),
+            jax.ShapeDtypeStruct((256, 256), jnp.bfloat16),
             jax.ShapeDtypeStruct((256, LANES), jnp.bfloat16),
             jax.ShapeDtypeStruct((8, LANES), jnp.float32),
             jax.ShapeDtypeStruct((64, LANES), jnp.float32),
         ),
         in_specs=[hbm] * 6,
-        out_specs=(vmem,) * 5,
+        out_specs=(vmem,) * 6,
         scratch_shapes=[
             pltpu.SMEM((3,), jnp.int32),
             pltpu.SMEM((3, 6), jnp.int32),
@@ -343,19 +370,23 @@
     )(*(in_hbm(x) for x in (layer_order, cut_index.T, slice_bits, strings, gate_stack, boundary.reshape(512, 32, 32))))
     pieces = pieces.reshape(64, 1, PIECE * LANES)
     got = lax.all_to_all(pieces, CUTS, 0, 0, tiled=True).reshape(64 * PIECE, LANES)
-    third = pl.pallas_call(
+    third, mine = pl.pallas_call(
         select_kernel,
-        out_shape=jax.ShapeDtypeStruct((16, 16, LANES), jnp.float32),
-        in_specs=[smem, vmem],
-        out_specs=vmem,
+        out_shape=(
+            jax.ShapeDtypeStruct((16, 16, LANES), jnp.float32),
+            jax.ShapeDtypeStruct((512, LANES), jnp.float32),
+        ),
+        in_specs=[vmem, vmem],
+        out_specs=(vmem, vmem),
         compiler_params=pltpu.CompilerParams(vmem_limit_bytes=8 << 20),
         name="select",
-    )(rows, got)
+    )(chosen, got)
+    theirs = lax.ppermute(mine, CORES, [(0, 1), (1, 0)])
     third = lax.all_to_all(third, WAVE, 0, 0, tiled=True)
     same, other = pl.pallas_call(
         inner_kernel,
         out_shape=(jax.ShapeDtypeStruct((16, 16, LANES), jnp.float32),) * 2,
-        in_specs=[smem] + [vmem] * 4,
+        in_specs=[smem] + [vmem] * 6,
         out_specs=(vmem, vmem),
         scratch_shapes=[
             pltpu.VMEM((256, 64), jnp.bfloat16),
@@ -363,14 +394,17 @@
             pltpu.VMEM((64, 64), jnp.float32),
             pltpu.VMEM((4, 512, LANES), jnp.float32),
             pltpu.VMEM((4, 64, LANES), jnp.float32),
-            pltpu.VMEM((64 * PIECE, LANES), jnp.float32),
+            pltpu.VMEM((2 * HALF, LANES), jnp.float32),
+            pltpu.VMEM((2 * HALF, LANES), jnp.float32),
+            pltpu.VMEM((256, LANES), jnp.float32),
+            pltpu.VMEM((256, LANES), jnp.float32),
             pltpu.VMEM((256 * UNROLL, LANES), jnp.float32),
             pltpu.VMEM((256 * UNROLL, LANES), jnp.float32),
         ],
         compiler_params=pltpu.CompilerParams(vmem_limit_bytes=16 << 20),
         cost_estimate=pl.CostEstimate(flops=1 << 30, bytes_accessed=1 << 20, transcendentals=0),
         name="inner",
-    )(rows, *tables, got)
+    )(rows, *tables, got, mine, theirs)
     partial_sums = pl.pallas_call(
         outer_kernel,
         out_shape=jax.ShapeDtypeStruct((16, 2, LANES), jnp.float32),

time: 67.5 us -> 65.3 us (0.967)
  blocking collectives: 50.6 us -> 48.7 us
    all_to_all x1, blocking collectives: 26 us -> 23.3 us  [on_device(): lax.all_to_all(pieces, CUTS, 0, 0, tiled=True).reshape(64 * PIECE, LANES)]
    all_to_all x2, blocking collectives: 24.6 us -> 25.4 us  [all_reduced(): got = lax.all_to_all(copies, axes, 0, 0, tiled=True)]
  transfers between devices with their start and end apart: 1 -> 2, of which waited for: 1 -> 1; matrix products, arithmetic and copies ran while one was open for 0% -> 0% of each run, Pallas kernels for 7% -> 8%
where the time goes in v6:
time: 65.3 us; the launch traced here: 64.9 us
  blocking collectives  48.7 us (75%)
  Pallas kernels  10.7 us (16%)
  starting transfers between devices  3.9 us (6%)
  waiting for transfers between devices  1.02 us (2%)
    all_to_all x2, blocking collectives, all_reduced(): got = lax.all_to_all(copies, axes, 0, 0, tiled=True)  25.4 us
    all_to_all x1, blocking collectives, on_device(): lax.all_to_all(pieces, CUTS, 0, 0, tiled=True).reshape(64 * PIECE, LANES)  23.3 us
    pallas_call x1, Pallas kernels, on_device(): pl.pallas_call(inner_kernel, out_shape=(jax.ShapeDtypeStruct((16, 16, LAN...  4.93 us
    pallas_call x1, Pallas kernels, on_device(): pl.pallas_call(pack_kernel, out_shape=(jax.ShapeDtypeStruct((64 * PIECE,...  4.54 us
    all_to_all x1, starting transfers between devices, on_device(): third = lax.all_to_all(third, WAVE, 0, 0, tiled=True)  3.51 us
  transfers between devices with their start and end apart: 2, of which 1 were waited for; matrix products, arithmetic and copies ran while one was open for 0% of the time, Pallas kernels for 8%

profile of v6, /device:TPU:1, one launch (start us, length us, event | category | flops | bytes accessed | tf_op | source)
XLA Modules:
  0.0 64.9 jit_solution(4495464070571232759)
XLA Ops:
  0.0 4.5 %pack.1 = (f32[1088,128]{1,0:T(8,128)S(1)}, s32[8,64]{1,0:T(8,128)S(1)}, bf16[256,256]{1,0:T(8,128)(2,1)S(1)}, bf16[256,128]{1,0:T(8,128)(2,1)S(1)}, f32[8,128]{1,0:T(8,128)S(1)}, /*index=5*/f32[64,128]{1,0:T(8,128)S(1)}) custom-call(s32[3]{0:T(128)} %order_hbm.1, s32[3,6]{1,0:T(4,128)} %bitcast.16, s32[1,6]{1,0:T(1,128)} %bits_hbm.1, s32[20,64]{1,0:T(8,128)} %bitcast.14, ...), custom_call_target="tpu_custom_call" | custom-call | tf_op jit(solution)/shard_map/pack/pallas_call | solution.py:344
  4.6 23.3 %all_to_all.20 = f32[64,1,2176]{2,1,0:T(1,128)S(1)} all-to-all(f32[64,1,2176]{2,1,0:T(1,128)S(1)} %bitcast.12), channel_id=1, replica_groups=mesh['cuts_0'=2,'cuts_1'=2,'cuts_2'=4,'cuts_3'=2,'cuts_4'=2,'grp'=4] {'c..., dimensions={0} | all-to-all | bytes 1114112 | tf_op jit(solution)/shard_map/all_to_all | solution.py:372
  27.8 1.0 %select.1 = (f32[16,16,128]{2,1,0:T(8,128)}, f32[512,128]{1,0:T(8,128)S(1)}) custom-call(bf16[256,256]{1,0:T(8,128)(2,1)S(1)} %get-tuple-element.15.chosen_ref, f32[1088,128]{1,0:T(8,128)S(1)} %bitcast.10), custom_call_target="tpu_custom_call" | custom-call | tf_op jit(solution)/shard_map/select/pallas_call | solution.py:373
  28.8 0.4 collective-permute-start
  29.2 3.5 %all-to-all-start.1 = ((f32[16,16,128]{2,1,0:T(8,128)}), f32[16,16,128]{2,1,0:T(8,128)S(1)}, u32[]{:S(2)}, u32[]{:S(2)}) async-start(f32[16,16,128]{2,1,0:T(8,128)} %get-tuple-element.17), calls=%async_computation.1 | async-start | bytes 262144 | tf_op jit(solution)/shard_map/all_to_all | solution.py:385
  32.7 0.0 collective-permute-done.theirs_ref
  32.7 4.9 %inner.1 = (f32[16,16,128]{2,1,0:T(8,128)S(1)}, f32[16,16,128]{2,1,0:T(8,128)S(1)}) custom-call(s32[8,64]{1,0:T(8,128)S(1)} %get-tuple-element.18.row_ref, bf16[256,128]{1,0:T(8,128)(2,1)S(1)} %get-tuple-element.19.pair_ref, f32[8,128]{1,0:T(8,128)S(1)} %get-tuple-element.20.j_ref, f32[64,128]{1,0:T(8,128)S(1)} %get-tuple-element.21.string_ref, ...), custom_call_target="tpu_custom_call" | custom-call | flops 1073741824 | bytes 1048576 | tf_op jit(solution)/shard_map/inner/pallas_call | solution.py:386
  37.7 1.0 %all-to-all-done.1.third_ref = f32[16,16,128]{2,1,0:T(8,128)S(1)} async-done(((f32[16,16,128]{2,1,0:T(8,128)}), f32[16,16,128]{2,1,0:T(8,128)S(1)}, u32[]{:S(2)}, u32[]{:S(2)}) %all-to-all-start.1) | async-done | bytes 131104 | tf_op jit(solution)/shard_map/all_to_all | solution.py:385
  38.7 0.2 outer.1
  38.9 16.1 %all_to_all.21 = f32[16,2,128]{2,1,0:T(2,128)S(1)} all-to-all(f32[16,2,128]{2,1,0:T(2,128)S(1)} %outer.1), channel_id=1, replica_groups=mesh['cuts_0'=2,'cuts_1'=2,'cuts_2'=4,'cuts_3'=2,'cuts_4'=2,'grp'=4] {'c..., dimensions={0} | all-to-all | bytes 32768 | tf_op jit(solution)/shard_map/all_to_all | solution.py:333
  55.0 9.3 %all_to_all.22 = f32[16,2,128]{2,1,0:T(2,128)S(1)} all-to-all(f32[16,2,128]{2,1,0:T(2,128)S(1)} %broadcast_in_dim.4), channel_id=1, replica_groups=mesh['cuts_0'=2,'cuts_1'=2,'cuts_2'=4,'cuts_3'=2,'cuts_4'=2,'grp'=4] {'c..., dimensions={0} | all-to-all | bytes 32768 | tf_op jit(solution)/shard_map/all_to_all | solution.py:333
  64.4 0.6 slice_bitcast_fusion
  (3 shorter events, 0.1 us)
Async XLA Ops:
  28.8 3.9 %collective-permute-start = (f32[512,128]{1,0:T(8,128)S(1)}, f32[512,128]{1,0:T(8,128)S(1)}, u32[]{:S(2)}, u32[]{:S(2)}) collective-permute-start(f32[512,128]{1,0:T(8,128)S(1)} %get-tuple-element.22.mine_ref), channel_id=1, source_target_pairs={{0,4},{4,0},{1,5},{5,1},{2,6},{6,2},{3,7},{7,3},{8,12},{12,8},{9,1... | collective-permute-start | bytes 786440 | tf_op jit(solution)/shard_map/ppermute | solution.py:384
  29.2 9.5 %all-to-all-start.1 = ((f32[16,16,128]{2,1,0:T(8,128)}), f32[16,16,128]{2,1,0:T(8,128)S(1)}, u32[]{:S(2)}, u32[]{:S(2)}) async-start(f32[16,16,128]{2,1,0:T(8,128)} %get-tuple-element.17), calls=%async_computation.1 | async-start | bytes 262144 | tf_op jit(solution)/shard_map/all_to_all | solution.py:385

commit v7 on v6

--- a/solution.py
+++ b/solution.py
@@ -113,11 +113,11 @@
         pltpu.make_async_copy(bits_hbm, bits_ref, sems.at[1]),
         pltpu.make_async_copy(string_hbm, string_ref, sems.at[2]),
         pltpu.make_async_copy(gate_hbm, gate_ref, sems.at[3]),
-        pltpu.make_async_copy(cut_hbm, cut_ref, sems.at[8]),
+        pltpu.make_async_copy(cut_hbm, cut_ref, sems.at[4]),
     ]
     large = [
-        pltpu.make_async_copy(boundary_hbm.at[:, pl.ds(8 * step, 8), :], boundary_ref.at[step], sems.at[4 + step])
-        for step in range(4)
+        pltpu.make_async_copy(boundary_hbm.at[:, pl.ds(4 * step, 4), :], boundary_ref.at[step], sems.at[5 + step])
+        for step in range(8)
     ]
     for copy in small + large:
         copy.start()
@@ -195,27 +195,26 @@
 
     def split(step):
         large[step].wait()
-        flat = boundary_ref.at[step].reshape(4096, 32)
+        flat = boundary_ref.at[step].reshape(2048, 32)
         for half in range(2):
-            right = jnp.concatenate(
-                [flat[pl.ds(4 * half + quarter, 512, stride=8), :] for quarter in range(4)], axis=1
-            )
+            right = jnp.concatenate([flat[pl.ds(2 * half + one, 512, stride=4), :] for one in range(2)], axis=1)
             high_ref[2 * step + half], low_ref[2 * step + half] = split_high_low(right)
 
     def multiplied(step):
-        for tile in (2 * step, 2 * step + 1):
-            by_high = dot(left_ref[...], high_ref[tile])
-            value = by_high[:32] + by_high[32:] + dot(left_ref[:32], low_ref[tile])
-            values = side_by_side(value[:16], value[16:])
-            for side in range(2):
-                for block_i in range(BLOCKS_I):
-                    put(block_i, 2 * tile + side, ROW_FIRST, values[side][4 * block_i : 4 * block_i + 4])
+        values = []
+        for half in range(2 * step, 2 * step + 2):
+            by_high = dot(left_ref[...], high_ref[half])
+            values.append(by_high[:32] + by_high[32:] + dot(left_ref[:32], low_ref[half]))
+        for half in range(2):
+            value = jnp.concatenate((values[half][:16], values[half][16:]), axis=1)
+            for block_i in range(BLOCKS_I):
+                put(block_i, 2 * step + half, ROW_FIRST, value[4 * block_i : 4 * block_i + 4])
 
     split(0)
-    for step in range(1, 4):
+    for step in range(1, 8):
         split(step)
         multiplied(step - 1)
-    multiplied(3)
+    multiplied(7)
 
 
 def select_kernel(chosen_ref, got_ref, out_ref, half_ref):
@@ -359,11 +358,11 @@
             pltpu.SMEM((1, 6), jnp.int32),
             pltpu.VMEM((20, 64), jnp.int32),
             pltpu.VMEM((3, 2, 16, 1024), jnp.float32),
-            pltpu.VMEM((4, 512, 8, 32), jnp.float32),
+            pltpu.VMEM((8, 512, 4, 32), jnp.float32),
             pltpu.VMEM((64, 512), jnp.bfloat16),
-            pltpu.VMEM((8, 512, LANES), jnp.bfloat16),
-            pltpu.VMEM((8, 512, LANES), jnp.bfloat16),
-            pltpu.SemaphoreType.DMA((9,)),
+            pltpu.VMEM((16, 512, 64), jnp.bfloat16),
+            pltpu.VMEM((16, 512, 64), jnp.bfloat16),
+            pltpu.SemaphoreType.DMA((13,)),
         ],
         compiler_params=pltpu.CompilerParams(vmem_limit_bytes=24 << 20),
         name="pack",

time: 65.3 us -> 65 us (level)
  no operation moved by 1% of the time
where the time goes in v7:
time: 65 us; the launch traced here: 64.7 us
  blocking collectives  48.7 us (75%)
  Pallas kernels  10.4 us (16%)
  starting transfers between devices  3.9 us (6%)
  waiting for transfers between devices  1 us (2%)
    all_to_all x2, blocking collectives, all_reduced(): got = lax.all_to_all(copies, axes, 0, 0, tiled=True)  25.5 us
    all_to_all x1, blocking collectives, on_device(): lax.all_to_all(pieces, CUTS, 0, 0, tiled=True).reshape(64 * PIECE, LANES)  23.3 us
    pallas_call x1, Pallas kernels, on_device(): pl.pallas_call(inner_kernel, out_shape=(jax.ShapeDtypeStruct((16, 16, LAN...  4.95 us
    pallas_call x1, Pallas kernels, on_device(): pl.pallas_call(pack_kernel, out_shape=(jax.ShapeDtypeStruct((64 * PIECE,...  4.28 us
    all_to_all x1, starting transfers between devices, on_device(): third = lax.all_to_all(third, WAVE, 0, 0, tiled=True)  3.51 us
  transfers between devices with their start and end apart: 2, of which 1 were waited for; matrix products, arithmetic and copies ran while one was open for 0% of the time, Pallas kernels for 8%

profile of v7, /device:TPU:1, one launch (start us, length us, event | category | flops | bytes accessed | tf_op | source)
XLA Modules:
  0.0 64.7 jit_solution(15324633211117547445)
XLA Ops:
  0.0 4.3 %pack.1 = (f32[1088,128]{1,0:T(8,128)S(1)}, s32[8,64]{1,0:T(8,128)S(1)}, bf16[256,256]{1,0:T(8,128)(2,1)S(1)}, bf16[256,128]{1,0:T(8,128)(2,1)S(1)}, f32[8,128]{1,0:T(8,128)S(1)}, /*index=5*/f32[64,128]{1,0:T(8,128)S(1)}) custom-call(s32[3]{0:T(128)} %order_hbm.1, s32[3,6]{1,0:T(4,128)} %bitcast.16, s32[1,6]{1,0:T(1,128)} %bits_hbm.1, s32[20,64]{1,0:T(8,128)} %bitcast.14, ...), custom_call_target="tpu_custom_call" | custom-call | tf_op jit(solution)/shard_map/pack/pallas_call | solution.py:343
  4.3 23.3 %all_to_all.20 = f32[64,1,2176]{2,1,0:T(1,128)S(1)} all-to-all(f32[64,1,2176]{2,1,0:T(1,128)S(1)} %bitcast.12), channel_id=1, replica_groups=mesh['cuts_0'=2,'cuts_1'=2,'cuts_2'=4,'cuts_3'=2,'cuts_4'=2,'grp'=4] {'c..., dimensions={0} | all-to-all | bytes 1114112 | tf_op jit(solution)/shard_map/all_to_all | solution.py:371
  27.5 1.0 %select.1 = (f32[16,16,128]{2,1,0:T(8,128)}, f32[512,128]{1,0:T(8,128)S(1)}) custom-call(bf16[256,256]{1,0:T(8,128)(2,1)S(1)} %get-tuple-element.15.chosen_ref, f32[1088,128]{1,0:T(8,128)S(1)} %bitcast.10), custom_call_target="tpu_custom_call" | custom-call | tf_op jit(solution)/shard_map/select/pallas_call | solution.py:372
  28.5 0.4 collective-permute-start
  28.9 3.5 %all-to-all-start.1 = ((f32[16,16,128]{2,1,0:T(8,128)}), f32[16,16,128]{2,1,0:T(8,128)S(1)}, u32[]{:S(2)}, u32[]{:S(2)}) async-start(f32[16,16,128]{2,1,0:T(8,128)} %get-tuple-element.17), calls=%async_computation.1 | async-start | bytes 262144 | tf_op jit(solution)/shard_map/all_to_all | solution.py:384
  32.4 0.0 collective-permute-done.theirs_ref
  32.5 4.9 %inner.1 = (f32[16,16,128]{2,1,0:T(8,128)S(1)}, f32[16,16,128]{2,1,0:T(8,128)S(1)}) custom-call(s32[8,64]{1,0:T(8,128)S(1)} %get-tuple-element.18.row_ref, bf16[256,128]{1,0:T(8,128)(2,1)S(1)} %get-tuple-element.19.pair_ref, f32[8,128]{1,0:T(8,128)S(1)} %get-tuple-element.20.j_ref, f32[64,128]{1,0:T(8,128)S(1)} %get-tuple-element.21.string_ref, ...), custom_call_target="tpu_custom_call" | custom-call | flops 1073741824 | bytes 1048576 | tf_op jit(solution)/shard_map/inner/pallas_call | solution.py:385
  37.4 1.0 %all-to-all-done.1.third_ref = f32[16,16,128]{2,1,0:T(8,128)S(1)} async-done(((f32[16,16,128]{2,1,0:T(8,128)}), f32[16,16,128]{2,1,0:T(8,128)S(1)}, u32[]{:S(2)}, u32[]{:S(2)}) %all-to-all-start.1) | async-done | bytes 131104 | tf_op jit(solution)/shard_map/all_to_all | solution.py:384
  38.4 0.2 outer.1
  38.6 16.1 %all_to_all.21 = f32[16,2,128]{2,1,0:T(2,128)S(1)} all-to-all(f32[16,2,128]{2,1,0:T(2,128)S(1)} %outer.1), channel_id=1, replica_groups=mesh['cuts_0'=2,'cuts_1'=2,'cuts_2'=4,'cuts_3'=2,'cuts_4'=2,'grp'=4] {'c..., dimensions={0} | all-to-all | bytes 32768 | tf_op jit(solution)/shard_map/all_to_all | solution.py:332
  54.7 9.4 %all_to_all.22 = f32[16,2,128]{2,1,0:T(2,128)S(1)} all-to-all(f32[16,2,128]{2,1,0:T(2,128)S(1)} %broadcast_in_dim.4), channel_id=1, replica_groups=mesh['cuts_0'=2,'cuts_1'=2,'cuts_2'=4,'cuts_3'=2,'cuts_4'=2,'grp'=4] {'c..., dimensions={0} | all-to-all | bytes 32768 | tf_op jit(solution)/shard_map/all_to_all | solution.py:332
  64.1 0.6 slice_bitcast_fusion
  (3 shorter events, 0.1 us)
Async XLA Ops:
  28.5 3.9 %collective-permute-start = (f32[512,128]{1,0:T(8,128)S(1)}, f32[512,128]{1,0:T(8,128)S(1)}, u32[]{:S(2)}, u32[]{:S(2)}) collective-permute-start(f32[512,128]{1,0:T(8,128)S(1)} %get-tuple-element.22.mine_ref), channel_id=1, source_target_pairs={{0,4},{4,0},{1,5},{5,1},{2,6},{6,2},{3,7},{7,3},{8,12},{12,8},{9,1... | collective-permute-start | bytes 786440 | tf_op jit(solution)/shard_map/ppermute | solution.py:383
  28.9 9.5 %all-to-all-start.1 = ((f32[16,16,128]{2,1,0:T(8,128)}), f32[16,16,128]{2,1,0:T(8,128)S(1)}, u32[]{:S(2)}, u32[]{:S(2)}) async-start(f32[16,16,128]{2,1,0:T(8,128)} %get-tuple-element.17), calls=%async_computation.1 | async-start | bytes 262144 | tf_op jit(solution)/shard_map/all_to_all | solution.py:384

commit v8 on v7

--- a/solution.py
+++ b/solution.py
@@ -12,8 +12,7 @@
 CUTS = ("cuts_0", "cuts_1", "cuts_2", "cuts_3", "cuts_4")
 WAVE = ("cuts_1", "cuts_2", "cuts_3")
 CORES = "cuts_4"
-PLANE = ("cuts_0", "cuts_1", "cuts_2")
-COLUMN = ("cuts_3", "cuts_4", "grp")
+CHIPS = ("cuts_3", "grp", "cuts_0", "cuts_1", "cuts_2")
 
 BLOCKS_I, BLOCKS_J = 4, 16
 LANES = 128
@@ -235,7 +234,9 @@
         half_ref[8 * source : 8 * source + 8, :] = got_ref[PIECE * source : PIECE * source + 8, :]
 
 
-def inner_kernel(row_ref, pair_ref, j_ref, string_ref, got_ref, mine_ref, theirs_ref, same_ref, other_ref, pairs_ref, allowed_ref, fixed_ref, sum_ref, whole_ref, second_ref, turned_ref, by_same_ref, by_other_ref, even_ref, odd_ref):
+def inner_kernel(row_vmem, pair_ref, j_ref, string_ref, got_ref, mine_ref, theirs_ref, same_ref, other_ref, pairs_ref, allowed_ref, fixed_ref, sum_ref, whole_ref, second_ref, turned_ref, by_same_ref, by_other_ref, even_ref, odd_ref, row_ref, row_sem):
+    to_smem = pltpu.make_async_copy(row_vmem, row_ref, row_sem)
+    to_smem.start()
     lane = lane_of((1, LANES))
     signs = 1.0 - 2.0 * got_ref[pl.ds(ROW_BITS, 64, stride=PIECE), :]
     signs = jnp.where(lane < 6, signs, jnp.where(lane == 6, 1.0, 0.0)).astype(jnp.bfloat16)
@@ -298,6 +299,7 @@
 
     for inside in range(UNROLL):
         counted(even_ref, inside, inside)
+    to_smem.wait()
     lax.fori_loop(0, 32 // UNROLL, several, 0)
     for part in range(2):
         for h in range(2):
@@ -320,18 +322,7 @@
     imag = jnp.sum(third * other_ref[...], axis=0)
     columns = jnp.concatenate((real, imag, jnp.zeros((96, LANES), jnp.float32)), axis=0).T
     sums = [jnp.sum(columns[32 * four : 32 * four + 32, :32], axis=0, keepdims=True) for four in range(4)]
-    unused = [jnp.zeros((1, 64), jnp.float32)]
-    real = jnp.concatenate([x[:, :16] for x in sums] + unused, axis=1)
-    imag = jnp.concatenate([x[:, 16:] for x in sums] + unused, axis=1)
-    for to in range(16):
-        out_ref[to, 0:1, :] = real
-        out_ref[to, 1:2, :] = imag
-
-
-def all_reduced(copies, axes, rows):
-    got = lax.all_to_all(copies, axes, 0, 0, tiled=True)
-    total = jnp.sum(got, axis=0, keepdims=True)
-    return jnp.broadcast_to(total, (rows,) + total.shape[1:])
+    out_ref[...] = jnp.concatenate([x[:, :16] for x in sums] + [x[:, 16:] for x in sums], axis=1)
 
 
 def on_device(boundary, gate_stack, layer_order, cut_index, slice_bits, bitstrings):
@@ -385,7 +376,7 @@
     same, other = pl.pallas_call(
         inner_kernel,
         out_shape=(jax.ShapeDtypeStruct((16, 16, LANES), jnp.float32),) * 2,
-        in_specs=[smem] + [vmem] * 6,
+        in_specs=[vmem] * 7,
         out_specs=(vmem, vmem),
         scratch_shapes=[
             pltpu.VMEM((256, 64), jnp.bfloat16),
@@ -399,6 +390,8 @@
             pltpu.VMEM((256, LANES), jnp.float32),
             pltpu.VMEM((256 * UNROLL, LANES), jnp.float32),
             pltpu.VMEM((256 * UNROLL, LANES), jnp.float32),
+            pltpu.SMEM((8, 64), jnp.int32),
+            pltpu.SemaphoreType.DMA,
         ],
         compiler_params=pltpu.CompilerParams(vmem_limit_bytes=16 << 20),
         cost_estimate=pl.CostEstimate(flops=1 << 30, bytes_accessed=1 << 20, transcendentals=0),
@@ -406,15 +399,16 @@
     )(rows, *tables, got, mine, theirs)
     partial_sums = pl.pallas_call(
         outer_kernel,
-        out_shape=jax.ShapeDtypeStruct((16, 2, LANES), jnp.float32),
+        out_shape=jax.ShapeDtypeStruct((1, LANES), jnp.float32),
         in_specs=[vmem, vmem, vmem],
         out_specs=vmem,
         compiler_params=pltpu.CompilerParams(vmem_limit_bytes=8 << 20),
         name="outer",
     )(third, same, other)
-    total = all_reduced(partial_sums, COLUMN, 16)
-    total = all_reduced(total, PLANE, 1)
-    return total[0, :, :64].T
+    chip_sums = partial_sums + lax.ppermute(partial_sums, CORES, [(0, 1), (1, 0)])
+    copies = jnp.broadcast_to(chip_sums[None], (lax.axis_size(CHIPS), 1, LANES))
+    total = jnp.sum(lax.all_to_all(copies, CHIPS, 0, 0, tiled=True), axis=0)
+    return total.reshape(2, 64).T
 
 
 def solution(mesh):

time: 65 us -> 63.4 us (0.975)
  blocking collectives: 48.7 us -> 44.5 us
  starting transfers between devices: 3.9 us -> 5.35 us
  waiting for transfers between devices: 1 us -> 2.25 us
    all_to_all x2 -> x1, blocking collectives: 25.5 us -> 21.2 us  [on_device(): total = jnp.sum(lax.all_to_all(copies, CHIPS, 0, 0, tiled=True), axis=0)]
    ppermute x0 -> x1, starting transfers between devices: none -> 1.45 us  [on_device(): lax.ppermute(partial_sums, CORES, [(0, 1), (1, 0)])]
    ppermute x0 -> x1, waiting for transfers between devices: none -> 0.82 us  [on_device(): lax.ppermute(partial_sums, CORES, [(0, 1), (1, 0)])]
  transfers between devices with their start and end apart: 2 -> 3, of which waited for: 1 -> 2; matrix products, arithmetic and copies ran while one was open for 0% -> 0% of each run, Pallas kernels for 8% -> 7%
where the time goes in v8:
time: 63.4 us; the launch traced here: 62.8 us
  blocking collectives  44.5 us (70%)
  Pallas kernels  9.96 us (16%)
  starting transfers between devices  5.35 us (8%)
  waiting for transfers between devices  2.25 us (4%)
  local copies, waits for them, and re-layouts  0.68 us (1%)
    all_to_all x1, blocking collectives, on_device(): lax.all_to_all(pieces, CUTS, 0, 0, tiled=True).reshape(64 * PIECE, LANES)  23.3 us
    all_to_all x1, blocking collectives, on_device(): total = jnp.sum(lax.all_to_all(copies, CHIPS, 0, 0, tiled=True), axis=0)  21.2 us
    pallas_call x1, Pallas kernels, on_device(): pl.pallas_call(inner_kernel, out_shape=(jax.ShapeDtypeStruct((16, 16, LAN...  4.51 us
    pallas_call x1, Pallas kernels, on_device(): pl.pallas_call(pack_kernel, out_shape=(jax.ShapeDtypeStruct((64 * PIECE,...  4.28 us
    all_to_all x1, starting transfers between devices, on_device(): third = lax.all_to_all(third, WAVE, 0, 0, tiled=True)  3.51 us
    ppermute x1, starting transfers between devices, on_device(): lax.ppermute(partial_sums, CORES, [(0, 1), (1, 0)])  1.45 us
    all_to_all x1, waiting for transfers between devices, on_device(): third = lax.all_to_all(third, WAVE, 0, 0, tiled=True)  1.43 us
  transfers between devices with their start and end apart: 3, of which 2 were waited for; matrix products, arithmetic and copies ran while one was open for 0% of the time, Pallas kernels for 7%

profile of v8, /device:TPU:1, one launch (start us, length us, event | category | flops | bytes accessed | tf_op | source)
XLA Modules:
  0.0 62.8 jit_solution(1719017949973894769)
XLA Ops:
  0.0 4.3 %pack.1 = (f32[1088,128]{1,0:T(8,128)S(1)}, s32[8,64]{1,0:T(8,128)S(1)}, bf16[256,256]{1,0:T(8,128)(2,1)S(1)}, bf16[256,128]{1,0:T(8,128)(2,1)S(1)}, f32[8,128]{1,0:T(8,128)S(1)}, /*index=5*/f32[64,128]{1,0:T(8,128)S(1)}) custom-call(s32[3]{0:T(128)} %order_hbm.1, s32[3,6]{1,0:T(4,128)} %bitcast.15, s32[1,6]{1,0:T(1,128)} %bits_hbm.1, s32[20,64]{1,0:T(8,128)} %bitcast.14, ...), custom_call_target="tpu_custom_call" | custom-call | tf_op jit(solution)/shard_map/pack/pallas_call | solution.py:334
  4.3 23.3 %all_to_all.15 = f32[64,1,2176]{2,1,0:T(1,128)S(1)} all-to-all(f32[64,1,2176]{2,1,0:T(1,128)S(1)} %bitcast.11), channel_id=1, replica_groups=mesh['cuts_0'=2,'cuts_1'=2,'cuts_2'=4,'cuts_3'=2,'cuts_4'=2,'grp'=4] {'c..., dimensions={0} | all-to-all | bytes 1114112 | tf_op jit(solution)/shard_map/all_to_all | solution.py:362
  27.5 1.0 %select.1 = (f32[16,16,128]{2,1,0:T(8,128)}, f32[512,128]{1,0:T(8,128)S(1)}) custom-call(bf16[256,256]{1,0:T(8,128)(2,1)S(1)} %get-tuple-element.15.chosen_ref, f32[1088,128]{1,0:T(8,128)S(1)} %bitcast.9), custom_call_target="tpu_custom_call" | custom-call | tf_op jit(solution)/shard_map/select/pallas_call | solution.py:363
  28.5 0.4 collective-permute-start
  28.9 3.5 %all-to-all-start.1 = ((f32[16,16,128]{2,1,0:T(8,128)}), f32[16,16,128]{2,1,0:T(8,128)S(1)}, u32[]{:S(2)}, u32[]{:S(2)}) async-start(f32[16,16,128]{2,1,0:T(8,128)} %get-tuple-element.17), calls=%async_computation.1 | async-start | bytes 262144 | tf_op jit(solution)/shard_map/all_to_all | solution.py:375
  32.4 0.0 collective-permute-done.theirs_ref
  32.5 4.5 %inner.1 = (f32[16,16,128]{2,1,0:T(8,128)S(1)}, f32[16,16,128]{2,1,0:T(8,128)S(1)}) custom-call(s32[8,64]{1,0:T(8,128)S(1)} %get-tuple-element.18.row_vmem, bf16[256,128]{1,0:T(8,128)(2,1)S(1)} %get-tuple-element.19.pair_ref, f32[8,128]{1,0:T(8,128)S(1)} %get-tuple-element.20.j_ref, f32[64,128]{1,0:T(8,128)S(1)} %get-tuple-element.21.string_ref, ...), custom_call_target="tpu_custom_call" | custom-call | flops 1073741824 | bytes 1048576 | tf_op jit(solution)/shard_map/inner/pallas_call | solution.py:376
  37.0 1.4 %all-to-all-done.1.third_ref = f32[16,16,128]{2,1,0:T(8,128)S(1)} async-done(((f32[16,16,128]{2,1,0:T(8,128)}), f32[16,16,128]{2,1,0:T(8,128)S(1)}, u32[]{:S(2)}, u32[]{:S(2)}) %all-to-all-start.1) | async-done | bytes 131104 | tf_op jit(solution)/shard_map/all_to_all | solution.py:375
  38.4 0.2 outer.1
  38.6 1.4 %collective-permute-start.1 = (f32[1,128]{1,0:T(1,128)S(1)}, f32[1,128]{1,0:T(1,128)S(1)}, u32[]{:S(2)}, u32[]{:S(2)}) collective-permute-start(f32[1,128]{1,0:T(1,128)S(1)} %outer.1), channel_id=1, source_target_pairs={{0,4},{4,0},{1,5},{5,1},{2,6},{6,2},{3,7},{7,3},{8,12},{12,8},{9,1... | collective-permute-start | bytes 1544 | tf_op jit(solution)/shard_map/ppermute | solution.py:408
  40.0 0.8 %collective-permute-done.1 = f32[1,128]{1,0:T(1,128)S(1)} collective-permute-done((f32[1,128]{1,0:T(1,128)S(1)}, f32[1,128]{1,0:T(1,128)S(1)}, u32[]{:S(2)}, u32[]{:S(2)}) %collective-permute-start.1) | collective-permute-done | bytes 544 | tf_op jit(solution)/shard_map/ppermute | solution.py:408
  40.9 21.2 %all_to_all.16 = f32[128,1,128]{2,1,0:T(1,128)S(1)} all-to-all(f32[128,1,128]{2,1,0:T(1,128)S(1)} %broadcast_in_dim.9), channel_id=1, replica_groups=mesh['cuts_0'=2,'cuts_1'=2,'cuts_2'=4,'cuts_3'=2,'cuts_4'=2,'grp'=4] {'c..., dimensions={0} | all-to-all | bytes 131072 | tf_op jit(solution)/shard_map/all_to_all | solution.py:410
  62.1 0.6 %reshape.20 = f32[2,64]{1,0:T(2,128)} reshape(f32[128]{0:T(128)S(1)} %reduce_sum.9) | data formatting | bytes 1024 | tf_op jit(solution)/shard_map/reshape | solution.py:411
  (3 shorter events, 0.1 us)
Async XLA Ops:
  28.5 3.9 %collective-permute-start = (f32[512,128]{1,0:T(8,128)S(1)}, f32[512,128]{1,0:T(8,128)S(1)}, u32[]{:S(2)}, u32[]{:S(2)}) collective-permute-start(f32[512,128]{1,0:T(8,128)S(1)} %get-tuple-element.22.mine_ref), channel_id=1, source_target_pairs={{0,4},{4,0},{1,5},{5,1},{2,6},{6,2},{3,7},{7,3},{8,12},{12,8},{9,1... | collective-permute-start | bytes 786440 | tf_op jit(solution)/shard_map/ppermute | solution.py:374
  28.9 9.5 %all-to-all-start.1 = ((f32[16,16,128]{2,1,0:T(8,128)}), f32[16,16,128]{2,1,0:T(8,128)S(1)}, u32[]{:S(2)}, u32[]{:S(2)}) async-start(f32[16,16,128]{2,1,0:T(8,128)} %get-tuple-element.17), calls=%async_computation.1 | async-start | bytes 262144 | tf_op jit(solution)/shard_map/all_to_all | solution.py:375
  38.6 2.3 %collective-permute-start.1 = (f32[1,128]{1,0:T(1,128)S(1)}, f32[1,128]{1,0:T(1,128)S(1)}, u32[]{:S(2)}, u32[]{:S(2)}) collective-permute-start(f32[1,128]{1,0:T(1,128)S(1)} %outer.1), channel_id=1, source_target_pairs={{0,4},{4,0},{1,5},{5,1},{2,6},{6,2},{3,7},{7,3},{8,12},{12,8},{9,1... | collective-permute-start | bytes 1544 | tf_op jit(solution)/shard_map/ppermute | solution.py:408

commit v9 on v8

--- a/solution.py
+++ b/solution.py
@@ -8,11 +8,12 @@
 from jax.sharding import Mesh
 from jax.sharding import PartitionSpec as P
 
-AXES = (2, 2, 4, 2, 2)
-CUTS = ("cuts_0", "cuts_1", "cuts_2", "cuts_3", "cuts_4")
-WAVE = ("cuts_1", "cuts_2", "cuts_3")
-CORES = "cuts_4"
-CHIPS = ("cuts_3", "grp", "cuts_0", "cuts_1", "cuts_2")
+AXES = (2, 2, 2, 2, 2, 2, 2, 2)
+CUTS = ("cuts_0", "cuts_1", "cuts_2", "cuts_3", "cuts_4", "cuts_5")
+GRP = ("grp_0", "grp_1")
+WAVE = ("cuts_1", "cuts_2", "cuts_3", "cuts_4")
+CORES = "cuts_5"
+CHIPS = ("cuts_4", "grp_0", "cuts_2", "cuts_0", "grp_1", "cuts_1", "cuts_3")
 
 BLOCKS_I, BLOCKS_J = 4, 16
 LANES = 128
@@ -56,8 +57,8 @@
 
 def place_in_blocks():
     block_j = 0
-    for axis, size in zip(WAVE, AXES[1:4], strict=True):
-        block_j = block_j * size + lax.axis_index(axis)
+    for axis in WAVE:
+        block_j = block_j * 2 + lax.axis_index(axis)
     return 2 * lax.axis_index(CUTS[0]) + lax.axis_index(CORES), block_j
 
 
@@ -124,7 +125,7 @@
         copy.wait()
 
     first, second, third = order_ref[0], order_ref[1], order_ref[2]
-    member = lax.axis_index("grp")
+    member = lax.axis_index(GRP)
     columns = pl.ds(pl.multiple_of(member * 256, 256), 256)
     real, imag = gate_ref[first, 0, :, columns], gate_ref[first, 1, :, columns]
 
@@ -412,15 +413,12 @@
 
 
 def solution(mesh):
-    finer = Mesh(
-        mesh.devices.reshape(AXES + (mesh.shape["grp"],)),
-        CUTS + ("grp",),
-    )
+    finer = Mesh(mesh.devices.reshape(AXES), CUTS + GRP)
     return jax.shard_map(
         on_device,
         mesh=finer,
         in_specs=(
-            P("grp", None, None, None, None),
+            P(GRP, None, None, None, None),
             P(None, None, CUTS, None),
             P(),
             P(),

time: 63.4 us -> 63 us (level)
  no operation moved by 1% of the time
where the time goes in v9:
time: 63 us; the launch traced here: 62.7 us
  blocking collectives  44.4 us (70%)
  Pallas kernels  9.95 us (16%)
  starting transfers between devices  5.35 us (8%)
  waiting for transfers between devices  2.26 us (4%)
  local copies, waits for them, and re-layouts  0.68 us (1%)
    all_to_all x1, blocking collectives, on_device(): lax.all_to_all(pieces, CUTS, 0, 0, tiled=True).reshape(64 * PIECE, LANES)  23.3 us
    all_to_all x1, blocking collectives, on_device(): total = jnp.sum(lax.all_to_all(copies, CHIPS, 0, 0, tiled=True), axis=0)  21.1 us
    pallas_call x1, Pallas kernels, on_device(): pl.pallas_call(inner_kernel, out_shape=(jax.ShapeDtypeStruct((16, 16, LAN...  4.5 us
    pallas_call x1, Pallas kernels, on_device(): pl.pallas_call(pack_kernel, out_shape=(jax.ShapeDtypeStruct((64 * PIECE,...  4.28 us
    all_to_all x1, starting transfers between devices, on_device(): third = lax.all_to_all(third, WAVE, 0, 0, tiled=True)  3.51 us
    ppermute x1, starting transfers between devices, on_device(): lax.ppermute(partial_sums, CORES, [(0, 1), (1, 0)])  1.45 us
    all_to_all x1, waiting for transfers between devices, on_device(): third = lax.all_to_all(third, WAVE, 0, 0, tiled=True)  1.44 us
  transfers between devices with their start and end apart: 3, of which 2 were waited for; matrix products, arithmetic and copies ran while one was open for 0% of the time, Pallas kernels for 7%

profile of v9, /device:TPU:1, one launch (start us, length us, event | category | flops | bytes accessed | tf_op | source)
XLA Modules:
  0.0 62.7 jit_solution(7287992666640333808)
XLA Ops:
  0.0 4.3 %pack.1 = (f32[1088,128]{1,0:T(8,128)S(1)}, s32[8,64]{1,0:T(8,128)S(1)}, bf16[256,256]{1,0:T(8,128)(2,1)S(1)}, bf16[256,128]{1,0:T(8,128)(2,1)S(1)}, f32[8,128]{1,0:T(8,128)S(1)}, /*index=5*/f32[64,128]{1,0:T(8,128)S(1)}) custom-call(s32[3]{0:T(128)} %order_hbm.1, s32[3,6]{1,0:T(4,128)} %bitcast.15, s32[1,6]{1,0:T(1,128)} %bits_hbm.1, s32[20,64]{1,0:T(8,128)} %bitcast.14, ...), custom_call_target="tpu_custom_call" | custom-call | tf_op jit(solution)/shard_map/pack/pallas_call | solution.py:335
  4.3 23.3 %all_to_all.15 = f32[64,1,2176]{2,1,0:T(1,128)S(1)} all-to-all(f32[64,1,2176]{2,1,0:T(1,128)S(1)} %bitcast.11), channel_id=1, replica_groups=mesh['cuts_0'=2,'cuts_1'=2,'cuts_2'=2,'cuts_3'=2,'cuts_4'=2,'cuts_5'=2,'..., dimensions={0} | all-to-all | bytes 1114112 | tf_op jit(solution)/shard_map/all_to_all | solution.py:363
  27.5 1.0 %select.1 = (f32[16,16,128]{2,1,0:T(8,128)}, f32[512,128]{1,0:T(8,128)S(1)}) custom-call(bf16[256,256]{1,0:T(8,128)(2,1)S(1)} %get-tuple-element.15.chosen_ref, f32[1088,128]{1,0:T(8,128)S(1)} %bitcast.9), custom_call_target="tpu_custom_call" | custom-call | tf_op jit(solution)/shard_map/select/pallas_call | solution.py:364
  28.5 0.4 collective-permute-start
  28.9 3.5 %all-to-all-start.1 = ((f32[16,16,128]{2,1,0:T(8,128)}), f32[16,16,128]{2,1,0:T(8,128)S(1)}, u32[]{:S(2)}, u32[]{:S(2)}) async-start(f32[16,16,128]{2,1,0:T(8,128)} %get-tuple-element.17), calls=%async_computation.1 | async-start | bytes 262144 | tf_op jit(solution)/shard_map/all_to_all | solution.py:376
  32.4 0.0 collective-permute-done.theirs_ref
  32.5 4.5 %inner.1 = (f32[16,16,128]{2,1,0:T(8,128)S(1)}, f32[16,16,128]{2,1,0:T(8,128)S(1)}) custom-call(s32[8,64]{1,0:T(8,128)S(1)} %get-tuple-element.18.row_vmem, bf16[256,128]{1,0:T(8,128)(2,1)S(1)} %get-tuple-element.19.pair_ref, f32[8,128]{1,0:T(8,128)S(1)} %get-tuple-element.20.j_ref, f32[64,128]{1,0:T(8,128)S(1)} %get-tuple-element.21.string_ref, ...), custom_call_target="tpu_custom_call" | custom-call | flops 1073741824 | bytes 1048576 | tf_op jit(solution)/shard_map/inner/pallas_call | solution.py:377
  37.0 1.4 %all-to-all-done.1.third_ref = f32[16,16,128]{2,1,0:T(8,128)S(1)} async-done(((f32[16,16,128]{2,1,0:T(8,128)}), f32[16,16,128]{2,1,0:T(8,128)S(1)}, u32[]{:S(2)}, u32[]{:S(2)}) %all-to-all-start.1) | async-done | bytes 131104 | tf_op jit(solution)/shard_map/all_to_all | solution.py:376
  38.4 0.2 outer.1
  38.6 1.4 %collective-permute-start.1 = (f32[1,128]{1,0:T(1,128)S(1)}, f32[1,128]{1,0:T(1,128)S(1)}, u32[]{:S(2)}, u32[]{:S(2)}) collective-permute-start(f32[1,128]{1,0:T(1,128)S(1)} %outer.1), channel_id=1, source_target_pairs={{0,4},{4,0},{1,5},{5,1},{2,6},{6,2},{3,7},{7,3},{8,12},{12,8},{9,1... | collective-permute-start | bytes 1544 | tf_op jit(solution)/shard_map/ppermute | solution.py:409
  40.0 0.8 %collective-permute-done.1 = f32[1,128]{1,0:T(1,128)S(1)} collective-permute-done((f32[1,128]{1,0:T(1,128)S(1)}, f32[1,128]{1,0:T(1,128)S(1)}, u32[]{:S(2)}, u32[]{:S(2)}) %collective-permute-start.1) | collective-permute-done | bytes 544 | tf_op jit(solution)/shard_map/ppermute | solution.py:409
  40.9 21.1 %all_to_all.16 = f32[128,1,128]{2,1,0:T(1,128)S(1)} all-to-all(f32[128,1,128]{2,1,0:T(1,128)S(1)} %broadcast_in_dim.9), channel_id=1, replica_groups=mesh['cuts_0'=2,'cuts_1'=2,'cuts_2'=2,'cuts_3'=2,'cuts_4'=2,'cuts_5'=2,'..., dimensions={0} | all-to-all | bytes 131072 | tf_op jit(solution)/shard_map/all_to_all | solution.py:411
  62.1 0.6 %reshape.20 = f32[2,64]{1,0:T(2,128)} reshape(f32[128]{0:T(128)S(1)} %reduce_sum.9) | data formatting | bytes 1024 | tf_op jit(solution)/shard_map/reshape | solution.py:412
  (3 shorter events, 0.1 us)
Async XLA Ops:
  28.5 3.9 %collective-permute-start = (f32[512,128]{1,0:T(8,128)S(1)}, f32[512,128]{1,0:T(8,128)S(1)}, u32[]{:S(2)}, u32[]{:S(2)}) collective-permute-start(f32[512,128]{1,0:T(8,128)S(1)} %get-tuple-element.22.mine_ref), channel_id=1, source_target_pairs={{0,4},{4,0},{1,5},{5,1},{2,6},{6,2},{3,7},{7,3},{8,12},{12,8},{9,1... | collective-permute-start | bytes 786440 | tf_op jit(solution)/shard_map/ppermute | solution.py:375
  28.9 9.5 %all-to-all-start.1 = ((f32[16,16,128]{2,1,0:T(8,128)}), f32[16,16,128]{2,1,0:T(8,128)S(1)}, u32[]{:S(2)}, u32[]{:S(2)}) async-start(f32[16,16,128]{2,1,0:T(8,128)} %get-tuple-element.17), calls=%async_computation.1 | async-start | bytes 262144 | tf_op jit(solution)/shard_map/all_to_all | solution.py:376
  38.6 2.3 %collective-permute-start.1 = (f32[1,128]{1,0:T(1,128)S(1)}, f32[1,128]{1,0:T(1,128)S(1)}, u32[]{:S(2)}, u32[]{:S(2)}) collective-permute-start(f32[1,128]{1,0:T(1,128)S(1)} %outer.1), channel_id=1, source_target_pairs={{0,4},{4,0},{1,5},{5,1},{2,6},{6,2},{3,7},{7,3},{8,12},{12,8},{9,1... | collective-permute-start | bytes 1544 | tf_op jit(solution)/shard_map/ppermute | solution.py:409

commit v10 on v9

--- a/solution.py
+++ b/solution.py
@@ -17,7 +17,7 @@
 
 BLOCKS_I, BLOCKS_J = 4, 16
 LANES = 128
-UNROLL = 8
+UNROLL = 16
 ROW_SECOND, ROW_FIRST, ROW_THIRD, ROW_BITS, PIECE = 0, 8, 12, 16, 17
 SPACED, HALF = 9, 64 * 9
 

time: 63 us -> 63 us (level)
  no operation moved by 1% of the time
where the time goes in v10:
time: 63 us; the launch traced here: 62.7 us
  blocking collectives  44.4 us (70%)
  Pallas kernels  9.96 us (16%)
  starting transfers between devices  5.35 us (8%)
  waiting for transfers between devices  2.24 us (4%)
  local copies, waits for them, and re-layouts  0.68 us (1%)
    all_to_all x1, blocking collectives, on_device(): lax.all_to_all(pieces, CUTS, 0, 0, tiled=True).reshape(64 * PIECE, LANES)  23.3 us
    all_to_all x1, blocking collectives, on_device(): total = jnp.sum(lax.all_to_all(copies, CHIPS, 0, 0, tiled=True), axis=0)  21.1 us
    pallas_call x1, Pallas kernels, on_device(): pl.pallas_call(inner_kernel, out_shape=(jax.ShapeDtypeStruct((16, 16, LAN...  4.52 us
    pallas_call x1, Pallas kernels, on_device(): pl.pallas_call(pack_kernel, out_shape=(jax.ShapeDtypeStruct((64 * PIECE,...  4.28 us
    all_to_all x1, starting transfers between devices, on_device(): third = lax.all_to_all(third, WAVE, 0, 0, tiled=True)  3.51 us
    ppermute x1, starting transfers between devices, on_device(): lax.ppermute(partial_sums, CORES, [(0, 1), (1, 0)])  1.45 us
    all_to_all x1, waiting for transfers between devices, on_device(): third = lax.all_to_all(third, WAVE, 0, 0, tiled=True)  1.42 us
  transfers between devices with their start and end apart: 3, of which 2 were waited for; matrix products, arithmetic and copies ran while one was open for 0% of the time, Pallas kernels for 7%

profile of v10, /device:TPU:1, one launch (start us, length us, event | category | flops | bytes accessed | tf_op | source)
XLA Modules:
  0.0 62.7 jit_solution(18421525250517490023)
XLA Ops:
  0.0 4.3 %pack.1 = (f32[1088,128]{1,0:T(8,128)S(1)}, s32[8,64]{1,0:T(8,128)S(1)}, bf16[256,256]{1,0:T(8,128)(2,1)S(1)}, bf16[256,128]{1,0:T(8,128)(2,1)S(1)}, f32[8,128]{1,0:T(8,128)S(1)}, /*index=5*/f32[64,128]{1,0:T(8,128)S(1)}) custom-call(s32[3]{0:T(128)} %order_hbm.1, s32[3,6]{1,0:T(4,128)} %bitcast.15, s32[1,6]{1,0:T(1,128)} %bits_hbm.1, s32[20,64]{1,0:T(8,128)} %bitcast.14, ...), custom_call_target="tpu_custom_call" | custom-call | tf_op jit(solution)/shard_map/pack/pallas_call | solution.py:335
  4.3 23.3 %all_to_all.15 = f32[64,1,2176]{2,1,0:T(1,128)S(1)} all-to-all(f32[64,1,2176]{2,1,0:T(1,128)S(1)} %bitcast.11), channel_id=1, replica_groups=mesh['cuts_0'=2,'cuts_1'=2,'cuts_2'=2,'cuts_3'=2,'cuts_4'=2,'cuts_5'=2,'..., dimensions={0} | all-to-all | bytes 1114112 | tf_op jit(solution)/shard_map/all_to_all | solution.py:363
  27.5 1.0 %select.1 = (f32[16,16,128]{2,1,0:T(8,128)}, f32[512,128]{1,0:T(8,128)S(1)}) custom-call(bf16[256,256]{1,0:T(8,128)(2,1)S(1)} %get-tuple-element.15.chosen_ref, f32[1088,128]{1,0:T(8,128)S(1)} %bitcast.9), custom_call_target="tpu_custom_call" | custom-call | tf_op jit(solution)/shard_map/select/pallas_call | solution.py:364
  28.5 0.4 collective-permute-start
  28.9 3.5 %all-to-all-start.1 = ((f32[16,16,128]{2,1,0:T(8,128)}), f32[16,16,128]{2,1,0:T(8,128)S(1)}, u32[]{:S(2)}, u32[]{:S(2)}) async-start(f32[16,16,128]{2,1,0:T(8,128)} %get-tuple-element.17), calls=%async_computation.1 | async-start | bytes 262144 | tf_op jit(solution)/shard_map/all_to_all | solution.py:376
  32.4 0.0 collective-permute-done.theirs_ref
  32.5 4.5 %inner.1 = (f32[16,16,128]{2,1,0:T(8,128)S(1)}, f32[16,16,128]{2,1,0:T(8,128)S(1)}) custom-call(s32[8,64]{1,0:T(8,128)S(1)} %get-tuple-element.18.row_vmem, bf16[256,128]{1,0:T(8,128)(2,1)S(1)} %get-tuple-element.19.pair_ref, f32[8,128]{1,0:T(8,128)S(1)} %get-tuple-element.20.j_ref, f32[64,128]{1,0:T(8,128)S(1)} %get-tuple-element.21.string_ref, ...), custom_call_target="tpu_custom_call" | custom-call | flops 1073741824 | bytes 1048576 | tf_op jit(solution)/shard_map/inner/pallas_call | solution.py:377
  37.0 1.4 %all-to-all-done.1.third_ref = f32[16,16,128]{2,1,0:T(8,128)S(1)} async-done(((f32[16,16,128]{2,1,0:T(8,128)}), f32[16,16,128]{2,1,0:T(8,128)S(1)}, u32[]{:S(2)}, u32[]{:S(2)}) %all-to-all-start.1) | async-done | bytes 131104 | tf_op jit(solution)/shard_map/all_to_all | solution.py:376
  38.4 0.2 outer.1
  38.6 1.4 %collective-permute-start.1 = (f32[1,128]{1,0:T(1,128)S(1)}, f32[1,128]{1,0:T(1,128)S(1)}, u32[]{:S(2)}, u32[]{:S(2)}) collective-permute-start(f32[1,128]{1,0:T(1,128)S(1)} %outer.1), channel_id=1, source_target_pairs={{0,4},{4,0},{1,5},{5,1},{2,6},{6,2},{3,7},{7,3},{8,12},{12,8},{9,1... | collective-permute-start | bytes 1544 | tf_op jit(solution)/shard_map/ppermute | solution.py:409
  40.0 0.8 %collective-permute-done.1 = f32[1,128]{1,0:T(1,128)S(1)} collective-permute-done((f32[1,128]{1,0:T(1,128)S(1)}, f32[1,128]{1,0:T(1,128)S(1)}, u32[]{:S(2)}, u32[]{:S(2)}) %collective-permute-start.1) | collective-permute-done | bytes 544 | tf_op jit(solution)/shard_map/ppermute | solution.py:409
  40.9 21.1 %all_to_all.16 = f32[128,1,128]{2,1,0:T(1,128)S(1)} all-to-all(f32[128,1,128]{2,1,0:T(1,128)S(1)} %broadcast_in_dim.9), channel_id=1, replica_groups=mesh['cuts_0'=2,'cuts_1'=2,'cuts_2'=2,'cuts_3'=2,'cuts_4'=2,'cuts_5'=2,'..., dimensions={0} | all-to-all | bytes 131072 | tf_op jit(solution)/shard_map/all_to_all | solution.py:411
  62.1 0.6 %reshape.20 = f32[2,64]{1,0:T(2,128)} reshape(f32[128]{0:T(128)S(1)} %reduce_sum.9) | data formatting | bytes 1024 | tf_op jit(solution)/shard_map/reshape | solution.py:412
  (3 shorter events, 0.1 us)
Async XLA Ops:
  28.5 3.9 %collective-permute-start = (f32[512,128]{1,0:T(8,128)S(1)}, f32[512,128]{1,0:T(8,128)S(1)}, u32[]{:S(2)}, u32[]{:S(2)}) collective-permute-start(f32[512,128]{1,0:T(8,128)S(1)} %get-tuple-element.22.mine_ref), channel_id=1, source_target_pairs={{0,4},{4,0},{1,5},{5,1},{2,6},{6,2},{3,7},{7,3},{8,12},{12,8},{9,1... | collective-permute-start | bytes 786440 | tf_op jit(solution)/shard_map/ppermute | solution.py:375
  28.9 9.5 %all-to-all-start.1 = ((f32[16,16,128]{2,1,0:T(8,128)}), f32[16,16,128]{2,1,0:T(8,128)S(1)}, u32[]{:S(2)}, u32[]{:S(2)}) async-start(f32[16,16,128]{2,1,0:T(8,128)} %get-tuple-element.17), calls=%async_computation.1 | async-start | bytes 262144 | tf_op jit(solution)/shard_map/all_to_all | solution.py:376
  38.6 2.3 %collective-permute-start.1 = (f32[1,128]{1,0:T(1,128)S(1)}, f32[1,128]{1,0:T(1,128)S(1)}, u32[]{:S(2)}, u32[]{:S(2)}) collective-permute-start(f32[1,128]{1,0:T(1,128)S(1)} %outer.1), channel_id=1, source_target_pairs={{0,4},{4,0},{1,5},{5,1},{2,6},{6,2},{3,7},{7,3},{8,12},{12,8},{9,1... | collective-permute-start | bytes 1544 | tf_op jit(solution)/shard_map/ppermute | solution.py:409

commit v11 on v9

--- a/solution.py
+++ b/solution.py
@@ -13,7 +13,7 @@
 GRP = ("grp_0", "grp_1")
 WAVE = ("cuts_1", "cuts_2", "cuts_3", "cuts_4")
 CORES = "cuts_5"
-CHIPS = ("cuts_4", "grp_0", "cuts_2", "cuts_0", "grp_1", "cuts_1", "cuts_3")
+CHIPS = ("cuts_4", "cuts_2", "grp_0", "cuts_0", "grp_1", "cuts_3", "cuts_1")
 
 BLOCKS_I, BLOCKS_J = 4, 16
 LANES = 128

time: 63 us -> 63.1 us (level)
  no operation moved by 1% of the time
where the time goes in v11:
time: 63.1 us; the launch traced here: 62.7 us
  blocking collectives  44.4 us (70%)
  Pallas kernels  9.96 us (16%)
  starting transfers between devices  5.35 us (8%)
  waiting for transfers between devices  2.25 us (4%)
  local copies, waits for them, and re-layouts  0.68 us (1%)
    all_to_all x1, blocking collectives, on_device(): lax.all_to_all(pieces, CUTS, 0, 0, tiled=True).reshape(64 * PIECE, LANES)  23.3 us
    all_to_all x1, blocking collectives, on_device(): total = jnp.sum(lax.all_to_all(copies, CHIPS, 0, 0, tiled=True), axis=0)  21.2 us
    pallas_call x1, Pallas kernels, on_device(): pl.pallas_call(inner_kernel, out_shape=(jax.ShapeDtypeStruct((16, 16, LAN...  4.51 us
    pallas_call x1, Pallas kernels, on_device(): pl.pallas_call(pack_kernel, out_shape=(jax.ShapeDtypeStruct((64 * PIECE,...  4.28 us
    all_to_all x1, starting transfers between devices, on_device(): third = lax.all_to_all(third, WAVE, 0, 0, tiled=True)  3.51 us
    ppermute x1, starting transfers between devices, on_device(): lax.ppermute(partial_sums, CORES, [(0, 1), (1, 0)])  1.45 us
    all_to_all x1, waiting for transfers between devices, on_device(): third = lax.all_to_all(third, WAVE, 0, 0, tiled=True)  1.43 us
  transfers between devices with their start and end apart: 3, of which 2 were waited for; matrix products, arithmetic and copies ran while one was open for 0% of the time, Pallas kernels for 7%

profile of v11, /device:TPU:1, one launch (start us, length us, event | category | flops | bytes accessed | tf_op | source)
XLA Modules:
  0.0 62.7 jit_solution(5319129866196408540)
XLA Ops:
  0.0 4.3 %pack.1 = (f32[1088,128]{1,0:T(8,128)S(1)}, s32[8,64]{1,0:T(8,128)S(1)}, bf16[256,256]{1,0:T(8,128)(2,1)S(1)}, bf16[256,128]{1,0:T(8,128)(2,1)S(1)}, f32[8,128]{1,0:T(8,128)S(1)}, /*index=5*/f32[64,128]{1,0:T(8,128)S(1)}) custom-call(s32[3]{0:T(128)} %order_hbm.1, s32[3,6]{1,0:T(4,128)} %bitcast.15, s32[1,6]{1,0:T(1,128)} %bits_hbm.1, s32[20,64]{1,0:T(8,128)} %bitcast.14, ...), custom_call_target="tpu_custom_call" | custom-call | tf_op jit(solution)/shard_map/pack/pallas_call | solution.py:335
  4.3 23.3 %all_to_all.15 = f32[64,1,2176]{2,1,0:T(1,128)S(1)} all-to-all(f32[64,1,2176]{2,1,0:T(1,128)S(1)} %bitcast.11), channel_id=1, replica_groups=mesh['cuts_0'=2,'cuts_1'=2,'cuts_2'=2,'cuts_3'=2,'cuts_4'=2,'cuts_5'=2,'..., dimensions={0} | all-to-all | bytes 1114112 | tf_op jit(solution)/shard_map/all_to_all | solution.py:363
  27.5 1.0 %select.1 = (f32[16,16,128]{2,1,0:T(8,128)}, f32[512,128]{1,0:T(8,128)S(1)}) custom-call(bf16[256,256]{1,0:T(8,128)(2,1)S(1)} %get-tuple-element.15.chosen_ref, f32[1088,128]{1,0:T(8,128)S(1)} %bitcast.9), custom_call_target="tpu_custom_call" | custom-call | tf_op jit(solution)/shard_map/select/pallas_call | solution.py:364
  28.5 0.4 collective-permute-start
  28.9 3.5 %all-to-all-start.1 = ((f32[16,16,128]{2,1,0:T(8,128)}), f32[16,16,128]{2,1,0:T(8,128)S(1)}, u32[]{:S(2)}, u32[]{:S(2)}) async-start(f32[16,16,128]{2,1,0:T(8,128)} %get-tuple-element.17), calls=%async_computation.1 | async-start | bytes 262144 | tf_op jit(solution)/shard_map/all_to_all | solution.py:376
  32.4 0.0 collective-permute-done.theirs_ref
  32.5 4.5 %inner.1 = (f32[16,16,128]{2,1,0:T(8,128)S(1)}, f32[16,16,128]{2,1,0:T(8,128)S(1)}) custom-call(s32[8,64]{1,0:T(8,128)S(1)} %get-tuple-element.18.row_vmem, bf16[256,128]{1,0:T(8,128)(2,1)S(1)} %get-tuple-element.19.pair_ref, f32[8,128]{1,0:T(8,128)S(1)} %get-tuple-element.20.j_ref, f32[64,128]{1,0:T(8,128)S(1)} %get-tuple-element.21.string_ref, ...), custom_call_target="tpu_custom_call" | custom-call | flops 1073741824 | bytes 1048576 | tf_op jit(solution)/shard_map/inner/pallas_call | solution.py:377
  37.0 1.4 %all-to-all-done.1.third_ref = f32[16,16,128]{2,1,0:T(8,128)S(1)} async-done(((f32[16,16,128]{2,1,0:T(8,128)}), f32[16,16,128]{2,1,0:T(8,128)S(1)}, u32[]{:S(2)}, u32[]{:S(2)}) %all-to-all-start.1) | async-done | bytes 131104 | tf_op jit(solution)/shard_map/all_to_all | solution.py:376
  38.4 0.2 outer.1
  38.6 1.4 %collective-permute-start.1 = (f32[1,128]{1,0:T(1,128)S(1)}, f32[1,128]{1,0:T(1,128)S(1)}, u32[]{:S(2)}, u32[]{:S(2)}) collective-permute-start(f32[1,128]{1,0:T(1,128)S(1)} %outer.1), channel_id=1, source_target_pairs={{0,4},{4,0},{1,5},{5,1},{2,6},{6,2},{3,7},{7,3},{8,12},{12,8},{9,1... | collective-permute-start | bytes 1544 | tf_op jit(solution)/shard_map/ppermute | solution.py:409
  40.0 0.8 %collective-permute-done.1 = f32[1,128]{1,0:T(1,128)S(1)} collective-permute-done((f32[1,128]{1,0:T(1,128)S(1)}, f32[1,128]{1,0:T(1,128)S(1)}, u32[]{:S(2)}, u32[]{:S(2)}) %collective-permute-start.1) | collective-permute-done | bytes 544 | tf_op jit(solution)/shard_map/ppermute | solution.py:409
  40.9 21.2 %all_to_all.16 = f32[128,1,128]{2,1,0:T(1,128)S(1)} all-to-all(f32[128,1,128]{2,1,0:T(1,128)S(1)} %broadcast_in_dim.9), channel_id=1, replica_groups=mesh['cuts_0'=2,'cuts_1'=2,'cuts_2'=2,'cuts_3'=2,'cuts_4'=2,'cuts_5'=2,'..., dimensions={0} | all-to-all | bytes 131072 | tf_op jit(solution)/shard_map/all_to_all | solution.py:411
  62.1 0.6 %reshape.20 = f32[2,64]{1,0:T(2,128)} reshape(f32[128]{0:T(128)S(1)} %reduce_sum.9) | data formatting | bytes 1024 | tf_op jit(solution)/shard_map/reshape | solution.py:412
  (3 shorter events, 0.1 us)
Async XLA Ops:
  28.5 3.9 %collective-permute-start = (f32[512,128]{1,0:T(8,128)S(1)}, f32[512,128]{1,0:T(8,128)S(1)}, u32[]{:S(2)}, u32[]{:S(2)}) collective-permute-start(f32[512,128]{1,0:T(8,128)S(1)} %get-tuple-element.22.mine_ref), channel_id=1, source_target_pairs={{0,4},{4,0},{1,5},{5,1},{2,6},{6,2},{3,7},{7,3},{8,12},{12,8},{9,1... | collective-permute-start | bytes 786440 | tf_op jit(solution)/shard_map/ppermute | solution.py:375
  28.9 9.5 %all-to-all-start.1 = ((f32[16,16,128]{2,1,0:T(8,128)}), f32[16,16,128]{2,1,0:T(8,128)S(1)}, u32[]{:S(2)}, u32[]{:S(2)}) async-start(f32[16,16,128]{2,1,0:T(8,128)} %get-tuple-element.17), calls=%async_computation.1 | async-start | bytes 262144 | tf_op jit(solution)/shard_map/all_to_all | solution.py:376
  38.6 2.3 %collective-permute-start.1 = (f32[1,128]{1,0:T(1,128)S(1)}, f32[1,128]{1,0:T(1,128)S(1)}, u32[]{:S(2)}, u32[]{:S(2)}) collective-permute-start(f32[1,128]{1,0:T(1,128)S(1)} %outer.1), channel_id=1, source_target_pairs={{0,4},{4,0},{1,5},{5,1},{2,6},{6,2},{3,7},{7,3},{8,12},{12,8},{9,1... | collective-permute-start | bytes 1544 | tf_op jit(solution)/shard_map/ppermute | solution.py:409

commit v12 on v11

--- a/solution.py
+++ b/solution.py
@@ -13,7 +13,7 @@
 GRP = ("grp_0", "grp_1")
 WAVE = ("cuts_1", "cuts_2", "cuts_3", "cuts_4")
 CORES = "cuts_5"
-CHIPS = ("cuts_4", "cuts_2", "grp_0", "cuts_0", "grp_1", "cuts_3", "cuts_1")
+CHIPS = ("cuts_4", "cuts_2", "grp_0", "cuts_0", "grp_1", "cuts_1", "cuts_3")
 
 BLOCKS_I, BLOCKS_J = 4, 16
 LANES = 128

time: 63.1 us -> 63.1 us (level)
  no operation moved by 1% of the time
where the time goes in v12:
time: 63.1 us; the launch traced here: 62.7 us
  blocking collectives  44.4 us (70%)
  Pallas kernels  9.96 us (16%)
  starting transfers between devices  5.35 us (8%)
  waiting for transfers between devices  2.24 us (4%)
  local copies, waits for them, and re-layouts  0.68 us (1%)
    all_to_all x1, blocking collectives, on_device(): lax.all_to_all(pieces, CUTS, 0, 0, tiled=True).reshape(64 * PIECE, LANES)  23.3 us
    all_to_all x1, blocking collectives, on_device(): total = jnp.sum(lax.all_to_all(copies, CHIPS, 0, 0, tiled=True), axis=0)  21.1 us
    pallas_call x1, Pallas kernels, on_device(): pl.pallas_call(inner_kernel, out_shape=(jax.ShapeDtypeStruct((16, 16, LAN...  4.52 us
    pallas_call x1, Pallas kernels, on_device(): pl.pallas_call(pack_kernel, out_shape=(jax.ShapeDtypeStruct((64 * PIECE,...  4.28 us
    all_to_all x1, starting transfers between devices, on_device(): third = lax.all_to_all(third, WAVE, 0, 0, tiled=True)  3.51 us
    ppermute x1, starting transfers between devices, on_device(): lax.ppermute(partial_sums, CORES, [(0, 1), (1, 0)])  1.45 us
    all_to_all x1, waiting for transfers between devices, on_device(): third = lax.all_to_all(third, WAVE, 0, 0, tiled=True)  1.42 us
  transfers between devices with their start and end apart: 3, of which 2 were waited for; matrix products, arithmetic and copies ran while one was open for 0% of the time, Pallas kernels for 7%

profile of v12, /device:TPU:1, one launch (start us, length us, event | category | flops | bytes accessed | tf_op | source)
XLA Modules:
  0.0 62.7 jit_solution(17788125606181691433)
XLA Ops:
  0.0 4.3 %pack.1 = (f32[1088,128]{1,0:T(8,128)S(1)}, s32[8,64]{1,0:T(8,128)S(1)}, bf16[256,256]{1,0:T(8,128)(2,1)S(1)}, bf16[256,128]{1,0:T(8,128)(2,1)S(1)}, f32[8,128]{1,0:T(8,128)S(1)}, /*index=5*/f32[64,128]{1,0:T(8,128)S(1)}) custom-call(s32[3]{0:T(128)} %order_hbm.1, s32[3,6]{1,0:T(4,128)} %bitcast.15, s32[1,6]{1,0:T(1,128)} %bits_hbm.1, s32[20,64]{1,0:T(8,128)} %bitcast.14, ...), custom_call_target="tpu_custom_call" | custom-call | tf_op jit(solution)/shard_map/pack/pallas_call | solution.py:335
  4.3 23.3 %all_to_all.15 = f32[64,1,2176]{2,1,0:T(1,128)S(1)} all-to-all(f32[64,1,2176]{2,1,0:T(1,128)S(1)} %bitcast.11), channel_id=1, replica_groups=mesh['cuts_0'=2,'cuts_1'=2,'cuts_2'=2,'cuts_3'=2,'cuts_4'=2,'cuts_5'=2,'..., dimensions={0} | all-to-all | bytes 1114112 | tf_op jit(solution)/shard_map/all_to_all | solution.py:363
  27.5 1.0 %select.1 = (f32[16,16,128]{2,1,0:T(8,128)}, f32[512,128]{1,0:T(8,128)S(1)}) custom-call(bf16[256,256]{1,0:T(8,128)(2,1)S(1)} %get-tuple-element.15.chosen_ref, f32[1088,128]{1,0:T(8,128)S(1)} %bitcast.9), custom_call_target="tpu_custom_call" | custom-call | tf_op jit(solution)/shard_map/select/pallas_call | solution.py:364
  28.5 0.4 collective-permute-start
  28.9 3.5 %all-to-all-start.1 = ((f32[16,16,128]{2,1,0:T(8,128)}), f32[16,16,128]{2,1,0:T(8,128)S(1)}, u32[]{:S(2)}, u32[]{:S(2)}) async-start(f32[16,16,128]{2,1,0:T(8,128)} %get-tuple-element.17), calls=%async_computation.1 | async-start | bytes 262144 | tf_op jit(solution)/shard_map/all_to_all | solution.py:376
  32.4 0.0 collective-permute-done.theirs_ref
  32.5 4.5 %inner.1 = (f32[16,16,128]{2,1,0:T(8,128)S(1)}, f32[16,16,128]{2,1,0:T(8,128)S(1)}) custom-call(s32[8,64]{1,0:T(8,128)S(1)} %get-tuple-element.18.row_vmem, bf16[256,128]{1,0:T(8,128)(2,1)S(1)} %get-tuple-element.19.pair_ref, f32[8,128]{1,0:T(8,128)S(1)} %get-tuple-element.20.j_ref, f32[64,128]{1,0:T(8,128)S(1)} %get-tuple-element.21.string_ref, ...), custom_call_target="tpu_custom_call" | custom-call | flops 1073741824 | bytes 1048576 | tf_op jit(solution)/shard_map/inner/pallas_call | solution.py:377
  37.0 1.4 %all-to-all-done.1.third_ref = f32[16,16,128]{2,1,0:T(8,128)S(1)} async-done(((f32[16,16,128]{2,1,0:T(8,128)}), f32[16,16,128]{2,1,0:T(8,128)S(1)}, u32[]{:S(2)}, u32[]{:S(2)}) %all-to-all-start.1) | async-done | bytes 131104 | tf_op jit(solution)/shard_map/all_to_all | solution.py:376
  38.4 0.2 outer.1
  38.6 1.4 %collective-permute-start.1 = (f32[1,128]{1,0:T(1,128)S(1)}, f32[1,128]{1,0:T(1,128)S(1)}, u32[]{:S(2)}, u32[]{:S(2)}) collective-permute-start(f32[1,128]{1,0:T(1,128)S(1)} %outer.1), channel_id=1, source_target_pairs={{0,4},{4,0},{1,5},{5,1},{2,6},{6,2},{3,7},{7,3},{8,12},{12,8},{9,1... | collective-permute-start | bytes 1544 | tf_op jit(solution)/shard_map/ppermute | solution.py:409
  40.0 0.8 %collective-permute-done.1 = f32[1,128]{1,0:T(1,128)S(1)} collective-permute-done((f32[1,128]{1,0:T(1,128)S(1)}, f32[1,128]{1,0:T(1,128)S(1)}, u32[]{:S(2)}, u32[]{:S(2)}) %collective-permute-start.1) | collective-permute-done | bytes 544 | tf_op jit(solution)/shard_map/ppermute | solution.py:409
  40.9 21.1 %all_to_all.16 = f32[128,1,128]{2,1,0:T(1,128)S(1)} all-to-all(f32[128,1,128]{2,1,0:T(1,128)S(1)} %broadcast_in_dim.9), channel_id=1, replica_groups=mesh['cuts_0'=2,'cuts_1'=2,'cuts_2'=2,'cuts_3'=2,'cuts_4'=2,'cuts_5'=2,'..., dimensions={0} | all-to-all | bytes 131072 | tf_op jit(solution)/shard_map/all_to_all | solution.py:411
  62.0 0.6 %reshape.20 = f32[2,64]{1,0:T(2,128)} reshape(f32[128]{0:T(128)S(1)} %reduce_sum.9) | data formatting | bytes 1024 | tf_op jit(solution)/shard_map/reshape | solution.py:412
  (3 shorter events, 0.1 us)
Async XLA Ops:
  28.5 3.9 %collective-permute-start = (f32[512,128]{1,0:T(8,128)S(1)}, f32[512,128]{1,0:T(8,128)S(1)}, u32[]{:S(2)}, u32[]{:S(2)}) collective-permute-start(f32[512,128]{1,0:T(8,128)S(1)} %get-tuple-element.22.mine_ref), channel_id=1, source_target_pairs={{0,4},{4,0},{1,5},{5,1},{2,6},{6,2},{3,7},{7,3},{8,12},{12,8},{9,1... | collective-permute-start | bytes 786440 | tf_op jit(solution)/shard_map/ppermute | solution.py:375
  28.9 9.5 %all-to-all-start.1 = ((f32[16,16,128]{2,1,0:T(8,128)}), f32[16,16,128]{2,1,0:T(8,128)S(1)}, u32[]{:S(2)}, u32[]{:S(2)}) async-start(f32[16,16,128]{2,1,0:T(8,128)} %get-tuple-element.17), calls=%async_computation.1 | async-start | bytes 262144 | tf_op jit(solution)/shard_map/all_to_all | solution.py:376
  38.6 2.3 %collective-permute-start.1 = (f32[1,128]{1,0:T(1,128)S(1)}, f32[1,128]{1,0:T(1,128)S(1)}, u32[]{:S(2)}, u32[]{:S(2)}) collective-permute-start(f32[1,128]{1,0:T(1,128)S(1)} %outer.1), channel_id=1, source_target_pairs={{0,4},{4,0},{1,5},{5,1},{2,6},{6,2},{3,7},{7,3},{8,12},{12,8},{9,1... | collective-permute-start | bytes 1544 | tf_op jit(solution)/shard_map/ppermute | solution.py:409
